TPU v7x, 128 devices: a whole 4x4x4 slice. The times are simulated.
128 devices in a mesh: row: 8 (over x, y_hi), col: 16 (over y_lo, z, core).
Axes of the slice: x: 4, y: 4 (y_hi: 2, y_lo: 2; y = y_hi * 2 + y_lo), z: 4, core: 2. Of those that a mesh axis runs over, the one named last changes fastest.
Arguments:
- incoming: float32 [8, 16, 4, 128, 128], P('row', 'col'), may hold values from -6 to 6
- block_map: int32 [8, 16, 4], P('row', 'col'), may hold values from 0 to 511, as said below
- panel_row: float32 [2, 8, 128, 32, 16, 128], P(None, 'row', None, None, 'col'), may hold values from -0.125 to 0.125
- diag_inverse: float32 [1, 16, 128, 128], P(None, 'col'), may hold values from -1 to 2.5
Outputs:
- panel_solution: float32 [128, 1, 16, 128], P('row', None, 'col')
- trailing_rhs: float32 [128, 31, 16, 128], P('row', None, 'col')
Inputs may be any that keep to these rules, and one draw needn't show every extreme that they name: block_map names every block index from 0 to 511 exactly once; the 4 blocks of one device lie in distinct grid columns, block b lying in grid column b mod 16.
All inputs are finite; a program needn't handle non-finite values.
Results may differ from a plain program's by a relative error of at most 0.00013.
Values sent between devices are 32-bit elements; how exact they have to be, the bound alone decides.
No kernel may reach another device: no remote copies, remote signals or barrier semaphores. Data moves between devices by JAX's collectives and lax.ppermute only.
A program may use at most 64 MiB of HBM per device.

v0:
```python
import jax
import jax.numpy as jnp
from jax import lax
from jax.sharding import PartitionSpec as P


def in_one_piece(arrays, axis, split_dim, concat_dim, along):
    columns = [a.reshape(*a.shape[:along], -1) for a in arrays]
    both = jnp.concatenate(columns, axis=along)
    whole, at, finished = (
        lax.all_to_all(both, axis, split_axis=split_dim, concat_axis=concat_dim, tiled=True),
        0,
        [],
    )
    for a, column in zip(arrays, columns):
        piece = whole[..., at : at + column.shape[along]]
        finished.append(piece.reshape(*piece.shape[:along], *a.shape[along:]))
        at += column.shape[along]
    return tuple(finished)


def from_everyone(array, axis):
    copies = jnp.broadcast_to(array, (lax.axis_size(axis), *array.shape))
    return lax.all_to_all(copies, axis, split_axis=0, concat_axis=0, tiled=True)


def in_order(parts, dim):
    dims = list(parts.shape[1:])
    dims[dim] *= parts.shape[0]
    return jnp.moveaxis(parts, 0, dim).reshape(dims)


def collect(array, axis, dim):
    parts = from_everyone(array, axis)
    return in_order(parts, dim)


def picked(array, axis, root):
    return lax.dynamic_index_in_dim(lax.all_gather(array, axis), root, 0, keepdims=False)


def split_up(array, dim, devices):
    dims = array.shape
    parts = array.reshape(*dims[:dim], devices, dims[dim] // devices, *dims[dim + 1 :])
    return jnp.moveaxis(parts, dim, 0)


def sum_at_owner(array, axis, dim):
    devices = lax.axis_size(axis)
    parts = lax.all_to_all(split_up(array, dim, devices), axis, 0, 0, tiled=True)
    return jnp.sum(parts, axis=0)


def take_at(array, position, axis):
    return lax.dynamic_index_in_dim(array, position, axis, keepdims=False)


def per_device(incoming, block_map, panel_row, diag_inverse):
    highest = lax.Precision.HIGHEST
    grid_rows = lax.axis_size("row")
    grid_cols = lax.axis_size("col")
    my_row = lax.axis_index("row")
    my_col = lax.axis_index("col")
    source_blocks = incoming.shape[2]
    rhs_count = incoming.shape[3]
    block_size = incoming.shape[4]
    rhs_share = rhs_count // grid_rows
    tile_rows = panel_row.shape[0]
    slot_count = panel_row.shape[3]
    tile_cols = diag_inverse.shape[0]
    panel_blocks = tile_rows * grid_rows
    targets = block_map.reshape(source_blocks)
    columns_of = (
        targets[None, :] % grid_cols == jnp.arange(grid_cols, dtype=jnp.int32)[:, None]
    ).astype(jnp.float32)
    pieces = incoming.reshape(source_blocks, grid_rows, rhs_share, block_size)
    outgoing = jnp.einsum("cu,upke->pcke", columns_of, pieces, precision=highest)
    labels = (
        jnp.einsum("cu,u->c", columns_of, (targets + 1).astype(jnp.float32), precision=highest)
        - 1.0
    )
    labels = jnp.broadcast_to(labels[None, :, None], (grid_rows, grid_cols, 1))
    received, labels_in = in_one_piece(
        (
            outgoing.reshape(grid_rows * grid_cols, rhs_share, block_size),
            labels.reshape(grid_rows * grid_cols, 1),
        ),
        ("row", "col"),
        0,
        0,
        1,
    )
    wanted = jnp.arange(slot_count, dtype=jnp.int32) * grid_cols + my_col
    matches = (labels_in[:, 0].astype(jnp.int32)[None, :] == wanted[:, None]).astype(jnp.float32)
    local_rhs = jnp.einsum("sq,qke->kse", matches, received, precision=highest)
    local_upper = panel_row.reshape(tile_rows, block_size, slot_count, block_size)
    inverse = diag_inverse.reshape(tile_cols, block_size, block_size)
    upper_panel = panel_row[:, :, :, :tile_cols]
    gathered_upper = collect(upper_panel, "row", 1).reshape(
        panel_blocks, block_size, tile_cols, block_size
    )

    def advance(block_index, slices):
        slot_index = block_index // grid_cols
        owner_col = block_index % grid_cols
        upper_strip = take_at(gathered_upper, slot_index, 2)
        carried = jnp.einsum("jkf,jfe->ke", slices, upper_strip, precision=highest)
        residue = take_at(local_rhs, slot_index, 1) - carried
        solved_slice = jnp.einsum(
            "kf,ef->ke", residue, take_at(inverse, slot_index, 0), precision=highest
        )
        shared = picked(solved_slice, "col", owner_col)
        return lax.dynamic_update_index_in_dim(slices, shared, block_index, 0)

    slices = lax.fori_loop(
        0, panel_blocks, advance, jnp.zeros((panel_blocks, rhs_share, block_size), jnp.float32)
    )
    solved = collect(slices, "row", 1)
    own_share = lax.dynamic_slice_in_dim(solved, my_row * rhs_share, rhs_share, 1)
    panel_part = jnp.take(
        own_share, jnp.arange(tile_cols, dtype=jnp.int32) * grid_cols + my_col, axis=0
    )
    panel_solution = jnp.transpose(panel_part, (1, 0, 2))[:, :, None, :]
    own_rows = jnp.take(solved, jnp.arange(tile_rows, dtype=jnp.int32) * grid_rows + my_row, axis=0)
    reduced = sum_at_owner(
        jnp.einsum("tkf,tfse->kse", own_rows, local_upper[:, :, tile_cols:, :], precision=highest),
        "row",
        0,
    )
    trailing = local_rhs[:, tile_cols:, :] - reduced
    return (panel_solution, trailing[:, :, None, :])


def solution(mesh):
    in_specs = (
        P("row", "col", None, None, None),
        P("row", "col", None),
        P(None, "row", None, None, "col", None),
        P(None, "col", None, None),
    )
    out_specs = (P("row", None, "col", None), P("row", None, "col", None))
    return jax.shard_map(
        per_device, mesh=mesh, in_specs=in_specs, out_specs=out_specs, check_vma=False
    )
```

profile of v0, /device:TPU:0, one launch (start us, length us, event | category | flops | bytes accessed | tf_op | source)
XLA Modules:
  0.0 410.0 jit_solution(710305567348503040)
XLA Ops:
  0.7 1.0 slice.19
  1.6 1.1 broadcast_in_dim.52
  2.7 7.0 %all-to-all-start.1 = ((f32[8,2,1,128,1,1,128]{6,3,1,5,4,2,0:T(8,128)}), f32[8,2,1,128,1,1,128]{6,3,1,5,4,2,0:T(8,128)S(1)}, u32[]{:S(2)}, u32[]{:S(2)}) async-start(f32[8,2,1,128,1,1,128]{6,3,1,5,4,2,0:T(8,128)} %broadcast_in_dim.52), calls=%async_computation.1 | async-start | bytes 2097152 | tf_op jit(solution)/shard_map/all_to_all | solution.py:24
  9.8 0.2 fusion.6
  10.1 0.8 convolution_bitcast_fusion.1
  10.9 0.3 copy.37
  11.2 0.3 copy.63
  11.6 2.1 copy.39
  13.8 11.9 %all-to-all-done.1 = f32[8,2,1,128,1,1,128]{6,3,1,5,4,2,0:T(8,128)S(1)} async-done(((f32[8,2,1,128,1,1,128]{6,3,1,5,4,2,0:T(8,128)}), f32[8,2,1,128,1,1,128]{6,3,1,5,4,2,0:T(8,128)S(1)}, u32[]{:S(2)}, u32[]{:S(2)}) %all-to-all-start.1) | async-done | bytes 1048608 | tf_op jit(solution)/shard_map/all_to_all | solution.py:24
  25.7 8.2 %all-to-all-start = ((f32[128,1,2049]{2,1,0:T(1,128)}), f32[128,1,2049]{2,1,0:T(1,128)S(1)}, u32[]{:S(2)}, u32[]{:S(2)}) async-start(f32[128,1,2049]{2,1,0:T(1,128)} %copy.39), calls=%async_computation | async-start | bytes 2228224 | tf_op jit(solution)/shard_map/all_to_all | solution.py:11
  34.0 19.9 %all-to-all-done = f32[128,1,2049]{2,1,0:T(1,128)S(1)} async-done(((f32[128,1,2049]{2,1,0:T(1,128)}), f32[128,1,2049]{2,1,0:T(1,128)S(1)}, u32[]{:S(2)}, u32[]{:S(2)}) %all-to-all-start) | async-done | bytes 1049120 | tf_op jit(solution)/shard_map/all_to_all | solution.py:11
  53.9 1.4 copy.40
  55.5 0.7 convolution_bitcast_fusion.2
  56.2 290.2 %while.16 = (s32[]{:T(128)}, f32[16,16,128]{2,1,0:T(8,128)S(1)}, f32[16,32,128]{2,1,0:T(8,128)S(1)}, f32[16,128,1,128]{3,1,0,2:T(8,128)S(1)}, f32[1,128,128]{2,1...) while((s32[]{:T(128)}, f32[16,16,128]{2,1,0:T(8,128)S(1)}, ...), condition=%wide.region_1.2_spmd, body=%wide.region_0.1_spmd.sunk | while | flops 53479436 | bytes 1450304 | solution.py:115
  56.2 0.6 fusion.43
  57.1 16.5 %all-gather.2 = f32[256,128]{1,0:T(8,128)S(1)} all-gather(f32[16,128]{1,0:T(8,128)S(1)} %fusion.44), channel_id=2, replica_groups=mesh['row'=8,'col'=16] {'col'}, dimensions={0}, use_global_device_ids=true | all-gather | bytes 139264 | tf_op jit(solution)/shard_map/while/body/eval_jaxpr/all_gather | solution.py:39
  73.6 0.6 fusion.43
  74.2 0.2 fusion.44
  74.4 18.1 %all-gather.2 = f32[256,128]{1,0:T(8,128)S(1)} all-gather(f32[16,128]{1,0:T(8,128)S(1)} %fusion.44), channel_id=2, replica_groups=mesh['row'=8,'col'=16] {'col'}, dimensions={0}, use_global_device_ids=true | all-gather | bytes 139264 | tf_op jit(solution)/shard_map/while/body/eval_jaxpr/all_gather | solution.py:39
  92.5 0.6 fusion.43
  93.1 0.2 fusion.44
  93.3 16.6 %all-gather.2 = f32[256,128]{1,0:T(8,128)S(1)} all-gather(f32[16,128]{1,0:T(8,128)S(1)} %fusion.44), channel_id=2, replica_groups=mesh['row'=8,'col'=16] {'col'}, dimensions={0}, use_global_device_ids=true | all-gather | bytes 139264 | tf_op jit(solution)/shard_map/while/body/eval_jaxpr/all_gather | solution.py:39
  110.0 0.6 fusion.43
  110.6 0.2 fusion.44
  110.8 18.0 %all-gather.2 = f32[256,128]{1,0:T(8,128)S(1)} all-gather(f32[16,128]{1,0:T(8,128)S(1)} %fusion.44), channel_id=2, replica_groups=mesh['row'=8,'col'=16] {'col'}, dimensions={0}, use_global_device_ids=true | all-gather | bytes 139264 | tf_op jit(solution)/shard_map/while/body/eval_jaxpr/all_gather | solution.py:39
  128.8 0.6 fusion.43
  129.4 0.2 fusion.44
  129.6 16.6 %all-gather.2 = f32[256,128]{1,0:T(8,128)S(1)} all-gather(f32[16,128]{1,0:T(8,128)S(1)} %fusion.44), channel_id=2, replica_groups=mesh['row'=8,'col'=16] {'col'}, dimensions={0}, use_global_device_ids=true | all-gather | bytes 139264 | tf_op jit(solution)/shard_map/while/body/eval_jaxpr/all_gather | solution.py:39
  146.3 0.6 fusion.43
  146.9 0.2 fusion.44
  147.1 18.0 %all-gather.2 = f32[256,128]{1,0:T(8,128)S(1)} all-gather(f32[16,128]{1,0:T(8,128)S(1)} %fusion.44), channel_id=2, replica_groups=mesh['row'=8,'col'=16] {'col'}, dimensions={0}, use_global_device_ids=true | all-gather | bytes 139264 | tf_op jit(solution)/shard_map/while/body/eval_jaxpr/all_gather | solution.py:39
  165.1 0.6 fusion.43
  165.7 0.2 fusion.44
  165.9 16.6 %all-gather.2 = f32[256,128]{1,0:T(8,128)S(1)} all-gather(f32[16,128]{1,0:T(8,128)S(1)} %fusion.44), channel_id=2, replica_groups=mesh['row'=8,'col'=16] {'col'}, dimensions={0}, use_global_device_ids=true | all-gather | bytes 139264 | tf_op jit(solution)/shard_map/while/body/eval_jaxpr/all_gather | solution.py:39
  182.5 0.6 fusion.43
  183.2 0.2 fusion.44
  183.4 18.0 %all-gather.2 = f32[256,128]{1,0:T(8,128)S(1)} all-gather(f32[16,128]{1,0:T(8,128)S(1)} %fusion.44), channel_id=2, replica_groups=mesh['row'=8,'col'=16] {'col'}, dimensions={0}, use_global_device_ids=true | all-gather | bytes 139264 | tf_op jit(solution)/shard_map/while/body/eval_jaxpr/all_gather | solution.py:39
  201.3 0.6 fusion.43
  202.2 16.6 %all-gather.2 = f32[256,128]{1,0:T(8,128)S(1)} all-gather(f32[16,128]{1,0:T(8,128)S(1)} %fusion.44), channel_id=2, replica_groups=mesh['row'=8,'col'=16] {'col'}, dimensions={0}, use_global_device_ids=true | all-gather | bytes 139264 | tf_op jit(solution)/shard_map/while/body/eval_jaxpr/all_gather | solution.py:39
  218.8 0.6 fusion.43
  219.6 18.0 %all-gather.2 = f32[256,128]{1,0:T(8,128)S(1)} all-gather(f32[16,128]{1,0:T(8,128)S(1)} %fusion.44), channel_id=2, replica_groups=mesh['row'=8,'col'=16] {'col'}, dimensions={0}, use_global_device_ids=true | all-gather | bytes 139264 | tf_op jit(solution)/shard_map/while/body/eval_jaxpr/all_gather | solution.py:39
  237.6 0.6 fusion.43
  238.4 16.6 %all-gather.2 = f32[256,128]{1,0:T(8,128)S(1)} all-gather(f32[16,128]{1,0:T(8,128)S(1)} %fusion.44), channel_id=2, replica_groups=mesh['row'=8,'col'=16] {'col'}, dimensions={0}, use_global_device_ids=true | all-gather | bytes 139264 | tf_op jit(solution)/shard_map/while/body/eval_jaxpr/all_gather | solution.py:39
  255.1 0.6 fusion.43
  255.9 18.0 %all-gather.2 = f32[256,128]{1,0:T(8,128)S(1)} all-gather(f32[16,128]{1,0:T(8,128)S(1)} %fusion.44), channel_id=2, replica_groups=mesh['row'=8,'col'=16] {'col'}, dimensions={0}, use_global_device_ids=true | all-gather | bytes 139264 | tf_op jit(solution)/shard_map/while/body/eval_jaxpr/all_gather | solution.py:39
  273.9 0.6 fusion.43
  274.7 16.6 %all-gather.2 = f32[256,128]{1,0:T(8,128)S(1)} all-gather(f32[16,128]{1,0:T(8,128)S(1)} %fusion.44), channel_id=2, replica_groups=mesh['row'=8,'col'=16] {'col'}, dimensions={0}, use_global_device_ids=true | all-gather | bytes 139264 | tf_op jit(solution)/shard_map/while/body/eval_jaxpr/all_gather | solution.py:39
  291.4 0.6 fusion.43
  292.2 18.0 %all-gather.2 = f32[256,128]{1,0:T(8,128)S(1)} all-gather(f32[16,128]{1,0:T(8,128)S(1)} %fusion.44), channel_id=2, replica_groups=mesh['row'=8,'col'=16] {'col'}, dimensions={0}, use_global_device_ids=true | all-gather | bytes 139264 | tf_op jit(solution)/shard_map/while/body/eval_jaxpr/all_gather | solution.py:39
  310.2 0.6 fusion.43
  311.0 16.6 %all-gather.2 = f32[256,128]{1,0:T(8,128)S(1)} all-gather(f32[16,128]{1,0:T(8,128)S(1)} %fusion.44), channel_id=2, replica_groups=mesh['row'=8,'col'=16] {'col'}, dimensions={0}, use_global_device_ids=true | all-gather | bytes 139264 | tf_op jit(solution)/shard_map/while/body/eval_jaxpr/all_gather | solution.py:39
  327.6 0.6 fusion.43
  328.5 18.0 %all-gather.2 = f32[256,128]{1,0:T(8,128)S(1)} all-gather(f32[16,128]{1,0:T(8,128)S(1)} %fusion.44), channel_id=2, replica_groups=mesh['row'=8,'col'=16] {'col'}, dimensions={0}, use_global_device_ids=true | all-gather | bytes 139264 | tf_op jit(solution)/shard_map/while/body/eval_jaxpr/all_gather | solution.py:39
  346.4 1.1 broadcast_in_dim.53
  347.5 3.6 all-to-all-start.2
  351.1 6.6 %copy.62 = f32[2,1,128,32,1,128]{5,2,0,3,4,1:T(8,128)} copy(f32[2,1,128,32,1,128]{5,4,3,2,1,0:T(1,128)} %param.8) | data formatting | bytes 8388608 | tf_op args[2]
  357.7 11.0 %all-to-all-done.2 = f32[8,16,16,128]{3,2,1,0:T(8,128)S(1)} async-done(((f32[8,16,16,128]{3,2,1,0:T(8,128)}), f32[8,16,16,128]{3,2,1,0:T(8,128)S(1)}, u32[]{:S(2)}, u32[]{:S(2)}) %all-to-all-start.2) | async-done | bytes 1048608 | tf_op jit(solution)/shard_map/all_to_all | solution.py:24
  368.7 0.6 gather_fusion
  369.3 4.5 %fusion.4 = f32[128,31,128,1]{2,0,3,1:T(8,128)S(1)} fusion(f32[2,128,32,128]{3,1,0,2:T(8,128)} %bitcast.100, f32[2,128,128]{2,1,0:T(8,128)S(1)} %gather_fusion, pred[2]{0:T(512)(128)(4,1)S(1)} %compare_and_fusion), kind=kOutput, calls=%fused_computation.9 | convolution fusion | flops 1560313856 | bytes 6225922 | tf_op jit(solution)/shard_map/tkf,tfse->kse/dot_general | solution.py:126
  373.8 1.5 copy.46
  375.3 3.8 all-to-all-start.3
  379.1 0.6 dynamic-slice_select_fusion
  379.7 29.0 %all-to-all-done.3 = f32[8,16,31,128]{3,1,2,0:T(8,128)S(1)} async-done(((f32[8,16,31,128]{3,1,2,0:T(8,128)}), f32[8,16,31,128]{3,1,2,0:T(8,128)S(1)}, u32[]{:S(2)}, u32[]{:S(2)}) %all-to-all-start.3) | async-done | bytes 2031648 | tf_op jit(solution)/shard_map/all_to_all | solution.py:50
  409.0 1.0 copy.50
  (66 shorter events, 2.7 us)
Async XLA Ops:
  0.6 9.4 %copy-start = (f32[1,1,4,128,128]{4,3,2,1,0:T(8,128)S(1)}, f32[1,1,4,128,128]{4,3,2,1,0:T(8,128)}, u32[]{:S(2)}) copy-start(f32[1,1,4,128,128]{4,3,2,1,0:T(8,128)} %param.6) | copy-start | bytes 786436
  0.6 9.1 %copy-start.4 = (s32[1,1,4]{2,1,0:T(1,128)S(1)}, s32[1,1,4]{2,1,0:T(1,128)}, u32[]{:S(2)}) copy-start(s32[1,1,4]{2,1,0:T(1,128)} %param.7) | copy-start | bytes 52
  2.7 23.0 %all-to-all-start.1 = ((f32[8,2,1,128,1,1,128]{6,3,1,5,4,2,0:T(8,128)}), f32[8,2,1,128,1,1,128]{6,3,1,5,4,2,0:T(8,128)S(1)}, u32[]{:S(2)}, u32[]{:S(2)}) async-start(f32[8,2,1,128,1,1,128]{6,3,1,5,4,2,0:T(8,128)} %broadcast_in_dim.52), calls=%async_computation.1 | async-start | bytes 2097152 | tf_op jit(solution)/shard_map/all_to_all | solution.py:24
  25.7 28.3 %all-to-all-start = ((f32[128,1,2049]{2,1,0:T(1,128)}), f32[128,1,2049]{2,1,0:T(1,128)S(1)}, u32[]{:S(2)}, u32[]{:S(2)}) async-start(f32[128,1,2049]{2,1,0:T(1,128)} %copy.39), calls=%async_computation | async-start | bytes 2228224 | tf_op jit(solution)/shard_map/all_to_all | solution.py:11
  55.4 0.8 copy-start.1
  346.4 11.2 %copy-start.2 = (f32[16,32,128]{2,1,0:T(8,128)}, f32[16,32,128]{2,1,0:T(8,128)S(1)}, u32[]{:S(2)}) copy-start(f32[16,32,128]{2,1,0:T(8,128)S(1)} %get-tuple-element.257) | copy-start | bytes 786436
  347.5 21.1 %all-to-all-start.2 = ((f32[8,16,16,128]{3,2,1,0:T(8,128)}), f32[8,16,16,128]{3,2,1,0:T(8,128)S(1)}, u32[]{:S(2)}, u32[]{:S(2)}) async-start(f32[8,16,16,128]{3,2,1,0:T(8,128)} %broadcast_in_dim.53), calls=%async_computation.2 | async-start | bytes 2097152 | tf_op jit(solution)/shard_map/all_to_all | solution.py:24
  375.3 33.5 %all-to-all-start.3 = ((f32[8,16,31,128]{3,1,2,0:T(8,128)}), f32[8,16,31,128]{3,1,2,0:T(8,128)S(1)}, u32[]{:S(2)}, u32[]{:S(2)}) async-start(f32[8,16,31,128]{3,1,2,0:T(8,128)} %copy.46), calls=%async_computation.3 | async-start | bytes 4063232 | tf_op jit(solution)/shard_map/all_to_all | solution.py:50
  379.7 29.2 %copy-start.3 = (f32[16,32,128]{2,1,0:T(8,128)S(1)}, f32[16,32,128]{2,1,0:T(8,128)}, u32[]{:S(2)}) copy-start(f32[16,32,128]{2,1,0:T(8,128)} %copy-done.2) | copy-start | bytes 786436
where the time goes:
time: 411 us; the launch traced here: 410 us
  blocking collectives  277 us (67%)
  waiting for transfers between devices  71.8 us (17%)
  starting transfers between devices  22.6 us (5%)
  matrix products  18.9 us (5%)
  local copies, waits for them, and re-layouts  17.6 us (4%)
    all_gather x16, blocking collectives, picked(): lax.all_gather(array, axis)  277 us
    all_to_all x1, waiting for transfers between devices, sum_at_owner(): lax.all_to_all(split_up(array, dim, devices), axis, 0, 0, tiled=True)  29 us
    all_to_all x2, waiting for transfers between devices, from_everyone(): return lax.all_to_all(copies, axis, split_axis=0, concat_axis=0, tiled=True)  22.8 us
    all_to_all x1, waiting for transfers between devices, in_one_piece(): lax.all_to_all(both, axis, split_axis=split_dim, concat_axis=concat_dim,...  19.9 us
    all_to_all x2, starting transfers between devices, from_everyone(): return lax.all_to_all(copies, axis, split_axis=0, concat_axis=0, tiled=True)  10.6 us
    dot_general x16, matrix products, advance(): carried = jnp.einsum('jkf,jfe->ke', slices, upper_strip, precision=highest)  9.94 us
  transfers between devices with their start and end apart: 4, of which 4 were waited for; matrix products, arithmetic and copies ran while one was open for 3% of the time, Pallas kernels for 0%

commit v1 on v0

v1 whole, which is shorter than its diff:
```python
import jax
import jax.numpy as jnp
from jax import lax
from jax.experimental import pallas as pl
from jax.experimental.pallas import tpu as pltpu
from jax.sharding import Mesh
from jax.sharding import PartitionSpec as P

HIGHEST = lax.Precision.HIGHEST
ROW = ("x", "yh")
COL = ("yl", "z", "core")
PLANE = ("z", "core")
BLOCK = 128


def rotated(array, axis, step):
    size = lax.axis_size(axis)
    return lax.ppermute(array, axis, [(i, (i + step) % size) for i in range(size)])


def around(array, axis):
    steps = range(1, lax.axis_size(axis))
    return jnp.stack([array] + [rotated(array, axis, step) for step in steps])


def to_everyone(array, axis):
    copies = jnp.broadcast_to(array, (lax.axis_size(axis), *array.shape))
    return lax.all_to_all(copies, axis, split_axis=0, concat_axis=0, tiled=True)


def split_bf16(value):
    high = value.astype(jnp.bfloat16)
    low = (value - high.astype(jnp.float32)).astype(jnp.bfloat16)
    return high, low


def solve_kernel(place_ref, start_ref, even_ref, odd_ref, out_ref):
    my_x, my_z, my_core = place_ref[0], place_ref[1], place_ref[2]
    blocks = start_ref.shape[0]
    rhs = start_ref.shape[1]

    def factor(j, i):
        dx = lax.rem(my_x - j // 2 + 4, 4)
        dz = lax.rem(my_z - i // 2 + 4, 4)
        dcore = lax.rem(my_core + i, 2)
        if j % 2 == 0:
            return even_ref[dcore, dz, dx]
        return odd_ref[dcore, dx, dz]

    rest = [start_ref[i] for i in range(blocks)]
    for j in range(blocks):
        done = rest[j]
        out_ref[j] = done
        high, low = split_bf16(done)
        both = jnp.concatenate([high, low], axis=0)
        for i in range(j + 1, blocks):
            w_high, w_low = split_bf16(factor(j, i))
            first = jnp.dot(both, w_high, preferred_element_type=jnp.float32)
            second = jnp.dot(high, w_low, preferred_element_type=jnp.float32)
            rest[i] = rest[i] - (first[:rhs] + first[rhs:] + second)


def solve_plane(place, start, even, odd):
    vmem = pl.BlockSpec(memory_space=pltpu.VMEM)
    return pl.pallas_call(
        solve_kernel,
        out_shape=jax.ShapeDtypeStruct(start.shape, jnp.float32),
        in_specs=[pl.BlockSpec(memory_space=pltpu.SMEM), vmem, vmem, vmem],
        out_specs=vmem,
        cost_estimate=pl.CostEstimate(flops=600_000_000, bytes_accessed=5_000_000, transcendentals=0),
    )(place, start, even, odd)


def per_device(incoming, block_map, panel_row, diag_inverse):
    my_x, my_yl, my_z, my_core = (lax.axis_index(a) for a in ("x", "yl", "z", "core"))
    my_yh = lax.axis_index("yh")
    my_col = lax.axis_index(COL)
    rows, cols = lax.axis_size(ROW), lax.axis_size(COL)
    plane = lax.axis_size(PLANE)
    sources = incoming.shape[2]
    share = BLOCK // rows
    slots = panel_row.shape[3]

    inverse = diag_inverse.reshape(BLOCK, BLOCK)
    upper = panel_row.reshape(2, BLOCK, slots, BLOCK)
    scaled = jnp.einsum("tpf,ef->tpe", upper[:, :, 0, :], inverse, precision=HIGHEST)
    mine = jnp.where(my_yl == 0, scaled[0], scaled[1])

    other = lax.ppermute(mine, "yh", [(0, 1), (1, 0)])
    even = jnp.where(my_yh == 0, mine, other)
    odd = jnp.where(my_yh == 0, other, mine)
    even = around(around(even, "x"), "z")
    odd = around(around(odd, "z"), "x")
    even = around(even, "core")
    odd = around(odd, "core")
    coupling = to_everyone(scaled[0], ROW)

    targets = block_map.reshape(sources)
    pieces = incoming.reshape(sources, rows, share, BLOCK)
    columns = jnp.arange(cols, dtype=jnp.int32)
    chosen = (targets[None, :] % cols) == columns[:, None]
    outgoing = jnp.zeros((rows, cols, share, BLOCK), jnp.float32)
    for u in range(sources):
        outgoing = jnp.where(chosen[None, :, u, None, None], pieces[u][:, None], outgoing)
    labels = jnp.max(jnp.where(chosen, targets[None, :] // cols, -1), axis=1).astype(jnp.float32)
    labels = jnp.broadcast_to(labels[None, :, None, None, None], (rows, cols, 1, 1, BLOCK))
    packed = jnp.concatenate([outgoing.reshape(rows, cols, share, 1, BLOCK), labels], axis=2)
    packed = packed.reshape(rows * cols, share + 1, 1, BLOCK)
    received = lax.all_to_all(packed, ROW + COL, 0, 0, tiled=True)
    slot_of = received[:, share, 0, 0].astype(jnp.int32)
    data = received[:, :share, 0, :]
    panel_rhs = jnp.sum(jnp.where((slot_of == 0)[:, None, None], data, 0.0), axis=0)
    matches = (slot_of[None, :] == jnp.arange(1, slots, dtype=jnp.int32)[:, None]).astype(jnp.float32)
    trailing_rhs = jnp.einsum("sq,qke->kse", matches, data, precision=HIGHEST)
    start = jnp.einsum("kf,ef->ke", panel_rhs, inverse, precision=HIGHEST)

    place = jnp.stack([my_x, my_z, my_core]).astype(jnp.int32)
    first = solve_plane(place, to_everyone(start, PLANE), even, odd)
    passed = lax.ppermute(first, "yl", [(0, 1)])
    carried = jnp.einsum("jkp,jpe->ke", passed, coupling, precision=HIGHEST)
    second = solve_plane(place, to_everyone(start - carried, PLANE), even, odd)
    solved = jnp.where(my_yl == 0, first, second)
    panel_solution = lax.dynamic_index_in_dim(solved, my_z * 2 + my_core, 0, keepdims=False)

    copies = jnp.broadcast_to(solved[:, None], (rows, 2, share, BLOCK))
    copies = copies.reshape(rows * 2, share, BLOCK)
    own_rows = lax.all_to_all(copies, ROW + ("yl",), 0, 0, tiled=True)
    own_rows = own_rows.reshape(rows, 2, share, BLOCK)
    partial = jnp.einsum("rtkp,tpse->rkse", own_rows, upper[:, :, 1:, :], precision=HIGHEST)
    parts = lax.all_to_all(partial, ROW, 0, 0, tiled=True)
    trailing = trailing_rhs - jnp.sum(parts, axis=0)
    return panel_solution[:, None, None, :], trailing[:, :, None, :]


def solution(mesh):
    fine = Mesh(mesh.devices.reshape(4, 2, 2, 4, 2), ("x", "yh", "yl", "z", "core"))
    in_specs = (
        P(ROW, COL, None, None, None),
        P(ROW, COL, None),
        P(None, ROW, None, None, COL, None),
        P(None, COL, None, None),
    )
    out_specs = (P(ROW, None, COL, None), P(ROW, None, COL, None))
    return jax.shard_map(
        per_device, mesh=fine, in_specs=in_specs, out_specs=out_specs, check_vma=False
    )
```

time: 411 us -> 185 us (0.45)
  blocking collectives: 277 us -> 25.9 us
  starting transfers between devices: 22.6 us -> 46.6 us
  other arithmetic: 0.96 us -> 17.5 us
  matrix products: 18.9 us -> 8.22 us
  Pallas kernels: 0 us -> 7.54 us
  local copies, waits for them, and re-layouts: 17.6 us -> 10.8 us
  waiting for transfers between devices: 71.8 us -> 67.1 us
    all_gather x16 -> x0, blocking collectives: 277 us -> none  [picked(): lax.all_gather(array, axis)]
    all_to_all x4, waiting for transfers between devices: 71.8 us -> 33.2 us  [the longest x1 27.5 us: per_device(): parts = lax.all_to_all(partial, ROW, 0, 0, tiled=True)]
    ppermute x0 -> x16, waiting for transfers between devices: none -> 33.9 us  [the longest x14 31.7 us: rotated(): lax.ppermute(array, axis, [(i, (i + step) % size) for i in range(size)])]
    all_to_all x0 -> x2, blocking collectives: none -> 25.9 us  [the longest x1 17.2 us: per_device(): own_rows = lax.all_to_all(copies, ROW + ('yl',), 0, 0, tiled=True)]
    ppermute x0 -> x16, starting transfers between devices: none -> 22.4 us  [the longest x14 16.5 us: rotated(): lax.ppermute(array, axis, [(i, (i + step) % size) for i in range(size)])]
    dot_general x36 -> x5, matrix products: 18.9 us -> 8.22 us  [the longest x1 5.74 us: per_device(): jnp.einsum('rtkp,tpse->rkse', own_rows, upper[:, :, 1:, :], precision=HIG...]
    another operation x0 -> x7, other arithmetic: none -> 9.29 us  [the longest x6 8.7 us: around(): return jnp.stack([array] + [rotated(array, axis, step) for step in steps])]
    pallas_call x0 -> x2, Pallas kernels: none -> 7.54 us  [solve_plane(): pl.pallas_call(solve_kernel, out_shape=jax.ShapeDtypeStruct(start.shape,...]
  transfers between devices with their start and end apart: 4 -> 20, of which waited for: 4 -> 10; matrix products, arithmetic and copies ran while one was open for 3% -> 11% of each run, Pallas kernels for 0% -> 2%
where the time goes in v1:
time: 185 us
  waiting for transfers between devices  67.1 us (36%)
  starting transfers between devices  46.6 us (25%)
  blocking collectives  25.9 us (14%)
  other arithmetic  17.5 us (9%)
  local copies, waits for them, and re-layouts  10.8 us (6%)
  matrix products  8.22 us (4%)
  Pallas kernels  7.54 us (4%)
    ppermute x14, waiting for transfers between devices, rotated(): lax.ppermute(array, axis, [(i, (i + step) % size) for i in range(size)])  31.7 us
    all_to_all x1, waiting for transfers between devices, per_device(): parts = lax.all_to_all(partial, ROW, 0, 0, tiled=True)  27.5 us
    all_to_all x1, blocking collectives, per_device(): own_rows = lax.all_to_all(copies, ROW + ('yl',), 0, 0, tiled=True)  17.2 us
    ppermute x14, starting transfers between devices, rotated(): lax.ppermute(array, axis, [(i, (i + step) % size) for i in range(size)])  16.5 us
    all_to_all x2, starting transfers between devices, to_everyone(): return lax.all_to_all(copies, axis, split_axis=0, concat_axis=0, tiled=True)  11.7 us
    all_to_all x1, starting transfers between devices, per_device(): received = lax.all_to_all(packed, ROW + COL, 0, 0, tiled=True)  8.92 us
    another operation x6, other arithmetic, around(): return jnp.stack([array] + [rotated(array, axis, step) for step in steps])  8.7 us
    all_to_all x1, blocking collectives, to_everyone(): return lax.all_to_all(copies, axis, split_axis=0, concat_axis=0, tiled=True)  8.67 us
  transfers between devices with their start and end apart: 20, of which 10 were waited for; matrix products, arithmetic and copies ran while one was open for 11% of the time, Pallas kernels for 2%

profile of v1, /device:TPU:0, one launch (start us, length us, event | category | flops | bytes accessed | tf_op | source)
XLA Modules:
  0.0 184.5 jit_solution(8170271163995309430)
XLA Ops:
  0.6 0.0 copy-start
  0.7 6.6 %copy.35 = f32[2,1,128,32,1,128]{5,2,0,3,4,1:T(8,128)} copy(f32[2,1,128,32,1,128]{5,4,3,2,1,0:T(1,128)} %param.6) | data formatting | bytes 8388608 | tf_op args[2]
  7.3 1.2 fusion.5
  8.5 3.4 %collective-permute-start = (f32[128,128]{1,0:T(8,128)S(1)}, f32[128,128]{1,0:T(8,128)S(1)}, u32[]{:S(2)}, u32[]{:S(2)}) collective-permute-start(f32[128,128]{1,0:T(8,128)S(1)} %fusion.6), channel_id=1, source_target_pairs={{0,16},{16,0},{1,17},{17,1},{2,18},{18,2},{3,19},{19,3},{4,20},{20... | collective-permute-start | bytes 196616 | tf_op jit(solution)/shard_map/ppermute | solution.py:89
  11.9 0.1 iota_compare_fusion
  12.0 0.1 select_reduce_fusion.1
  12.1 0.1 broadcast_in_dim.180
  12.2 0.1 broadcast_in_dim.150
  12.3 0.1 broadcast_in_dim.157
  12.4 0.1 broadcast_in_dim.171
  12.5 0.1 broadcast_in_dim.164
  12.6 0.1 broadcast_in_dim.153
  12.7 0.1 broadcast_in_dim.160
  12.8 0.1 broadcast_in_dim.167
  12.8 0.1 broadcast_in_dim.174
  12.9 3.1 %broadcast_select_fusion.2 = f32[128,16,1,128]{3,2,1,0:T(1,128)S(1)} fusion(f32[128,16,1,128]{3,2,1,0:T(1,128)S(1)} %bitcast.124, pred[128]{0:T(512)(128)(4,1)S(1)} %broadcast_in_dim.150, f32[128,16,1,128]{3,2,1,0:T(1,128)S(1)} %bitcast.125, pred[128]{0:T(512)(128)(4,1)S(1)} %broadcast_in_dim.157, f32[128,16,1,128]{3,2,1,0:T(1,128)S(1)} %bitcast.126, ...), kind=kLoop, calls=%fused_computation.7 | loop fusion | flops 1048576 | bytes 5243392 | tf_op jit(solution)/shard_map/jit(_where)/select_n | solution.py:104
  16.0 0.2 broadcast_in_dim.181
  16.2 2.0 %pad_maximum_fusion.2 = f32[128,17,1,128]{3,2,1,0:T(1,128)} fusion(f32[128,1,1,128]{3,2,1,0:T(1,128)S(1)} %broadcast_in_dim.181, f32[128,16,1,128]{3,2,1,0:T(1,128)S(1)} %broadcast_select_fusion.2), kind=kLoop, calls=%fused_computation.13 | loop fusion | flops 278528 | bytes 2228224 | tf_op jit(solution)/shard_map/concatenate | solution.py:107
  18.2 8.9 %all-to-all-start = ((f32[128,17,1,128]{3,2,1,0:T(1,128)}), f32[128,17,1,128]{3,2,1,0:T(1,128)S(1)}, u32[]{:S(2)}, u32[]{:S(2)}) async-start(f32[128,17,1,128]{3,2,1,0:T(1,128)} %pad_maximum_fusion.2), calls=%async_computation | async-start | bytes 2228224 | tf_op jit(solution)/shard_map/all_to_all | solution.py:109
  27.2 2.2 %collective-permute-start.3 = (f32[128,128]{1,0:T(8,128)S(1)}, f32[128,128]{1,0:T(8,128)S(1)}, u32[]{:S(2)}, u32[]{:S(2)}) collective-permute-start(f32[128,128]{1,0:T(8,128)S(1)} %get-tuple-element.23), channel_id=1, source_target_pairs={{0,96},{32,0},{64,32},{96,64},{1,97},{33,1},{65,33},{97,65},{2,98}... | collective-permute-start | bytes 196616 | tf_op jit(solution)/shard_map/ppermute | solution.py:18
  29.4 0.9 collective-permute-start.2
  30.3 0.9 collective-permute-start.1
  31.1 11.2 %collective-permute-done.3 = f32[128,128]{1,0:T(8,128)S(1)} collective-permute-done((f32[128,128]{1,0:T(8,128)S(1)}, f32[128,128]{1,0:T(8,128)S(1)}, u32[]{:S(2)}, u32[]{:S(2)}) %collective-permute-start.3) | collective-permute-done | bytes 65568 | tf_op jit(solution)/shard_map/ppermute | solution.py:18
  42.3 1.5 collective-permute-done.2
  43.8 0.5 collective-permute-done.1
  44.4 3.5 %collective-permute-start.6 = (f32[4,128,128]{2,1,0:T(8,128)S(1)}, f32[4,128,128]{2,1,0:T(8,128)S(1)}, u32[]{:S(2)}, u32[]{:S(2)}) collective-permute-start(f32[4,128,128]{2,1,0:T(8,128)S(1)} %get-tuple-element.17), channel_id=1, source_target_pairs={{0,6},{2,0},{4,2},{6,4},{1,7},{3,1},{5,3},{7,5},{8,14},{10,8},{12,... | collective-permute-start | bytes 786440 | tf_op jit(solution)/shard_map/ppermute | solution.py:18
  47.9 0.6 collective-permute-start.10
  48.4 0.1 collective-permute-start.9
  48.6 1.3 collective-permute-start.8
  49.9 4.1 %collective-permute-start.5 = (f32[4,128,128]{2,1,0:T(8,128)S(1)}, f32[4,128,128]{2,1,0:T(8,128)S(1)}, u32[]{:S(2)}, u32[]{:S(2)}) collective-permute-start(f32[4,128,128]{2,1,0:T(8,128)S(1)} %get-tuple-element.17), channel_id=1, source_target_pairs={{0,4},{2,6},{4,0},{6,2},{1,5},{3,7},{5,1},{7,3},{8,12},{10,14},{12... | collective-permute-start | bytes 786440 | tf_op jit(solution)/shard_map/ppermute | solution.py:18
  54.0 7.6 %collective-permute-done.10 = f32[128,128]{1,0:T(8,128)S(1)} collective-permute-done((f32[128,128]{1,0:T(8,128)S(1)}, f32[128,128]{1,0:T(8,128)S(1)}, u32[]{:S(2)}, u32[]{:S(2)}) %collective-permute-start.10) | collective-permute-done | bytes 65568 | tf_op jit(solution)/shard_map/ppermute | solution.py:18
  61.7 1.4 collective-permute-start.13
  63.1 1.5 collective-permute-start.12
  64.6 6.0 %collective-permute-done.4 = f32[4,128,128]{2,1,0:T(8,128)S(1)} collective-permute-done((f32[4,128,128]{2,1,0:T(8,128)S(1)}, f32[4,128,128]{2,1,0:T(8,128)S(1)}, u32[]{:S(2)}, u32[]{:S(2)}) %collective-permute-start.4) | collective-permute-done | bytes 262176 | tf_op jit(solution)/shard_map/ppermute | solution.py:18
  70.6 1.3 fusion.18
  71.9 1.9 %collective-permute-done.12 = f32[4,128,128]{2,1,0:T(8,128)S(1)} collective-permute-done((f32[4,128,128]{2,1,0:T(8,128)S(1)}, f32[4,128,128]{2,1,0:T(8,128)S(1)}, u32[]{:S(2)}, u32[]{:S(2)}) %collective-permute-start.12) | collective-permute-done | bytes 262176 | tf_op jit(solution)/shard_map/ppermute | solution.py:18
  73.8 2.9 %collective-permute-done.11 = f32[4,128,128]{2,1,0:T(8,128)S(1)} collective-permute-done((f32[4,128,128]{2,1,0:T(8,128)S(1)}, f32[4,128,128]{2,1,0:T(8,128)S(1)}, u32[]{:S(2)}, u32[]{:S(2)}) %collective-permute-start.11) | collective-permute-done | bytes 262176 | tf_op jit(solution)/shard_map/ppermute | solution.py:18
  76.7 1.7 fusion.17
  78.4 0.1 slice.62
  78.5 2.4 %fusion.7 = s32[128]{0:T(128)S(1)} fusion(f32[128,17,1,128]{3,2,1,0:T(1,128)S(1)} %all-to-all-done), kind=kLoop, calls=%fused_computation.28 | loop fusion | flops 128 | bytes 1024 | tf_op jit(solution)/shard_map/convert_element_type | solution.py:110
  80.9 0.4 select_reduce_fusion
  81.2 0.2 fusion.9
  81.4 0.7 broadcast_in_dim.184
  82.1 6.4 %all-to-all-start.1 = ((f32[8,16,128]{2,1,0:T(8,128)}), f32[8,16,128]{2,1,0:T(8,128)S(1)}, u32[]{:S(2)}, u32[]{:S(2)}) async-start(f32[8,16,128]{2,1,0:T(8,128)} %broadcast_in_dim.184), calls=%async_computation.1 | async-start | bytes 131072 | tf_op jit(solution)/shard_map/all_to_all | solution.py:28
  88.5 5.6 %all-to-all-done.1.start_ref = f32[8,16,128]{2,1,0:T(8,128)S(1)} async-done(((f32[8,16,128]{2,1,0:T(8,128)}), f32[8,16,128]{2,1,0:T(8,128)S(1)}, u32[]{:S(2)}, u32[]{:S(2)}) %all-to-all-start.1) | async-done | bytes 65568 | tf_op jit(solution)/shard_map/all_to_all | solution.py:28
  94.1 0.8 broadcast_in_dim.185
  94.9 5.3 %all-to-all-start.2 = ((f32[8,128,128]{2,1,0:T(8,128)}), f32[8,128,128]{2,1,0:T(8,128)S(1)}, u32[]{:S(2)}, u32[]{:S(2)}) async-start(f32[8,128,128]{2,1,0:T(8,128)} %broadcast_in_dim.185), calls=%async_computation.2 | async-start | bytes 1048576 | tf_op jit(solution)/shard_map/all_to_all | solution.py:28
  100.3 0.6 pad_add_fusion.place_ref
  100.8 2.9 %pad_maximum_fusion.even_ref = f32[2,4,4,128,128]{4,3,2,1,0:T(8,128)} fusion(f32[1,4,4,128,128]{4,3,2,1,0:T(8,128)} %bitcast.32, f32[1,4,4,128,128]{4,3,2,1,0:T(8,128)S(1)} %get-tuple-element.12), kind=kLoop, calls=%fused_computation.3 | loop fusion | flops 524288 | bytes 4194304 | tf_op jit(solution)/shard_map/stack | solution.py:23
  103.7 2.8 %pad_maximum_fusion.1.odd_ref = f32[2,4,4,128,128]{4,3,2,1,0:T(8,128)} fusion(f32[1,4,4,128,128]{4,3,2,1,0:T(8,128)} %bitcast.42, f32[1,4,4,128,128]{4,3,2,1,0:T(8,128)S(1)} %copy-done.1), kind=kLoop, calls=%fused_computation.4 | loop fusion | flops 524288 | bytes 4194304 | tf_op jit(solution)/shard_map/stack | solution.py:23
  106.5 3.8 %shard_map.59 = f32[8,16,128]{2,1,0:T(8,128)} custom-call(s32[3]{0:T(128)} %pad_add_fusion.place_ref, f32[8,16,128]{2,1,0:T(8,128)} %copy-done.3, f32[2,4,4,128,128]{4,3,2,1,0:T(8,128)} %pad_maximum_fusion.even_ref, f32[2,4,4,128,128]{4,3,2,1,0:T(8,128)} %pad_maximum_fusion.1.odd_ref), custom_call_target="tpu_custom_call" | custom-call | flops 600000000 | bytes 5000000 | tf_op jit(solution)/shard_map/pallas_call | solution.py:65
  110.3 2.5 %collective-permute-start.15 = (f32[8,16,128]{2,1,0:T(8,128)}, f32[8,16,128]{2,1,0:T(8,128)S(1)}, u32[]{:S(2)}, u32[]{:S(2)}) collective-permute-start(f32[8,16,128]{2,1,0:T(8,128)} %shard_map.59), channel_id=1, source_target_pairs={{0,8},{1,9},{2,10},{3,11},{4,12},{5,13},{6,14},{7,15},{16,24},{17,... | collective-permute-start | bytes 196616 | tf_op jit(solution)/shard_map/ppermute | solution.py:119
  112.8 2.2 %collective-permute-done.15 = f32[8,16,128]{2,1,0:T(8,128)S(1)} collective-permute-done((f32[8,16,128]{2,1,0:T(8,128)}, f32[8,16,128]{2,1,0:T(8,128)S(1)}, u32[]{:S(2)}, u32[]{:S(2)}) %collective-permute-start.15) | collective-permute-done | bytes 65568 | tf_op jit(solution)/shard_map/ppermute | solution.py:119
  115.0 0.4 fusion.4
  115.4 8.7 %all_to_all.30.start_ref = f32[8,16,128]{2,1,0:T(8,128)} all-to-all(f32[8,16,128]{2,1,0:T(8,128)S(1)} %broadcast_in_dim.186), channel_id=1, replica_groups=mesh['x'=4,'yh'=2,'yl'=2,'z'=4,'core'=2] {'z','core'}, dimensions={0} | all-to-all | bytes 131072 | tf_op jit(solution)/shard_map/all_to_all | solution.py:28
  124.1 3.8 %shard_map.60 = f32[8,16,128]{2,1,0:T(8,128)} custom-call(s32[3]{0:T(128)} %pad_add_fusion.place_ref, f32[8,16,128]{2,1,0:T(8,128)} %all_to_all.30.start_ref, f32[2,4,4,128,128]{4,3,2,1,0:T(8,128)} %pad_maximum_fusion.even_ref, f32[2,4,4,128,128]{4,3,2,1,0:T(8,128)} %pad_maximum_fusion.1.odd_ref), custom_call_target="tpu_custom_call" | custom-call | flops 600000000 | bytes 5000000 | tf_op jit(solution)/shard_map/pallas_call | solution.py:65
  127.9 17.2 %all_to_all.31 = f32[16,16,128]{2,1,0:T(8,128)S(1)} all-to-all(f32[16,16,128]{2,1,0:T(8,128)S(1)} %bitcast.129), channel_id=1, replica_groups=mesh['x'=4,'yh'=2,'yl'=2,'z'=4,'core'=2] {'x','yh','yl'}, dimensions={0} | all-to-all | bytes 262144 | tf_op jit(solution)/shard_map/all_to_all | solution.py:127
  145.1 5.7 %fusion.1 = f32[8,16,31,128]{3,1,2,0:T(8,128)} fusion(f32[8,2,16,128,1]{3,2,1,4,0:T(8,128)S(1)} %bitcast.128, f32[2,128,32,128]{3,1,0,2:T(8,128)} %bitcast.123), kind=kOutput, calls=%fused_computation.9 | convolution fusion | flops 1560281088 | bytes 6225920 | tf_op jit(solution)/shard_map/rtkp,tpse->rkse/dot_general | solution.py:129
  150.8 3.6 %all-to-all-start.5 = ((f32[8,16,31,128]{3,1,2,0:T(8,128)}), f32[8,16,31,128]{3,1,2,0:T(8,128)S(1)}, u32[]{:S(2)}, u32[]{:S(2)}) async-start(f32[8,16,31,128]{3,1,2,0:T(8,128)} %fusion.1), calls=%async_computation.5 | async-start | bytes 4063232 | tf_op jit(solution)/shard_map/all_to_all | solution.py:130
  154.5 0.6 constant_dynamic-slice_fusion
  155.1 27.5 %all-to-all-done.5 = f32[8,16,31,128]{3,1,2,0:T(8,128)S(1)} async-done(((f32[8,16,31,128]{3,1,2,0:T(8,128)}), f32[8,16,31,128]{3,1,2,0:T(8,128)S(1)}, u32[]{:S(2)}, u32[]{:S(2)}) %all-to-all-start.5) | async-done | bytes 2031648 | tf_op jit(solution)/shard_map/all_to_all | solution.py:130
  182.6 0.1 reduce_sum.19
  182.8 0.8 fusion.3
  183.5 1.0 copy.25
  (44 shorter events, 0.3 us)
Async XLA Ops:
  0.6 6.6 %copy-start = (f32[1,1,128,128]{3,2,1,0:T(8,128)S(1)}, f32[1,1,128,128]{3,2,1,0:T(8,128)}, u32[]{:S(2)}) copy-start(f32[1,1,128,128]{3,2,1,0:T(8,128)} %param.7) | copy-start | bytes 196612
  0.6 11.2 %copy-start.5 = (s32[1,1,4]{2,1,0:T(1,128)S(1)}, s32[1,1,4]{2,1,0:T(1,128)}, u32[]{:S(2)}) copy-start(s32[1,1,4]{2,1,0:T(1,128)} %param.5) | copy-start | bytes 52
  0.7 11.5 %copy-start.4 = (f32[1,1,4,128,128]{4,3,2,1,0:T(8,128)S(1)}, f32[1,1,4,128,128]{4,3,2,1,0:T(8,128)}, u32[]{:S(2)}) copy-start(f32[1,1,4,128,128]{4,3,2,1,0:T(8,128)} %param.4) | copy-start | bytes 786436
  8.5 18.7 %collective-permute-start = (f32[128,128]{1,0:T(8,128)S(1)}, f32[128,128]{1,0:T(8,128)S(1)}, u32[]{:S(2)}, u32[]{:S(2)}) collective-permute-start(f32[128,128]{1,0:T(8,128)S(1)} %fusion.6), channel_id=1, source_target_pairs={{0,16},{16,0},{1,17},{17,1},{2,18},{18,2},{3,19},{19,3},{4,20},{20... | collective-permute-start | bytes 196616 | tf_op jit(solution)/shard_map/ppermute | solution.py:89
  18.2 60.2 %all-to-all-start = ((f32[128,17,1,128]{3,2,1,0:T(1,128)}), f32[128,17,1,128]{3,2,1,0:T(1,128)S(1)}, u32[]{:S(2)}, u32[]{:S(2)}) async-start(f32[128,17,1,128]{3,2,1,0:T(1,128)} %pad_maximum_fusion.2), calls=%async_computation | async-start | bytes 2228224 | tf_op jit(solution)/shard_map/all_to_all | solution.py:109
  27.2 15.1 %collective-permute-start.3 = (f32[128,128]{1,0:T(8,128)S(1)}, f32[128,128]{1,0:T(8,128)S(1)}, u32[]{:S(2)}, u32[]{:S(2)}) collective-permute-start(f32[128,128]{1,0:T(8,128)S(1)} %get-tuple-element.23), channel_id=1, source_target_pairs={{0,96},{32,0},{64,32},{96,64},{1,97},{33,1},{65,33},{97,65},{2,98}... | collective-permute-start | bytes 196616 | tf_op jit(solution)/shard_map/ppermute | solution.py:18
  29.4 14.4 %collective-permute-start.2 = (f32[128,128]{1,0:T(8,128)S(1)}, f32[128,128]{1,0:T(8,128)S(1)}, u32[]{:S(2)}, u32[]{:S(2)}) collective-permute-start(f32[128,128]{1,0:T(8,128)S(1)} %get-tuple-element.23), channel_id=1, source_target_pairs={{0,64},{32,96},{64,0},{96,32},{1,65},{33,97},{65,1},{97,33},{2,66}... | collective-permute-start | bytes 196616 | tf_op jit(solution)/shard_map/ppermute | solution.py:18
  30.3 14.1 %collective-permute-start.1 = (f32[128,128]{1,0:T(8,128)S(1)}, f32[128,128]{1,0:T(8,128)S(1)}, u32[]{:S(2)}, u32[]{:S(2)}) collective-permute-start(f32[128,128]{1,0:T(8,128)S(1)} %get-tuple-element.23), channel_id=1, source_target_pairs={{0,32},{32,64},{64,96},{96,0},{1,33},{33,65},{65,97},{97,1},{2,34}... | collective-permute-start | bytes 196616 | tf_op jit(solution)/shard_map/ppermute | solution.py:18
  44.4 20.2 %collective-permute-start.6 = (f32[4,128,128]{2,1,0:T(8,128)S(1)}, f32[4,128,128]{2,1,0:T(8,128)S(1)}, u32[]{:S(2)}, u32[]{:S(2)}) collective-permute-start(f32[4,128,128]{2,1,0:T(8,128)S(1)} %get-tuple-element.17), channel_id=1, source_target_pairs={{0,6},{2,0},{4,2},{6,4},{1,7},{3,1},{5,3},{7,5},{8,14},{10,8},{12,... | collective-permute-start | bytes 786440 | tf_op jit(solution)/shard_map/ppermute | solution.py:18
  47.9 13.8 %collective-permute-start.10 = (f32[128,128]{1,0:T(8,128)S(1)}, f32[128,128]{1,0:T(8,128)S(1)}, u32[]{:S(2)}, u32[]{:S(2)}) collective-permute-start(f32[128,128]{1,0:T(8,128)S(1)} %get-tuple-element.22), channel_id=1, source_target_pairs={{0,6},{2,0},{4,2},{6,4},{1,7},{3,1},{5,3},{7,5},{8,14},{10,8},{12,... | collective-permute-start | bytes 196616 | tf_op jit(solution)/shard_map/ppermute | solution.py:18
  48.4 13.2 %collective-permute-start.9 = (f32[128,128]{1,0:T(8,128)S(1)}, f32[128,128]{1,0:T(8,128)S(1)}, u32[]{:S(2)}, u32[]{:S(2)}) collective-permute-start(f32[128,128]{1,0:T(8,128)S(1)} %get-tuple-element.22), channel_id=1, source_target_pairs={{0,4},{2,6},{4,0},{6,2},{1,5},{3,7},{5,1},{7,3},{8,12},{10,14},{12... | collective-permute-start | bytes 196616 | tf_op jit(solution)/shard_map/ppermute | solution.py:18
  48.6 13.1 %collective-permute-start.8 = (f32[128,128]{1,0:T(8,128)S(1)}, f32[128,128]{1,0:T(8,128)S(1)}, u32[]{:S(2)}, u32[]{:S(2)}) collective-permute-start(f32[128,128]{1,0:T(8,128)S(1)} %get-tuple-element.22), channel_id=1, source_target_pairs={{0,2},{2,4},{4,6},{6,0},{1,3},{3,5},{5,7},{7,1},{8,10},{10,12},{12... | collective-permute-start | bytes 196616 | tf_op jit(solution)/shard_map/ppermute | solution.py:18
  49.9 14.7 %collective-permute-start.5 = (f32[4,128,128]{2,1,0:T(8,128)S(1)}, f32[4,128,128]{2,1,0:T(8,128)S(1)}, u32[]{:S(2)}, u32[]{:S(2)}) collective-permute-start(f32[4,128,128]{2,1,0:T(8,128)S(1)} %get-tuple-element.17), channel_id=1, source_target_pairs={{0,4},{2,6},{4,0},{6,2},{1,5},{3,7},{5,1},{7,3},{8,12},{10,14},{12... | collective-permute-start | bytes 786440 | tf_op jit(solution)/shard_map/ppermute | solution.py:18
  61.7 8.9 %collective-permute-start.4 = (f32[4,128,128]{2,1,0:T(8,128)S(1)}, f32[4,128,128]{2,1,0:T(8,128)S(1)}, u32[]{:S(2)}, u32[]{:S(2)}) collective-permute-start(f32[4,128,128]{2,1,0:T(8,128)S(1)} %get-tuple-element.17), channel_id=1, source_target_pairs={{0,2},{2,4},{4,6},{6,0},{1,3},{3,5},{5,7},{7,1},{8,10},{10,12},{12... | collective-permute-start | bytes 786440 | tf_op jit(solution)/shard_map/ppermute | solution.py:18
  61.7 10.2 %collective-permute-start.13 = (f32[4,128,128]{2,1,0:T(8,128)S(1)}, f32[4,128,128]{2,1,0:T(8,128)S(1)}, u32[]{:S(2)}, u32[]{:S(2)}) collective-permute-start(f32[4,128,128]{2,1,0:T(8,128)S(1)} %get-tuple-element.15), channel_id=1, source_target_pairs={{0,96},{32,0},{64,32},{96,64},{1,97},{33,1},{65,33},{97,65},{2,98}... | collective-permute-start | bytes 786440 | tf_op jit(solution)/shard_map/ppermute | solution.py:18
  63.1 10.7 %collective-permute-start.12 = (f32[4,128,128]{2,1,0:T(8,128)S(1)}, f32[4,128,128]{2,1,0:T(8,128)S(1)}, u32[]{:S(2)}, u32[]{:S(2)}) collective-permute-start(f32[4,128,128]{2,1,0:T(8,128)S(1)} %get-tuple-element.15), channel_id=1, source_target_pairs={{0,64},{32,96},{64,0},{96,32},{1,65},{33,97},{65,1},{97,33},{2,66}... | collective-permute-start | bytes 786440 | tf_op jit(solution)/shard_map/ppermute | solution.py:18
  64.6 12.1 %collective-permute-start.11 = (f32[4,128,128]{2,1,0:T(8,128)S(1)}, f32[4,128,128]{2,1,0:T(8,128)S(1)}, u32[]{:S(2)}, u32[]{:S(2)}) collective-permute-start(f32[4,128,128]{2,1,0:T(8,128)S(1)} %get-tuple-element.15), channel_id=1, source_target_pairs={{0,32},{32,64},{64,96},{96,0},{1,33},{33,65},{65,97},{97,1},{2,34}... | collective-permute-start | bytes 786440 | tf_op jit(solution)/shard_map/ppermute | solution.py:18
  71.9 29.0 %collective-permute-start.7 = (f32[4,4,128,128]{3,2,1,0:T(8,128)}, f32[4,4,128,128]{3,2,1,0:T(8,128)}, u32[]{:S(2)}, u32[]{:S(2)}) collective-permute-start(f32[4,4,128,128]{3,2,1,0:T(8,128)} %get-tuple-element.13), channel_id=1, source_target_pairs={{0,1},{1,0},{2,3},{3,2},{4,5},{5,4},{6,7},{7,6},{8,9},{9,8},{10,11... | collective-permute-start | bytes 3145736 | tf_op jit(solution)/shard_map/ppermute | solution.py:18
  78.4 25.3 %collective-permute-start.14 = (f32[4,4,128,128]{3,2,1,0:T(8,128)}, f32[4,4,128,128]{3,2,1,0:T(8,128)}, u32[]{:S(2)}, u32[]{:S(2)}) collective-permute-start(f32[4,4,128,128]{3,2,1,0:T(8,128)} %get-tuple-element.11), channel_id=1, source_target_pairs={{0,1},{1,0},{2,3},{3,2},{4,5},{5,4},{6,7},{7,6},{8,9},{9,8},{10,11... | collective-permute-start | bytes 3145736 | tf_op jit(solution)/shard_map/ppermute | solution.py:18
  82.1 12.0 %all-to-all-start.1 = ((f32[8,16,128]{2,1,0:T(8,128)}), f32[8,16,128]{2,1,0:T(8,128)S(1)}, u32[]{:S(2)}, u32[]{:S(2)}) async-start(f32[8,16,128]{2,1,0:T(8,128)} %broadcast_in_dim.184), calls=%async_computation.1 | async-start | bytes 131072 | tf_op jit(solution)/shard_map/all_to_all | solution.py:28
  94.1 9.6 %copy-start.3 = (f32[8,16,128]{2,1,0:T(8,128)}, f32[8,16,128]{2,1,0:T(8,128)S(1)}, u32[]{:S(2)}) copy-start(f32[8,16,128]{2,1,0:T(8,128)S(1)} %all-to-all-done.1.start_ref) | copy-start | bytes 196612
  94.9 17.9 %all-to-all-start.2 = ((f32[8,128,128]{2,1,0:T(8,128)}), f32[8,128,128]{2,1,0:T(8,128)S(1)}, u32[]{:S(2)}, u32[]{:S(2)}) async-start(f32[8,128,128]{2,1,0:T(8,128)} %broadcast_in_dim.185), calls=%async_computation.2 | async-start | bytes 1048576 | tf_op jit(solution)/shard_map/all_to_all | solution.py:28
  100.8 2.9 %copy-start.1 = (f32[1,4,4,128,128]{4,3,2,1,0:T(8,128)S(1)}, f32[1,4,4,128,128]{4,3,2,1,0:T(8,128)}, u32[]{:S(2)}) copy-start(f32[1,4,4,128,128]{4,3,2,1,0:T(8,128)} %get-tuple-element.10) | copy-start | bytes 3145732
  110.3 4.7 %collective-permute-start.15 = (f32[8,16,128]{2,1,0:T(8,128)}, f32[8,16,128]{2,1,0:T(8,128)S(1)}, u32[]{:S(2)}, u32[]{:S(2)}) collective-permute-start(f32[8,16,128]{2,1,0:T(8,128)} %shard_map.59), channel_id=1, source_target_pairs={{0,8},{1,9},{2,10},{3,11},{4,12},{5,13},{6,14},{7,15},{16,24},{17,... | collective-permute-start | bytes 196616 | tf_op jit(solution)/shard_map/ppermute | solution.py:119
  124.1 3.8 %copy-start.2 = (f32[8,16,128]{2,1,0:T(8,128)S(1)}, f32[8,16,128]{2,1,0:T(8,128)}, u32[]{:S(2)}) copy-start(f32[8,16,128]{2,1,0:T(8,128)} %shard_map.59) | copy-start | bytes 196612
  150.8 31.8 %all-to-all-start.5 = ((f32[8,16,31,128]{3,1,2,0:T(8,128)}), f32[8,16,31,128]{3,1,2,0:T(8,128)S(1)}, u32[]{:S(2)}, u32[]{:S(2)}) async-start(f32[8,16,31,128]{3,1,2,0:T(8,128)} %fusion.1), calls=%async_computation.5 | async-start | bytes 4063232 | tf_op jit(solution)/shard_map/all_to_all | solution.py:130

commit v2 on v1

v2 whole, which is shorter than its diff:
```python
import jax
import jax.numpy as jnp
from jax import lax
from jax.experimental import pallas as pl
from jax.experimental.pallas import tpu as pltpu
from jax.sharding import Mesh
from jax.sharding import PartitionSpec as P


HIGHEST = lax.Precision.HIGHEST
ROW = ("x", "yh")
COL = ("yl", "z", "core")
PLANE = ("z", "core")
BLOCK = 128
HALF = 8
VMEM = pl.BlockSpec(memory_space=pltpu.VMEM)
SMEM = pl.BlockSpec(memory_space=pltpu.SMEM)


def rotated(array, axis, step):
    size = lax.axis_size(axis)
    return lax.ppermute(array, axis, [(i, (i + step) % size) for i in range(size)])


def around(array, axis):
    steps = range(1, lax.axis_size(axis))
    return [array] + [rotated(array, axis, step) for step in steps]


def split_bf16(value):
    high = value.astype(jnp.bfloat16)
    low = (value - high.astype(jnp.float32)).astype(jnp.bfloat16)
    return high, low


def product(left, right, right_dim=0):
    l_high, l_low = left
    r_high, r_low = split_bf16(right)
    dims = (((1,), (right_dim,)), ((), ()))
    both = jnp.concatenate([l_high, l_low], axis=0)
    first = lax.dot_general(both, r_high, dims, preferred_element_type=jnp.float32)
    second = lax.dot_general(l_high, r_low, dims, preferred_element_type=jnp.float32)
    rows = l_high.shape[0]
    return first[:rows] + first[rows:] + second


def solve_blocks(place_ref, start, even_refs, odd_refs):
    my_x, my_z, my_core = place_ref[0], place_ref[1], place_ref[2]

    def factor(j, i):
        dx = lax.rem(my_x - j // 2 + 4, 4)
        dz = lax.rem(my_z - i // 2 + 4, 4)
        own_ref, other_ref = even_refs if j % 2 == 0 else odd_refs
        at = (dz, dx) if j % 2 == 0 else (dx, dz)
        return jnp.where(my_core == i % 2, own_ref[at], other_ref[at])

    rest = [product(split_bf16(start(i)), factor(i, i), 1) for i in range(HALF)]
    for j in range(HALF):
        done = split_bf16(rest[j])
        for i in range(j + 1, HALF):
            rest[i] = rest[i] - product(done, factor(j, i))
    return rest


def first_kernel(place_ref, start_ref, e0_ref, e1_ref, o0_ref, o1_ref, out_ref):
    solved = solve_blocks(
        place_ref, lambda i: start_ref[i], (e0_ref, e1_ref), (o0_ref, o1_ref)
    )
    for i in range(HALF):
        out_ref[i] = solved[i]


def coupling_kernel(place_ref, start_ref, passed_ref, x_ref, out_ref):
    my_x, my_z, my_core = place_ref[0], place_ref[1], place_ref[2]
    total = start_ref[my_z * 2 + my_core]
    for j in range(HALF):
        dx = lax.rem(my_x - j // 2 + 4, 4)
        total = total - product(split_bf16(passed_ref[j]), x_ref[dx, j % 2])
    out_ref[...] = total


def second_kernel(place_ref, start_ref, first_ref, e0_ref, e1_ref, o0_ref, o1_ref, out_ref):
    my_z, my_core = place_ref[1], place_ref[2]

    def start(i):
        return start_ref[lax.rem(my_z - i // 2 + 4, 4), lax.rem(my_core + i, 2)]

    solved = solve_blocks(place_ref, start, (e0_ref, e1_ref), (o0_ref, o1_ref))
    for i in range(HALF):
        block = jnp.where(place_ref[3] == 0, first_ref[i], solved[i])
        out_ref[i, 0] = block
        out_ref[i, 1] = block


def local_kernel(kernel, shape, *args):
    return pl.pallas_call(
        kernel,
        out_shape=jax.ShapeDtypeStruct(shape, jnp.float32),
        in_specs=[SMEM] + [VMEM] * (len(args) - 1),
        out_specs=VMEM,
        cost_estimate=pl.CostEstimate(flops=600_000_000, bytes_accessed=5_000_000, transcendentals=0),
    )(*args)


def per_device(incoming, block_map, panel_row, diag_inverse):
    my_x, my_yh, my_yl, my_z, my_core = (lax.axis_index(a) for a in ("x", "yh", "yl", "z", "core"))
    my_row = lax.axis_index(ROW)
    my_plane = lax.axis_index(PLANE)
    rows, cols = lax.axis_size(ROW), lax.axis_size(COL)
    sources = incoming.shape[2]
    share = BLOCK // rows
    slots = panel_row.shape[3]
    place = jnp.stack([my_x, my_z, my_core, my_yl]).astype(jnp.int32)

    targets = block_map.reshape(sources)
    blocks = incoming.reshape(sources, BLOCK, BLOCK)
    pieces = blocks.reshape(sources, rows, share, BLOCK).transpose(1, 0, 2, 3)
    labels = jnp.concatenate([targets, targets]).astype(jnp.float32)
    labels = jnp.broadcast_to(labels[None, :, None], (rows, 2 * sources, BLOCK))
    packed = jnp.concatenate([pieces.reshape(rows, sources * share, BLOCK), labels], axis=1)

    inverse = diag_inverse.reshape(BLOCK, BLOCK)
    upper = panel_row.reshape(2, BLOCK, slots, BLOCK)
    panel = upper[:, :, 0, :]
    scaled = jnp.einsum("tpf,ef->tpe", panel, inverse, precision=HIGHEST)
    mine = jnp.where(my_yl == 0, scaled[0], scaled[1])
    mine = jnp.where(my_row == my_plane, inverse, mine)

    pair = jnp.stack([mine, panel[0]])
    other = lax.ppermute(pair, "yh", [(0, 1), (1, 0)])
    even = jnp.where(my_yh == 0, pair, other)
    odd = jnp.where(my_yh == 0, other, pair)
    received = lax.all_to_all(packed, ROW, 0, 0, tiled=True)
    by_x = around(jnp.stack([even[0], even[1], odd[1]]), "x")
    by_z = around(odd[0], "z")
    coupling = jnp.stack([p[1:] for p in by_x])
    even = jnp.stack([p[0] for p in by_x])
    upper, even = lax.optimization_barrier((upper, even))
    even = jnp.stack(around(even, "z"))
    odd = jnp.stack(around(jnp.stack(by_z), "x"))

    data = received[:, : sources * share].reshape(rows, sources, share, BLOCK)
    label = received[:, sources * share : sources * share + sources, None, :]

    def belonging(half):
        wanted = (half * HALF + jnp.arange(HALF, dtype=jnp.int32)).astype(jnp.float32)
        return jnp.sum(
            jnp.where(label[None] == wanted[:, None, None, None, None], data[None], 0.0), axis=(1, 2)
        )

    start = belonging(my_yl) + rotated(belonging(1 - my_yl), "yl", 1)
    start = start + rotated(start, "core", 1)
    start = sum(around(start, "z"))

    even_other = rotated(even, "core", 1)
    odd_other = rotated(odd, "core", 1)
    factors = (even, even_other, odd, odd_other)

    chosen = (targets[None, :] % cols) == jnp.arange(cols, dtype=jnp.int32)[:, None]
    outgoing = jnp.zeros((cols, BLOCK, BLOCK), jnp.float32)
    for u in range(sources):
        outgoing = jnp.where(chosen[:, u, None, None], blocks[u][None], outgoing)
    slot_label = jnp.max(jnp.where(chosen, targets[None, :] // cols, -1), axis=1)
    slot_label = jnp.broadcast_to(slot_label.astype(jnp.float32)[:, None, None], (cols, 8, BLOCK))
    outgoing = jnp.concatenate([outgoing, slot_label], axis=1)

    shape = (HALF, share, BLOCK)
    first = local_kernel(first_kernel, shape, place, start, *factors)
    passed = lax.ppermute(first, "yl", [(0, 1)])
    arrived = lax.all_to_all(outgoing, COL, 0, 0, tiled=True)
    residual = local_kernel(
        coupling_kernel, (share, BLOCK), place, start, passed, coupling
    )
    residual = jnp.stack(around(jnp.stack(around(residual, "core")), "z"))
    copies = local_kernel(
        second_kernel, (HALF, 2, share, BLOCK), place, residual, first, *factors
    )
    copies, arrived = lax.optimization_barrier((copies, arrived))
    panel_solution = lax.dynamic_index_in_dim(copies[:, 0], my_plane, 0, keepdims=False)

    own_rows = lax.all_to_all(
        copies.reshape(rows * 2, share, BLOCK), ROW + ("yl",), 0, 0, tiled=True
    ).reshape(rows, 2, share, BLOCK)
    slot_of = arrived[:, BLOCK, 0].astype(jnp.int32)
    matches = (slot_of[None, :] == jnp.arange(1, slots, dtype=jnp.int32)[:, None]).astype(jnp.float32)
    held = arrived[:, :BLOCK].reshape(cols, rows, share, BLOCK)
    held = jnp.einsum("sq,qrke->rkse", matches, held, precision=HIGHEST)
    partial = held - jnp.einsum(
        "rtkp,tpse->rkse", own_rows, upper[:, :, 1:, :], precision=lax.Precision.HIGH
    )
    trailing = lax.dynamic_index_in_dim(partial, my_row, 0, keepdims=False)
    for step in range(1, rows):
        part = lax.dynamic_index_in_dim(partial, my_row ^ step, 0, keepdims=False)
        trailing = trailing + lax.ppermute(part, ROW, [(i, i ^ step) for i in range(rows)])
    return panel_solution[:, None, None, :], trailing[:, :, None, :]


def solution(mesh):
    fine = Mesh(mesh.devices.reshape(4, 2, 2, 4, 2), ("x", "yh", "yl", "z", "core"))
    in_specs = (
        P(ROW, COL, None, None, None),
        P(ROW, COL, None),
        P(None, ROW, None, None, COL, None),
        P(None, COL, None, None),
    )
    out_specs = (P(ROW, None, COL, None), P(ROW, None, COL, None))
    return jax.shard_map(per_device, mesh=fine, in_specs=in_specs, out_specs=out_specs, check_vma=False)
```

time: 185 us -> 163 us (0.88)
  blocking collectives: 25.9 us -> 0 us
  starting transfers between devices: 46.6 us -> 67.4 us
  waiting for transfers between devices: 67.1 us -> 56.6 us
  other arithmetic: 17.5 us -> 7.74 us
  local copies, waits for them, and re-layouts: 10.8 us -> 14.5 us
  matrix products: 8.22 us -> 5.44 us
  Pallas kernels: 7.54 us -> 10 us
    all_to_all x4 -> x3, waiting for transfers between devices: 33.2 us -> 6.7 us  [the longest x1 6.69 us: per_device(): lax.all_to_all(copies.reshape(rows * 2, share, BLOCK), ROW + ('yl',), 0,...]
    all_to_all x2 -> x0, blocking collectives: 25.9 us -> none  [the longest x1 17.2 us: per_device(): own_rows = lax.all_to_all(copies, ROW + ('yl',), 0, 0, tiled=True)]
    ppermute x1 -> x8, waiting for transfers between devices: 0.01 us -> 16.3 us  [the longest x7 16.3 us: per_device(): lax.ppermute(part, ROW, [(i, i ^ step) for i in range(rows)])]
    ppermute x14 -> x23, starting transfers between devices: 16.5 us -> 31.5 us  [rotated(): lax.ppermute(array, axis, [(i, (i + step) % size) for i in range(size)])]
    ppermute x1 -> x8, starting transfers between devices: 3.39 us -> 18 us  [the longest x7 14.6 us: per_device(): lax.ppermute(part, ROW, [(i, i ^ step) for i in range(rows)])]
    all_to_all x4 -> x3, starting transfers between devices: 24.2 us -> 14.5 us  [the longest x1 6.49 us: per_device(): lax.all_to_all(copies.reshape(rows * 2, share, BLOCK), ROW + ('yl',), 0,...]
    another operation x7 -> x11, other arithmetic: 9.29 us -> 2.98 us  [the longest x2 1.33 us: per_device(): residual = jnp.stack(around(jnp.stack(around(residual, 'core')), 'z'))]
    dot_general x5 -> x3, matrix products: 8.22 us -> 5.44 us  [the longest x1 3.4 us: per_device(): jnp.einsum('rtkp,tpse->rkse', own_rows, upper[:, :, 1:, :], precision=lax...]
  transfers between devices with their start and end apart: 20 -> 35, of which waited for: 10 -> 20; matrix products, arithmetic and copies ran while one was open for 11% -> 8% of each run, Pallas kernels for 2% -> 6%
where the time goes in v2:
time: 163 us
  starting transfers between devices  67.4 us (41%)
  waiting for transfers between devices  56.6 us (35%)
  local copies, waits for them, and re-layouts  14.5 us (9%)
  Pallas kernels  10 us (6%)
  other arithmetic  7.74 us (5%)
  matrix products  5.44 us (3%)
    ppermute x23, waiting for transfers between devices, rotated(): lax.ppermute(array, axis, [(i, (i + step) % size) for i in range(size)])  32.3 us
    ppermute x23, starting transfers between devices, rotated(): lax.ppermute(array, axis, [(i, (i + step) % size) for i in range(size)])  31.5 us
    ppermute x7, waiting for transfers between devices, per_device(): lax.ppermute(part, ROW, [(i, i ^ step) for i in range(rows)])  16.3 us
    ppermute x7, starting transfers between devices, per_device(): lax.ppermute(part, ROW, [(i, i ^ step) for i in range(rows)])  14.6 us
    pallas_call x3, Pallas kernels, local_kernel(): pl.pallas_call(kernel, out_shape=jax.ShapeDtypeStruct(shape, jnp.float32)...  10 us
    unnamed x22, local copies, waits for them, and re-layouts  9.17 us
    all_to_all x1, waiting for transfers between devices, per_device(): lax.all_to_all(copies.reshape(rows * 2, share, BLOCK), ROW + ('yl',), 0,...  6.69 us
    all_to_all x1, starting transfers between devices, per_device(): lax.all_to_all(copies.reshape(rows * 2, share, BLOCK), ROW + ('yl',), 0,...  6.49 us
  transfers between devices with their start and end apart: 35, of which 20 were waited for; matrix products, arithmetic and copies ran while one was open for 8% of the time, Pallas kernels for 6%

profile of v2, /device:TPU:0, one launch (start us, length us, event | category | flops | bytes accessed | tf_op | source)
XLA Modules:
  0.0 162.8 jit_solution(6349734065769830616)
XLA Ops:
  0.7 4.7 %copy.90 = f32[2,1,128,32,1,128]{5,2,3,0,4,1:T(8,128)S(1)} copy(f32[2,1,128,32,1,128]{5,4,3,2,1,0:T(1,128)} %param.6) | data formatting | bytes 8388608 | tf_op args[2]
  5.4 1.9 %copy-done = f32[2,1,128,32,1,128]{5,2,3,0,4,1:T(8,128)} copy-done((f32[2,1,128,32,1,128]{5,2,3,0,4,1:T(8,128)}, f32[2,1,128,32,1,128]{5,2,3,0,4,1:T(8,128)S(1)}, u32[]{:S(2)}) %copy-start) | copy-done | bytes 4194328
  7.7 3.4 %collective-permute-start.5 = (f32[2,128,128]{2,1,0:T(8,128)S(1)}, f32[2,128,128]{2,1,0:T(8,128)S(1)}, u32[]{:S(2)}, u32[]{:S(2)}) collective-permute-start(f32[2,128,128]{2,1,0:T(8,128)S(1)} %pad_maximum_fusion.8), channel_id=1, source_target_pairs={{0,16},{16,0},{1,17},{17,1},{2,18},{18,2},{3,19},{19,3},{4,20},{20... | collective-permute-start | bytes 393224 | tf_op jit(solution)/shard_map/ppermute | solution.py:130
  11.2 0.8 pad_maximum_fusion.4
  12.0 4.3 %all-to-all-start = ((f32[8,72,128]{2,1,0:T(8,128)}), f32[8,72,128]{2,1,0:T(8,128)S(1)}, u32[]{:S(2)}, u32[]{:S(2)}) async-start(f32[8,72,128]{2,1,0:T(8,128)} %pad_maximum_fusion.4), calls=%async_computation | async-start | bytes 589824 | tf_op jit(solution)/shard_map/all_to_all | solution.py:133
  17.1 2.0 %collective-permute-start.13 = (f32[128,128]{1,0:T(8,128)S(1)}, f32[128,128]{1,0:T(8,128)S(1)}, u32[]{:S(2)}, u32[]{:S(2)}) collective-permute-start(f32[128,128]{1,0:T(8,128)S(1)} %get-tuple-element.39), channel_id=1, source_target_pairs={{0,2},{2,4},{4,6},{6,0},{1,3},{3,5},{5,7},{7,1},{8,10},{10,12},{12... | collective-permute-start | bytes 196616 | tf_op jit(solution)/shard_map/ppermute | solution.py:22
  19.1 3.6 %collective-permute-start.14 = (f32[128,128]{1,0:T(8,128)S(1)}, f32[128,128]{1,0:T(8,128)S(1)}, u32[]{:S(2)}, u32[]{:S(2)}) collective-permute-start(f32[128,128]{1,0:T(8,128)S(1)} %get-tuple-element.39), channel_id=1, source_target_pairs={{0,4},{2,6},{4,0},{6,2},{1,5},{3,7},{5,1},{7,3},{8,12},{10,14},{12... | collective-permute-start | bytes 196616 | tf_op jit(solution)/shard_map/ppermute | solution.py:22
  22.7 1.0 collective-permute-start.15
  23.7 3.3 %collective-permute-start.8 = (f32[3,128,128]{2,1,0:T(8,128)S(1)}, f32[3,128,128]{2,1,0:T(8,128)S(1)}, u32[]{:S(2)}, u32[]{:S(2)}) collective-permute-start(f32[3,128,128]{2,1,0:T(8,128)S(1)} %pad_maximum_fusion.7), channel_id=1, source_target_pairs={{0,96},{32,0},{64,32},{96,64},{1,97},{33,1},{65,33},{97,65},{2,98}... | collective-permute-start | bytes 589832 | tf_op jit(solution)/shard_map/ppermute | solution.py:22
  27.0 0.9 collective-permute-start.7
  27.9 0.9 collective-permute-start.6
  28.8 1.8 %collective-permute-start.16 = (f32[4,128,128]{2,1,0:T(8,128)S(1)}, f32[4,128,128]{2,1,0:T(8,128)S(1)}, u32[]{:S(2)}, u32[]{:S(2)}) collective-permute-start(f32[4,128,128]{2,1,0:T(8,128)S(1)} %get-tuple-element.35), channel_id=1, source_target_pairs={{0,32},{32,64},{64,96},{96,0},{1,33},{33,65},{65,97},{97,1},{2,34}... | collective-permute-start | bytes 786440 | tf_op jit(solution)/shard_map/ppermute | solution.py:22
  31.3 1.1 pad_maximum_fusion
  32.4 2.1 %collective-permute-start.17 = (f32[4,128,128]{2,1,0:T(8,128)S(1)}, f32[4,128,128]{2,1,0:T(8,128)S(1)}, u32[]{:S(2)}, u32[]{:S(2)}) collective-permute-start(f32[4,128,128]{2,1,0:T(8,128)S(1)} %get-tuple-element.35), channel_id=1, source_target_pairs={{0,64},{32,96},{64,0},{96,32},{1,65},{33,97},{65,1},{97,33},{2,66}... | collective-permute-start | bytes 786440 | tf_op jit(solution)/shard_map/ppermute | solution.py:22
  34.5 3.7 %all-to-all-start.1 = ((f32[16,136,128]{2,1,0:T(8,128)}), f32[16,136,128]{2,1,0:T(8,128)S(1)}, u32[]{:S(2)}, u32[]{:S(2)}) async-start(f32[16,136,128]{2,1,0:T(8,128)} %pad_maximum_fusion), calls=%async_computation.1 | async-start | bytes 2228224 | tf_op jit(solution)/shard_map/all_to_all | solution.py:170
  38.7 2.4 %collective-permute-start.18 = (f32[4,128,128]{2,1,0:T(8,128)S(1)}, f32[4,128,128]{2,1,0:T(8,128)S(1)}, u32[]{:S(2)}, u32[]{:S(2)}) collective-permute-start(f32[4,128,128]{2,1,0:T(8,128)S(1)} %get-tuple-element.35), channel_id=1, source_target_pairs={{0,96},{32,0},{64,32},{96,64},{1,97},{33,1},{65,33},{97,65},{2,98}... | collective-permute-start | bytes 786440 | tf_op jit(solution)/shard_map/ppermute | solution.py:22
  41.1 0.8 slice.132
  42.0 1.1 collective-permute-start.9
  43.1 2.0 %collective-permute-start.10 = (f32[4,128,128]{2,1,0:T(8,128)S(1)}, f32[4,128,128]{2,1,0:T(8,128)S(1)}, u32[]{:S(2)}, u32[]{:S(2)}) collective-permute-start(f32[4,128,128]{2,1,0:T(8,128)S(1)} %pad_maximum_fusion.5), channel_id=1, source_target_pairs={{0,4},{2,6},{4,0},{6,2},{1,5},{3,7},{5,1},{7,3},{8,12},{10,14},{12... | collective-permute-start | bytes 786440 | tf_op jit(solution)/shard_map/ppermute | solution.py:22
  45.1 0.8 collective-permute-done.16
  45.9 0.7 collective-permute-start.11
  46.7 2.0 %collective-permute-done.17 = f32[4,128,128]{2,1,0:T(8,128)S(1)} collective-permute-done((f32[4,128,128]{2,1,0:T(8,128)S(1)}, f32[4,128,128]{2,1,0:T(8,128)S(1)}, u32[]{:S(2)}, u32[]{:S(2)}) %collective-permute-start.17) | collective-permute-done | bytes 262176 | tf_op jit(solution)/shard_map/ppermute | solution.py:22
  48.9 11.3 %collective-permute-done.9 = f32[4,128,128]{2,1,0:T(8,128)S(1)} collective-permute-done((f32[4,128,128]{2,1,0:T(8,128)S(1)}, f32[4,128,128]{2,1,0:T(8,128)S(1)}, u32[]{:S(2)}, u32[]{:S(2)}) %collective-permute-start.9) | collective-permute-done | bytes 262176 | tf_op jit(solution)/shard_map/ppermute | solution.py:22
  60.2 5.6 %collective-permute-done.10 = f32[4,128,128]{2,1,0:T(8,128)S(1)} collective-permute-done((f32[4,128,128]{2,1,0:T(8,128)S(1)}, f32[4,128,128]{2,1,0:T(8,128)S(1)}, u32[]{:S(2)}, u32[]{:S(2)}) %collective-permute-start.10) | collective-permute-done | bytes 262176 | tf_op jit(solution)/shard_map/ppermute | solution.py:22
  66.7 1.6 collective-permute-start
  68.3 2.9 %collective-permute-done = f32[8,16,128]{2,1,0:T(8,128)S(1)} collective-permute-done((f32[8,16,128]{2,1,0:T(8,128)S(1)}, f32[8,16,128]{2,1,0:T(8,128)S(1)}, u32[]{:S(2)}, u32[]{:S(2)}) %collective-permute-start) | collective-permute-done | bytes 65568 | tf_op jit(solution)/shard_map/ppermute | solution.py:22
  71.4 0.9 slice_bitcast_fusion.1
  72.7 2.1 %collective-permute-start.3 = (f32[8,16,128]{2,1,0:T(8,128)S(1)}, f32[8,16,128]{2,1,0:T(8,128)S(1)}, u32[]{:S(2)}, u32[]{:S(2)}) collective-permute-start(f32[8,16,128]{2,1,0:T(8,128)S(1)} %add.120), channel_id=1, source_target_pairs={{0,4},{2,6},{4,0},{6,2},{1,5},{3,7},{5,1},{7,3},{8,12},{10,14},{12... | collective-permute-start | bytes 196616 | tf_op jit(solution)/shard_map/ppermute | solution.py:22
  74.7 1.7 %collective-permute-start.4 = (f32[8,16,128]{2,1,0:T(8,128)S(1)}, f32[8,16,128]{2,1,0:T(8,128)S(1)}, u32[]{:S(2)}, u32[]{:S(2)}) collective-permute-start(f32[8,16,128]{2,1,0:T(8,128)S(1)} %add.120), channel_id=1, source_target_pairs={{0,6},{2,0},{4,2},{6,4},{1,7},{3,1},{5,3},{7,5},{8,14},{10,8},{12,... | collective-permute-start | bytes 196616 | tf_op jit(solution)/shard_map/ppermute | solution.py:22
  76.5 3.0 %collective-permute-done.2 = f32[8,16,128]{2,1,0:T(8,128)S(1)} collective-permute-done((f32[8,16,128]{2,1,0:T(8,128)S(1)}, f32[8,16,128]{2,1,0:T(8,128)S(1)}, u32[]{:S(2)}, u32[]{:S(2)}) %collective-permute-start.2) | collective-permute-done | bytes 65568 | tf_op jit(solution)/shard_map/ppermute | solution.py:22
  80.1 0.6 add_add_fusion.start_ref
  80.7 1.0 copy-done.3
  81.7 4.0 %shard_map.59.first_ref = f32[8,16,128]{2,1,0:T(8,128)} custom-call(s32[4]{0:T(128)} %pad_add_fusion.place_ref, f32[8,16,128]{2,1,0:T(8,128)} %add_add_fusion.start_ref, f32[4,4,128,128]{3,2,1,0:T(8,128)} %copy-done.2, f32[4,4,128,128]{3,2,1,0:T(8,128)} %collective-permute-done.12.e1_ref, f32[4,4,128,128]{3,2,1,0:T(8,128)} %copy-done.1, ...), custom_call_target="tpu_custom_call" | custom-call | flops 600000000 | bytes 5000000 | tf_op jit(solution)/shard_map/pallas_call | solution.py:96
  85.7 3.4 %collective-permute-start.20 = (f32[8,16,128]{2,1,0:T(8,128)}, f32[8,16,128]{2,1,0:T(8,128)S(1)}, u32[]{:S(2)}, u32[]{:S(2)}) collective-permute-start(f32[8,16,128]{2,1,0:T(8,128)} %shard_map.59.first_ref), channel_id=1, source_target_pairs={{0,8},{1,9},{2,10},{3,11},{4,12},{5,13},{6,14},{7,15},{16,24},{17,... | collective-permute-start | bytes 196616 | tf_op jit(solution)/shard_map/ppermute | solution.py:169
  89.0 0.9 pad_maximum_fusion.3.x_ref
  89.9 1.3 collective-permute-done.20.passed_ref
  91.3 0.6 copy-done.8
  91.9 2.0 %shard_map.60 = f32[16,128]{1,0:T(8,128)} custom-call(s32[4]{0:T(128)} %pad_add_fusion.place_ref, f32[8,16,128]{2,1,0:T(8,128)} %add_add_fusion.start_ref, f32[8,16,128]{2,1,0:T(8,128)} %copy-done.8, f32[4,2,128,128]{3,2,1,0:T(8,128)} %pad_maximum_fusion.3.x_ref), custom_call_target="tpu_custom_call" | custom-call | flops 600000000 | bytes 5000000 | tf_op jit(solution)/shard_map/pallas_call | solution.py:96
  93.9 1.4 collective-permute-done.21
  95.2 0.7 fusion.22
  95.9 1.0 collective-permute-start.22
  97.0 3.1 %collective-permute-start.23 = (f32[2,16,128]{2,1,0:T(8,128)S(1)}, f32[2,16,128]{2,1,0:T(8,128)S(1)}, u32[]{:S(2)}, u32[]{:S(2)}) collective-permute-start(f32[2,16,128]{2,1,0:T(8,128)S(1)} %get-tuple-element.42), channel_id=1, source_target_pairs={{0,4},{2,6},{4,0},{6,2},{1,5},{3,7},{5,1},{7,3},{8,12},{10,14},{12... | collective-permute-start | bytes 49160 | tf_op jit(solution)/shard_map/ppermute | solution.py:22
  100.1 0.8 collective-permute-done.22
  100.9 1.3 collective-permute-done.23
  102.2 1.6 collective-permute-done.24
  103.8 0.6 pad_maximum_fusion.9.start_ref
  104.5 4.0 %shard_map.61 = f32[8,2,16,128]{3,2,1,0:T(8,128)} custom-call(s32[4]{0:T(128)} %pad_add_fusion.place_ref, f32[4,2,16,128]{3,2,1,0:T(8,128)} %pad_maximum_fusion.9.start_ref, f32[8,16,128]{2,1,0:T(8,128)} %shard_map.59.first_ref, f32[4,4,128,128]{3,2,1,0:T(8,128)} %copy-done.2, f32[4,4,128,128]{3,2,1,0:T(8,128)} %collective-permute-done.12.e1_ref, ...), custom_call_target="tpu_custom_call" | custom-call | flops 600000000 | bytes 5000000 | tf_op jit(solution)/shard_map/pallas_call | solution.py:96
  108.5 6.5 %all-to-all-start.2 = ((f32[16,16,128]{2,1,0:T(8,128)}), f32[16,16,128]{2,1,0:T(8,128)S(1)}, u32[]{:S(2)}, u32[]{:S(2)}) async-start(f32[16,16,128]{2,1,0:T(8,128)} %bitcast.148), calls=%async_computation.2 | async-start | bytes 262144 | tf_op jit(solution)/shard_map/all_to_all | solution.py:181
  116.2 6.7 %all-to-all-done.2 = f32[16,16,128]{2,1,0:T(8,128)S(1)} async-done(((f32[16,16,128]{2,1,0:T(8,128)}), f32[16,16,128]{2,1,0:T(8,128)S(1)}, u32[]{:S(2)}, u32[]{:S(2)}) %all-to-all-start.2) | async-done | bytes 131104 | tf_op jit(solution)/shard_map/all_to_all | solution.py:181
  122.9 3.4 %fusion.3 = f32[8,16,31,128]{3,1,2,0:T(8,128)S(1)} fusion(f32[8,2,16,128,1]{3,2,1,4,0:T(8,128)S(1)} %bitcast.149, f32[2,128,32,128]{3,1,2,0:T(8,128)} %bitcast.142), kind=kOutput, calls=%fused_computation.7 | convolution fusion | flops 780140544 | bytes 6225920 | tf_op jit(solution)/shard_map/rtkp,tpse->rkse/dot_general | solution.py:188
  126.3 1.8 %bitcast_subtract_fusion = f32[8,16,31,128]{3,2,1,0:T(8,128)S(1)} fusion(f32[8,16,31,128]{3,1,2,0:T(8,128)S(1)} %fusion.3, f32[16,8,16,128]{3,0,2,1:T(8,128)S(1)} %bitcast.143, s32[31]{0:T(128)S(1)} %iota_add_fusion, s32[16]{0:T(128)S(1)} %convert_reduce_fusion), kind=kOutput, calls=%fused_computation.4 | convolution fusion | flops 98025968 | bytes 5111996 | tf_op jit(solution)/shard_map/sq,qrke->rkse/dot_general | solution.py:187
  128.4 1.6 collective-permute-start.25
  130.9 3.1 %collective-permute-start.27 = (f32[16,31,128]{2,0,1:T(8,128)S(1)}, f32[16,31,128]{2,0,1:T(8,128)S(1)}, u32[]{:S(2)}, u32[]{:S(2)}) collective-permute-start(f32[16,31,128]{2,0,1:T(8,128)S(1)} %bitcast.156), channel_id=1, source_target_pairs={{0,48},{16,32},{32,16},{48,0},{64,112},{80,96},{96,80},{112,64},{1... | collective-permute-start | bytes 761864 | tf_op jit(solution)/shard_map/ppermute | solution.py:194
  134.1 1.3 collective-permute-start.28
  135.6 3.3 %collective-permute-start.29 = (f32[16,31,128]{2,0,1:T(8,128)S(1)}, f32[16,31,128]{2,0,1:T(8,128)S(1)}, u32[]{:S(2)}, u32[]{:S(2)}) collective-permute-start(f32[16,31,128]{2,0,1:T(8,128)S(1)} %bitcast.158), channel_id=1, source_target_pairs={{0,80},{16,64},{32,112},{48,96},{64,16},{80,0},{96,48},{112,32},{1... | collective-permute-start | bytes 761864 | tf_op jit(solution)/shard_map/ppermute | solution.py:194
  138.9 0.8 copy.92
  139.9 1.2 collective-permute-start.30
  141.1 3.6 %collective-permute-start.31 = (f32[16,31,128]{2,0,1:T(8,128)S(1)}, f32[16,31,128]{2,0,1:T(8,128)S(1)}, u32[]{:S(2)}, u32[]{:S(2)}) collective-permute-start(f32[16,31,128]{2,0,1:T(8,128)S(1)} %bitcast.159), channel_id=1, source_target_pairs={{0,112},{16,96},{32,80},{48,64},{64,48},{80,32},{96,16},{112,0},{1... | collective-permute-start | bytes 761864 | tf_op jit(solution)/shard_map/ppermute | solution.py:194
  145.3 0.8 collective-permute-done.27
  146.1 3.2 %collective-permute-done.28 = f32[16,31,128]{2,0,1:T(8,128)S(1)} collective-permute-done((f32[16,31,128]{2,0,1:T(8,128)S(1)}, f32[16,31,128]{2,0,1:T(8,128)S(1)}, u32[]{:S(2)}, u32[]{:S(2)}) %collective-permute-start.28) | collective-permute-done | bytes 253984 | tf_op jit(solution)/shard_map/ppermute | solution.py:194
  149.3 4.2 %collective-permute-done.29 = f32[16,31,128]{2,0,1:T(8,128)S(1)} collective-permute-done((f32[16,31,128]{2,0,1:T(8,128)S(1)}, f32[16,31,128]{2,0,1:T(8,128)S(1)}, u32[]{:S(2)}, u32[]{:S(2)}) %collective-permute-start.29) | collective-permute-done | bytes 253984 | tf_op jit(solution)/shard_map/ppermute | solution.py:194
  153.6 3.7 %collective-permute-done.30 = f32[16,31,128]{2,0,1:T(8,128)S(1)} collective-permute-done((f32[16,31,128]{2,0,1:T(8,128)}, f32[16,31,128]{2,0,1:T(8,128)S(1)}, u32[]{:S(2)}, u32[]{:S(2)}) %collective-permute-start.30) | collective-permute-done | bytes 253984 | tf_op jit(solution)/shard_map/ppermute | solution.py:194
  157.3 4.3 %collective-permute-done.31 = f32[16,31,128]{2,0,1:T(8,128)S(1)} collective-permute-done((f32[16,31,128]{2,0,1:T(8,128)S(1)}, f32[16,31,128]{2,0,1:T(8,128)S(1)}, u32[]{:S(2)}, u32[]{:S(2)}) %collective-permute-start.31) | collective-permute-done | bytes 253984 | tf_op jit(solution)/shard_map/ppermute | solution.py:194
  161.8 1.0 copy.70
  (94 shorter events, 8.3 us)
Async XLA Ops:
  0.6 6.7 %copy-start.7 = (f32[1,1,128,128]{3,2,1,0:T(8,128)S(1)}, f32[1,1,128,128]{3,2,1,0:T(8,128)}, u32[]{:S(2)}) copy-start(f32[1,1,128,128]{3,2,1,0:T(8,128)} %param.7) | copy-start | bytes 196612
  0.7 10.4 %copy-start.5 = (f32[1,1,4,128,128]{4,3,2,1,0:T(8,128)S(1)}, f32[1,1,4,128,128]{4,3,2,1,0:T(8,128)}, u32[]{:S(2)}) copy-start(f32[1,1,4,128,128]{4,3,2,1,0:T(8,128)} %param.4) | copy-start | bytes 786436
  0.7 10.4 %copy-start.9 = (s32[1,1,4]{2,1,0:T(1,128)S(1)}, s32[1,1,4]{2,1,0:T(1,128)}, u32[]{:S(2)}) copy-start(s32[1,1,4]{2,1,0:T(1,128)} %param.5) | copy-start | bytes 52
  5.3 2.0 %copy-start = (f32[2,1,128,32,1,128]{5,2,3,0,4,1:T(8,128)}, f32[2,1,128,32,1,128]{5,2,3,0,4,1:T(8,128)S(1)}, u32[]{:S(2)}) copy-start(f32[2,1,128,32,1,128]{5,2,3,0,4,1:T(8,128)S(1)} %copy.90) | copy-start | bytes 12582916
  7.7 9.4 %collective-permute-start.5 = (f32[2,128,128]{2,1,0:T(8,128)S(1)}, f32[2,128,128]{2,1,0:T(8,128)S(1)}, u32[]{:S(2)}, u32[]{:S(2)}) collective-permute-start(f32[2,128,128]{2,1,0:T(8,128)S(1)} %pad_maximum_fusion.8), channel_id=1, source_target_pairs={{0,16},{16,0},{1,17},{17,1},{2,18},{18,2},{3,19},{19,3},{4,20},{20... | collective-permute-start | bytes 393224 | tf_op jit(solution)/shard_map/ppermute | solution.py:130
  12.0 22.5 %all-to-all-start = ((f32[8,72,128]{2,1,0:T(8,128)}), f32[8,72,128]{2,1,0:T(8,128)S(1)}, u32[]{:S(2)}, u32[]{:S(2)}) async-start(f32[8,72,128]{2,1,0:T(8,128)} %pad_maximum_fusion.4), calls=%async_computation | async-start | bytes 589824 | tf_op jit(solution)/shard_map/all_to_all | solution.py:133
  17.1 10.8 %collective-permute-start.13 = (f32[128,128]{1,0:T(8,128)S(1)}, f32[128,128]{1,0:T(8,128)S(1)}, u32[]{:S(2)}, u32[]{:S(2)}) collective-permute-start(f32[128,128]{1,0:T(8,128)S(1)} %get-tuple-element.39), channel_id=1, source_target_pairs={{0,2},{2,4},{4,6},{6,0},{1,3},{3,5},{5,7},{7,1},{8,10},{10,12},{12... | collective-permute-start | bytes 196616 | tf_op jit(solution)/shard_map/ppermute | solution.py:22
  19.1 9.6 %collective-permute-start.14 = (f32[128,128]{1,0:T(8,128)S(1)}, f32[128,128]{1,0:T(8,128)S(1)}, u32[]{:S(2)}, u32[]{:S(2)}) collective-permute-start(f32[128,128]{1,0:T(8,128)S(1)} %get-tuple-element.39), channel_id=1, source_target_pairs={{0,4},{2,6},{4,0},{6,2},{1,5},{3,7},{5,1},{7,3},{8,12},{10,14},{12... | collective-permute-start | bytes 196616 | tf_op jit(solution)/shard_map/ppermute | solution.py:22
  22.7 6.1 %collective-permute-start.15 = (f32[128,128]{1,0:T(8,128)S(1)}, f32[128,128]{1,0:T(8,128)S(1)}, u32[]{:S(2)}, u32[]{:S(2)}) collective-permute-start(f32[128,128]{1,0:T(8,128)S(1)} %get-tuple-element.39), channel_id=1, source_target_pairs={{0,6},{2,0},{4,2},{6,4},{1,7},{3,1},{5,3},{7,5},{8,14},{10,8},{12,... | collective-permute-start | bytes 196616 | tf_op jit(solution)/shard_map/ppermute | solution.py:22
  23.7 18.2 %collective-permute-start.8 = (f32[3,128,128]{2,1,0:T(8,128)S(1)}, f32[3,128,128]{2,1,0:T(8,128)S(1)}, u32[]{:S(2)}, u32[]{:S(2)}) collective-permute-start(f32[3,128,128]{2,1,0:T(8,128)S(1)} %pad_maximum_fusion.7), channel_id=1, source_target_pairs={{0,96},{32,0},{64,32},{96,64},{1,97},{33,1},{65,33},{97,65},{2,98}... | collective-permute-start | bytes 589832 | tf_op jit(solution)/shard_map/ppermute | solution.py:22
  27.0 14.1 %collective-permute-start.7 = (f32[3,128,128]{2,1,0:T(8,128)S(1)}, f32[3,128,128]{2,1,0:T(8,128)}, u32[]{:S(2)}, u32[]{:S(2)}) collective-permute-start(f32[3,128,128]{2,1,0:T(8,128)S(1)} %pad_maximum_fusion.7), channel_id=1, source_target_pairs={{0,64},{32,96},{64,0},{96,32},{1,65},{33,97},{65,1},{97,33},{2,66}... | collective-permute-start | bytes 589832 | tf_op jit(solution)/shard_map/ppermute | solution.py:22
  27.9 10.8 %collective-permute-start.6 = (f32[3,128,128]{2,1,0:T(8,128)S(1)}, f32[3,128,128]{2,1,0:T(8,128)S(1)}, u32[]{:S(2)}, u32[]{:S(2)}) collective-permute-start(f32[3,128,128]{2,1,0:T(8,128)S(1)} %pad_maximum_fusion.7), channel_id=1, source_target_pairs={{0,32},{32,64},{64,96},{96,0},{1,33},{33,65},{65,97},{97,1},{2,34}... | collective-permute-start | bytes 589832 | tf_op jit(solution)/shard_map/ppermute | solution.py:22
  28.8 17.1 %collective-permute-start.16 = (f32[4,128,128]{2,1,0:T(8,128)S(1)}, f32[4,128,128]{2,1,0:T(8,128)S(1)}, u32[]{:S(2)}, u32[]{:S(2)}) collective-permute-start(f32[4,128,128]{2,1,0:T(8,128)S(1)} %get-tuple-element.35), channel_id=1, source_target_pairs={{0,32},{32,64},{64,96},{96,0},{1,33},{33,65},{65,97},{97,1},{2,34}... | collective-permute-start | bytes 786440 | tf_op jit(solution)/shard_map/ppermute | solution.py:22
  32.4 16.3 %collective-permute-start.17 = (f32[4,128,128]{2,1,0:T(8,128)S(1)}, f32[4,128,128]{2,1,0:T(8,128)S(1)}, u32[]{:S(2)}, u32[]{:S(2)}) collective-permute-start(f32[4,128,128]{2,1,0:T(8,128)S(1)} %get-tuple-element.35), channel_id=1, source_target_pairs={{0,64},{32,96},{64,0},{96,32},{1,65},{33,97},{65,1},{97,33},{2,66}... | collective-permute-start | bytes 786440 | tf_op jit(solution)/shard_map/ppermute | solution.py:22
  34.5 14.3 %copy-start.4 = (f32[8,72,128]{2,1,0:T(8,128)}, f32[8,72,128]{2,1,0:T(8,128)S(1)}, u32[]{:S(2)}) copy-start(f32[8,72,128]{2,1,0:T(8,128)S(1)} %all-to-all-done) | copy-start | bytes 884740
  34.5 74.0 %all-to-all-start.1 = ((f32[16,136,128]{2,1,0:T(8,128)}), f32[16,136,128]{2,1,0:T(8,128)S(1)}, u32[]{:S(2)}, u32[]{:S(2)}) async-start(f32[16,136,128]{2,1,0:T(8,128)} %pad_maximum_fusion), calls=%async_computation.1 | async-start | bytes 2228224 | tf_op jit(solution)/shard_map/all_to_all | solution.py:170
  38.7 10.0 %collective-permute-start.18 = (f32[4,128,128]{2,1,0:T(8,128)S(1)}, f32[4,128,128]{2,1,0:T(8,128)S(1)}, u32[]{:S(2)}, u32[]{:S(2)}) collective-permute-start(f32[4,128,128]{2,1,0:T(8,128)S(1)} %get-tuple-element.35), channel_id=1, source_target_pairs={{0,96},{32,0},{64,32},{96,64},{1,97},{33,1},{65,33},{97,65},{2,98}... | collective-permute-start | bytes 786440 | tf_op jit(solution)/shard_map/ppermute | solution.py:22
  42.0 18.2 %collective-permute-start.9 = (f32[4,128,128]{2,1,0:T(8,128)S(1)}, f32[4,128,128]{2,1,0:T(8,128)S(1)}, u32[]{:S(2)}, u32[]{:S(2)}) collective-permute-start(f32[4,128,128]{2,1,0:T(8,128)S(1)} %pad_maximum_fusion.5), channel_id=1, source_target_pairs={{0,2},{2,4},{4,6},{6,0},{1,3},{3,5},{5,7},{7,1},{8,10},{10,12},{12... | collective-permute-start | bytes 786440 | tf_op jit(solution)/shard_map/ppermute | solution.py:22
  43.1 22.8 %collective-permute-start.10 = (f32[4,128,128]{2,1,0:T(8,128)S(1)}, f32[4,128,128]{2,1,0:T(8,128)S(1)}, u32[]{:S(2)}, u32[]{:S(2)}) collective-permute-start(f32[4,128,128]{2,1,0:T(8,128)S(1)} %pad_maximum_fusion.5), channel_id=1, source_target_pairs={{0,4},{2,6},{4,0},{6,2},{1,5},{3,7},{5,1},{7,3},{8,12},{10,14},{12... | collective-permute-start | bytes 786440 | tf_op jit(solution)/shard_map/ppermute | solution.py:22
  45.9 20.0 %collective-permute-start.11 = (f32[4,128,128]{2,1,0:T(8,128)S(1)}, f32[4,128,128]{2,1,0:T(8,128)S(1)}, u32[]{:S(2)}, u32[]{:S(2)}) collective-permute-start(f32[4,128,128]{2,1,0:T(8,128)S(1)} %pad_maximum_fusion.5), channel_id=1, source_target_pairs={{0,6},{2,0},{4,2},{6,4},{1,7},{3,1},{5,3},{7,5},{8,14},{10,8},{12,... | collective-permute-start | bytes 786440 | tf_op jit(solution)/shard_map/ppermute | solution.py:22
  48.8 31.9 %copy-start.1 = (f32[4,4,128,128]{3,2,1,0:T(8,128)}, f32[4,4,128,128]{3,2,1,0:T(8,128)S(1)}, u32[]{:S(2)}) copy-start(f32[4,4,128,128]{3,2,1,0:T(8,128)S(1)} %pad_maximum_fusion.2.o0_ref) | copy-start | bytes 3145732
  48.8 31.9 %collective-permute-start.19 = (f32[4,4,128,128]{3,2,1,0:T(8,128)S(1)}, f32[4,4,128,128]{3,2,1,0:T(8,128)S(1)}, u32[]{:S(2)}, u32[]{:S(2)}) collective-permute-start(f32[4,4,128,128]{3,2,1,0:T(8,128)S(1)} %pad_maximum_fusion.2.o0_ref), channel_id=1, source_target_pairs={{0,1},{1,0},{2,3},{3,2},{4,5},{5,4},{6,7},{7,6},{8,9},{9,8},{10,11... | collective-permute-start | bytes 3145736 | tf_op jit(solution)/shard_map/ppermute | solution.py:22
  48.9 17.2 %slice-start = ((f32[8,72,128]{2,1,0:T(8,128)}), f32[8,64,128]{2,1,0:T(8,128)S(1)}, s32[]{:S(2)}) async-start(f32[8,72,128]{2,1,0:T(8,128)} %copy-done.4), calls=%async_computation.3 | async-start | bytes 524288 | tf_op jit(solution)/shard_map/slice | solution.py:142
  66.0 15.7 %copy-start.2 = (f32[4,4,128,128]{3,2,1,0:T(8,128)}, f32[4,4,128,128]{3,2,1,0:T(8,128)S(1)}, u32[]{:S(2)}) copy-start(f32[4,4,128,128]{3,2,1,0:T(8,128)S(1)} %pad_maximum_fusion.1.e0_ref) | copy-start | bytes 3145732
  66.0 15.7 %collective-permute-start.12 = (f32[4,4,128,128]{3,2,1,0:T(8,128)S(1)}, f32[4,4,128,128]{3,2,1,0:T(8,128)}, u32[]{:S(2)}, u32[]{:S(2)}) collective-permute-start(f32[4,4,128,128]{3,2,1,0:T(8,128)S(1)} %pad_maximum_fusion.1.e0_ref), channel_id=1, source_target_pairs={{0,1},{1,0},{2,3},{3,2},{4,5},{5,4},{6,7},{7,6},{8,9},{9,8},{10,11... | collective-permute-start | bytes 3145736 | tf_op jit(solution)/shard_map/ppermute | solution.py:22
  66.7 4.6 %collective-permute-start = (f32[8,16,128]{2,1,0:T(8,128)S(1)}, f32[8,16,128]{2,1,0:T(8,128)S(1)}, u32[]{:S(2)}, u32[]{:S(2)}) collective-permute-start(f32[8,16,128]{2,1,0:T(8,128)S(1)} %get-tuple-element.20), channel_id=1, source_target_pairs={{0,8},{8,0},{1,9},{9,1},{2,10},{10,2},{3,11},{11,3},{4,12},{12,4},... | collective-permute-start | bytes 196616 | tf_op jit(solution)/shard_map/ppermute | solution.py:22
  71.2 1.3 collective-permute-start.1
  72.6 6.9 %collective-permute-start.2 = (f32[8,16,128]{2,1,0:T(8,128)S(1)}, f32[8,16,128]{2,1,0:T(8,128)S(1)}, u32[]{:S(2)}, u32[]{:S(2)}) collective-permute-start(f32[8,16,128]{2,1,0:T(8,128)S(1)} %add.120), channel_id=1, source_target_pairs={{0,2},{2,4},{4,6},{6,0},{1,3},{3,5},{5,7},{7,1},{8,10},{10,12},{12... | collective-permute-start | bytes 196616 | tf_op jit(solution)/shard_map/ppermute | solution.py:22
  72.7 6.8 %collective-permute-start.3 = (f32[8,16,128]{2,1,0:T(8,128)S(1)}, f32[8,16,128]{2,1,0:T(8,128)S(1)}, u32[]{:S(2)}, u32[]{:S(2)}) collective-permute-start(f32[8,16,128]{2,1,0:T(8,128)S(1)} %add.120), channel_id=1, source_target_pairs={{0,4},{2,6},{4,0},{6,2},{1,5},{3,7},{5,1},{7,3},{8,12},{10,14},{12... | collective-permute-start | bytes 196616 | tf_op jit(solution)/shard_map/ppermute | solution.py:22
  74.7 5.3 %collective-permute-start.4 = (f32[8,16,128]{2,1,0:T(8,128)S(1)}, f32[8,16,128]{2,1,0:T(8,128)S(1)}, u32[]{:S(2)}, u32[]{:S(2)}) collective-permute-start(f32[8,16,128]{2,1,0:T(8,128)S(1)} %add.120), channel_id=1, source_target_pairs={{0,6},{2,0},{4,2},{6,4},{1,7},{3,1},{5,3},{7,5},{8,14},{10,8},{12,... | collective-permute-start | bytes 196616 | tf_op jit(solution)/shard_map/ppermute | solution.py:22
  80.7 1.0 copy-start.3
  85.7 5.6 %collective-permute-start.20 = (f32[8,16,128]{2,1,0:T(8,128)}, f32[8,16,128]{2,1,0:T(8,128)S(1)}, u32[]{:S(2)}, u32[]{:S(2)}) collective-permute-start(f32[8,16,128]{2,1,0:T(8,128)} %shard_map.59.first_ref), channel_id=1, source_target_pairs={{0,8},{1,9},{2,10},{3,11},{4,12},{5,13},{6,14},{7,15},{16,24},{17,... | collective-permute-start | bytes 196616 | tf_op jit(solution)/shard_map/ppermute | solution.py:169
  91.3 0.6 copy-start.8
  93.9 1.4 collective-permute-start.21
  95.9 4.9 %collective-permute-start.22 = (f32[2,16,128]{2,1,0:T(8,128)S(1)}, f32[2,16,128]{2,1,0:T(8,128)S(1)}, u32[]{:S(2)}, u32[]{:S(2)}) collective-permute-start(f32[2,16,128]{2,1,0:T(8,128)S(1)} %get-tuple-element.42), channel_id=1, source_target_pairs={{0,2},{2,4},{4,6},{6,0},{1,3},{3,5},{5,7},{7,1},{8,10},{10,12},{12... | collective-permute-start | bytes 49160 | tf_op jit(solution)/shard_map/ppermute | solution.py:22
  97.0 5.2 %collective-permute-start.23 = (f32[2,16,128]{2,1,0:T(8,128)S(1)}, f32[2,16,128]{2,1,0:T(8,128)S(1)}, u32[]{:S(2)}, u32[]{:S(2)}) collective-permute-start(f32[2,16,128]{2,1,0:T(8,128)S(1)} %get-tuple-element.42), channel_id=1, source_target_pairs={{0,4},{2,6},{4,0},{6,2},{1,5},{3,7},{5,1},{7,3},{8,12},{10,14},{12... | collective-permute-start | bytes 49160 | tf_op jit(solution)/shard_map/ppermute | solution.py:22
  100.1 3.7 %collective-permute-start.24 = (f32[2,16,128]{2,1,0:T(8,128)S(1)}, f32[2,16,128]{2,1,0:T(8,128)S(1)}, u32[]{:S(2)}, u32[]{:S(2)}) collective-permute-start(f32[2,16,128]{2,1,0:T(8,128)S(1)} %get-tuple-element.42), channel_id=1, source_target_pairs={{0,6},{2,0},{4,2},{6,4},{1,7},{3,1},{5,3},{7,5},{8,14},{10,8},{12,... | collective-permute-start | bytes 49160 | tf_op jit(solution)/shard_map/ppermute | solution.py:22
  108.5 14.3 %all-to-all-start.2 = ((f32[16,16,128]{2,1,0:T(8,128)}), f32[16,16,128]{2,1,0:T(8,128)S(1)}, u32[]{:S(2)}, u32[]{:S(2)}) async-start(f32[16,16,128]{2,1,0:T(8,128)} %bitcast.148), calls=%async_computation.2 | async-start | bytes 262144 | tf_op jit(solution)/shard_map/all_to_all | solution.py:181
  128.2 16.4 %copy-start.6 = (f32[8,2,16,128]{3,2,1,0:T(8,128)S(1)}, f32[8,2,16,128]{3,2,1,0:T(8,128)}, u32[]{:S(2)}) copy-start(f32[8,2,16,128]{3,2,1,0:T(8,128)} %shard_map.61) | copy-start | bytes 393220
  128.4 11.5 %collective-permute-start.25 = (f32[16,31,128]{2,0,1:T(8,128)S(1)}, f32[16,31,128]{2,0,1:T(8,128)S(1)}, u32[]{:S(2)}, u32[]{:S(2)}) collective-permute-start(f32[16,31,128]{2,0,1:T(8,128)S(1)} %bitcast.161), channel_id=1, source_target_pairs={{0,16},{16,0},{32,48},{48,32},{64,80},{80,64},{96,112},{112,96},{1... | collective-permute-start | bytes 761864 | tf_op jit(solution)/shard_map/ppermute | solution.py:194
  130.2 10.9 %collective-permute-start.26 = (f32[16,31,128]{2,0,1:T(8,128)S(1)}, f32[16,31,128]{2,0,1:T(8,128)S(1)}, u32[]{:S(2)}, u32[]{:S(2)}) collective-permute-start(f32[16,31,128]{2,0,1:T(8,128)S(1)} %bitcast.160), channel_id=1, source_target_pairs={{0,32},{16,48},{32,0},{48,16},{64,96},{80,112},{96,64},{112,80},{1... | collective-permute-start | bytes 761864 | tf_op jit(solution)/shard_map/ppermute | solution.py:194
  130.9 15.3 %collective-permute-start.27 = (f32[16,31,128]{2,0,1:T(8,128)S(1)}, f32[16,31,128]{2,0,1:T(8,128)S(1)}, u32[]{:S(2)}, u32[]{:S(2)}) collective-permute-start(f32[16,31,128]{2,0,1:T(8,128)S(1)} %bitcast.156), channel_id=1, source_target_pairs={{0,48},{16,32},{32,16},{48,0},{64,112},{80,96},{96,80},{112,64},{1... | collective-permute-start | bytes 761864 | tf_op jit(solution)/shard_map/ppermute | solution.py:194
  134.1 15.2 %collective-permute-start.28 = (f32[16,31,128]{2,0,1:T(8,128)S(1)}, f32[16,31,128]{2,0,1:T(8,128)S(1)}, u32[]{:S(2)}, u32[]{:S(2)}) collective-permute-start(f32[16,31,128]{2,0,1:T(8,128)S(1)} %bitcast.157), channel_id=1, source_target_pairs={{0,64},{16,80},{32,96},{48,112},{64,0},{80,16},{96,32},{112,48},{1... | collective-permute-start | bytes 761864 | tf_op jit(solution)/shard_map/ppermute | solution.py:194
  135.6 18.0 %collective-permute-start.29 = (f32[16,31,128]{2,0,1:T(8,128)S(1)}, f32[16,31,128]{2,0,1:T(8,128)S(1)}, u32[]{:S(2)}, u32[]{:S(2)}) collective-permute-start(f32[16,31,128]{2,0,1:T(8,128)S(1)} %bitcast.158), channel_id=1, source_target_pairs={{0,80},{16,64},{32,112},{48,96},{64,16},{80,0},{96,48},{112,32},{1... | collective-permute-start | bytes 761864 | tf_op jit(solution)/shard_map/ppermute | solution.py:194
  139.9 17.4 %collective-permute-start.30 = (f32[16,31,128]{2,0,1:T(8,128)}, f32[16,31,128]{2,0,1:T(8,128)S(1)}, u32[]{:S(2)}, u32[]{:S(2)}) collective-permute-start(f32[16,31,128]{2,0,1:T(8,128)} %bitcast.134), channel_id=1, source_target_pairs={{0,96},{16,112},{32,64},{48,80},{64,32},{80,48},{96,0},{112,16},{1... | collective-permute-start | bytes 761864 | tf_op jit(solution)/shard_map/ppermute | solution.py:194
  141.1 20.5 %collective-permute-start.31 = (f32[16,31,128]{2,0,1:T(8,128)S(1)}, f32[16,31,128]{2,0,1:T(8,128)S(1)}, u32[]{:S(2)}, u32[]{:S(2)}) collective-permute-start(f32[16,31,128]{2,0,1:T(8,128)S(1)} %bitcast.159), channel_id=1, source_target_pairs={{0,112},{16,96},{32,80},{48,64},{64,48},{80,32},{96,16},{112,0},{1... | collective-permute-start | bytes 761864 | tf_op jit(solution)/shard_map/ppermute | solution.py:194

commit v3 on v2

--- a/solution.py
+++ b/solution.py
@@ -92,6 +92,71 @@
         out_ref[i, 1] = block
 
 
+def weights_kernel(after_ref, upper_ref, high_ref, low_ref):
+    for s in range(upper_ref.shape[2]):
+        high, low = split_bf16(upper_ref[:, :, s, :].reshape(2 * BLOCK, BLOCK))
+        high_ref[s] = high
+        low_ref[s] = low
+
+
+def update_kernel(
+    place_ref, slot_ref, rows_ref, held_ref, high_ref, low_ref,
+    a_keep, a_send, b_keep, b_one, b_two, b_three, left_high, left_low,
+):
+    step = pl.program_id(0)
+    count = high_ref.shape[0]
+    last = pl.num_programs(0) - 1
+    groups = [(yh, dx) for yh in range(2) for dx in range(4)]
+    share = BLOCK // len(groups)
+
+    def group_row(yh, dx):
+        return lax.rem(place_ref[0] + dx, 4) * 2 + lax.rem(place_ref[4] + yh, 2)
+
+    @pl.when(step == 0)
+    def _():
+        for g, (yh, dx) in enumerate(groups):
+            for t in range(2):
+                high, low = split_bf16(-rows_ref[group_row(yh, dx), t])
+                at = (pl.ds(g * share, share), pl.ds(t * BLOCK, BLOCK))
+                left_high[at] = high
+                left_low[at] = low
+
+    def put(slot, values, add):
+        @pl.when(slot < 16)
+        def _():
+            for g, (yh, dx) in enumerate(groups):
+                ref = (a_keep, a_send)[yh].at[dx, jnp.maximum(slot - 1, 0)]
+                ref[...] = values(g) + ref[...] if add else values(g)
+
+        @pl.when(slot >= 16)
+        def _():
+            for g, (yh, dx) in enumerate(groups):
+                ref = (b_keep, b_one, b_two, b_three)[dx].at[yh, jnp.maximum(slot - 16, 0)]
+                ref[...] = values(g) + ref[...] if add else values(g)
+
+    for i in range(count):
+        both = jnp.concatenate([left_high[...], left_low[...]], axis=0)
+        first = jnp.dot(both, high_ref[i], preferred_element_type=jnp.float32)
+        second = jnp.dot(left_high[...], low_ref[i], preferred_element_type=jnp.float32)
+        total = first[:BLOCK] + first[BLOCK:] + second
+        put(step * count + i, lambda g: total[g * share : (g + 1) * share], False)
+
+    @pl.when(step == last)
+    def _():
+        def join(q, carry):
+            def values(g):
+                row = group_row(*groups[g]) * share
+                return held_ref[q, pl.ds(pl.multiple_of(row, share), share), :]
+
+            @pl.when(slot_ref[q] >= 1)
+            def _():
+                put(slot_ref[q], values, True)
+
+            return carry
+
+        lax.fori_loop(0, held_ref.shape[0], join, 0)
+
+
 def local_kernel(kernel, shape, *args):
     return pl.pallas_call(
         kernel,
@@ -102,6 +167,39 @@
     )(*args)
 
 
+def split_weights(after, upper):
+    slots, step = upper.shape[2], 8
+    shape = jax.ShapeDtypeStruct((slots, 2 * BLOCK, BLOCK), jnp.bfloat16)
+    spec = pl.BlockSpec((step, 2 * BLOCK, BLOCK), lambda i: (i, 0, 0))
+    return pl.pallas_call(
+        weights_kernel,
+        out_shape=(shape, shape),
+        grid=(slots // step,),
+        in_specs=[
+            pl.BlockSpec((8, BLOCK), lambda i: (0, 0)),
+            pl.BlockSpec((2, BLOCK, step, BLOCK), lambda i: (0, 0, i, 0)),
+        ],
+        out_specs=(spec, spec),
+        cost_estimate=pl.CostEstimate(flops=600_000_000, bytes_accessed=8_000_000, transcendentals=0),
+    )(after, upper)
+
+
+def update(place, slot_of, own_rows, arrived, high, low):
+    slots, step = high.shape[0], 8
+    share = own_rows.shape[2]
+    spec = pl.BlockSpec((step, 2 * BLOCK, BLOCK), lambda i: (i, 0, 0))
+    shapes = [(4, 15, share, BLOCK)] * 2 + [(2, 16, share, BLOCK)] * 4
+    return pl.pallas_call(
+        update_kernel,
+        out_shape=tuple(jax.ShapeDtypeStruct(shape, jnp.float32) for shape in shapes),
+        grid=(slots // step,),
+        in_specs=[SMEM, SMEM, VMEM, VMEM, spec, spec],
+        out_specs=(VMEM,) * 6,
+        scratch_shapes=[pltpu.VMEM((BLOCK, 2 * BLOCK), jnp.bfloat16)] * 2,
+        cost_estimate=pl.CostEstimate(flops=900_000_000, bytes_accessed=8_000_000, transcendentals=0),
+    )(place, slot_of, own_rows, arrived, high, low)
+
+
 def per_device(incoming, block_map, panel_row, diag_inverse):
     my_x, my_yh, my_yl, my_z, my_core = (lax.axis_index(a) for a in ("x", "yh", "yl", "z", "core"))
     my_row = lax.axis_index(ROW)
@@ -110,7 +208,7 @@
     sources = incoming.shape[2]
     share = BLOCK // rows
     slots = panel_row.shape[3]
-    place = jnp.stack([my_x, my_z, my_core, my_yl]).astype(jnp.int32)
+    place = jnp.stack([my_x, my_z, my_core, my_yl, my_yh]).astype(jnp.int32)
 
     targets = block_map.reshape(sources)
     blocks = incoming.reshape(sources, BLOCK, BLOCK)
@@ -135,7 +233,7 @@
     by_z = around(odd[0], "z")
     coupling = jnp.stack([p[1:] for p in by_x])
     even = jnp.stack([p[0] for p in by_x])
-    upper, even = lax.optimization_barrier((upper, even))
+    weights = split_weights(by_x[1][0, :8], upper)
     even = jnp.stack(around(even, "z"))
     odd = jnp.stack(around(jnp.stack(by_z), "x"))
 
@@ -151,10 +249,6 @@
     start = belonging(my_yl) + rotated(belonging(1 - my_yl), "yl", 1)
     start = start + rotated(start, "core", 1)
     start = sum(around(start, "z"))
-
-    even_other = rotated(even, "core", 1)
-    odd_other = rotated(odd, "core", 1)
-    factors = (even, even_other, odd, odd_other)
 
     chosen = (targets[None, :] % cols) == jnp.arange(cols, dtype=jnp.int32)[:, None]
     outgoing = jnp.zeros((cols, BLOCK, BLOCK), jnp.float32)
@@ -164,6 +258,11 @@
     slot_label = jnp.broadcast_to(slot_label.astype(jnp.float32)[:, None, None], (cols, 8, BLOCK))
     outgoing = jnp.concatenate([outgoing, slot_label], axis=1)
 
+    even, odd, start, coupling, outgoing = lax.optimization_barrier(
+        (even, odd, start, coupling, outgoing)
+    )
+    factors = (even, rotated(even, "core", 1), odd, rotated(odd, "core", 1))
+
     shape = (HALF, share, BLOCK)
     first = local_kernel(first_kernel, shape, place, start, *factors)
     passed = lax.ppermute(first, "yl", [(0, 1)])
@@ -172,9 +271,7 @@
         coupling_kernel, (share, BLOCK), place, start, passed, coupling
     )
     residual = jnp.stack(around(jnp.stack(around(residual, "core")), "z"))
-    copies = local_kernel(
-        second_kernel, (HALF, 2, share, BLOCK), place, residual, first, *factors
-    )
+    copies = local_kernel(second_kernel, (HALF, 2, share, BLOCK), place, residual, first, *factors)
     copies, arrived = lax.optimization_barrier((copies, arrived))
     panel_solution = lax.dynamic_index_in_dim(copies[:, 0], my_plane, 0, keepdims=False)
 
@@ -182,16 +279,14 @@
         copies.reshape(rows * 2, share, BLOCK), ROW + ("yl",), 0, 0, tiled=True
     ).reshape(rows, 2, share, BLOCK)
     slot_of = arrived[:, BLOCK, 0].astype(jnp.int32)
-    matches = (slot_of[None, :] == jnp.arange(1, slots, dtype=jnp.int32)[:, None]).astype(jnp.float32)
-    held = arrived[:, :BLOCK].reshape(cols, rows, share, BLOCK)
-    held = jnp.einsum("sq,qrke->rkse", matches, held, precision=HIGHEST)
-    partial = held - jnp.einsum(
-        "rtkp,tpse->rkse", own_rows, upper[:, :, 1:, :], precision=lax.Precision.HIGH
-    )
-    trailing = lax.dynamic_index_in_dim(partial, my_row, 0, keepdims=False)
-    for step in range(1, rows):
-        part = lax.dynamic_index_in_dim(partial, my_row ^ step, 0, keepdims=False)
-        trailing = trailing + lax.ppermute(part, ROW, [(i, i ^ step) for i in range(rows)])
+    a_keep, a_send, b_keep, *b_sends = update(place, slot_of, own_rows, arrived, *weights)
+    a_part = a_keep + rotated(a_send, "yh", 1)
+    b_part = b_keep
+    for step, b_send in zip((1, 2, 3), b_sends):
+        b_part = b_part + rotated(b_send, "x", step)
+    b_part = b_part[0] + rotated(b_part[1], "yh", 1)
+    a_part = a_part[0] + sum(rotated(a_part[step], "x", step) for step in (1, 2, 3))
+    trailing = jnp.concatenate([a_part, b_part], axis=0).transpose(1, 0, 2)
     return panel_solution[:, None, None, :], trailing[:, :, None, :]
 
 
@@ -204,4 +299,6 @@
         P(None, COL, None, None),
     )
     out_specs = (P(ROW, None, COL, None), P(ROW, None, COL, None))
-    return jax.shard_map(per_device, mesh=fine, in_specs=in_specs, out_specs=out_specs, check_vma=False)
+    return jax.shard_map(
+        per_device, mesh=fine, in_specs=in_specs, out_specs=out_specs, check_vma=False
+    )

time: 163 us -> 167 us (1.025)
  Pallas kernels: 10 us -> 33.1 us
  waiting for transfers between devices: 56.6 us -> 35.8 us
  starting transfers between devices: 67.4 us -> 76 us
  local copies, waits for them, and re-layouts: 14.5 us -> 7.83 us
  matrix products: 5.44 us -> 1.12 us
  other arithmetic: 7.74 us -> 11.2 us
    ppermute x23 -> x31, starting transfers between devices: 31.5 us -> 54.8 us  [rotated(): lax.ppermute(array, axis, [(i, (i + step) % size) for i in range(size)])]
    pallas_call x0 -> x2, Pallas kernels: none -> 23.1 us  [the longest x1 12.6 us: split_weights(): pl.pallas_call(weights_kernel, out_shape=(shape, shape), grid=(slots // s...]
    ppermute x7 -> x0, waiting for transfers between devices: 16.3 us -> none  [per_device(): lax.ppermute(part, ROW, [(i, i ^ step) for i in range(rows)])]
    ppermute x7 -> x0, starting transfers between devices: 14.6 us -> none  [per_device(): lax.ppermute(part, ROW, [(i, i ^ step) for i in range(rows)])]
    unnamed x22 -> x17, local copies, waits for them, and re-layouts: 9.17 us -> 2.26 us
    all_to_all x1, waiting for transfers between devices: 6.69 us -> 0.01 us  [per_device(): lax.all_to_all(copies.reshape(rows * 2, share, BLOCK), ROW + ('yl',), 0,...]
    dot_general x2 -> x0, matrix products: 5.17 us -> none  [the longest x1 3.4 us: per_device(): jnp.einsum('rtkp,tpse->rkse', own_rows, upper[:, :, 1:, :], precision=lax...]
    ppermute x1, waiting for transfers between devices: 1.34 us -> 6.03 us  [per_device(): passed = lax.ppermute(first, 'yl', [(0, 1)])]
  transfers between devices with their start and end apart: 35 -> 36, of which waited for: 20 -> 14; matrix products, arithmetic and copies ran while one was open for 8% -> 8% of each run, Pallas kernels for 6% -> 14%
where the time goes in v3:
time: 167 us; the launch traced here: 166 us
  starting transfers between devices  76 us (46%)
  waiting for transfers between devices  35.8 us (21%)
  Pallas kernels  33.1 us (20%)
  other arithmetic  11.2 us (7%)
  local copies, waits for them, and re-layouts  7.83 us (5%)
    ppermute x31, starting transfers between devices, rotated(): lax.ppermute(array, axis, [(i, (i + step) % size) for i in range(size)])  54.8 us
    ppermute x31, waiting for transfers between devices, rotated(): lax.ppermute(array, axis, [(i, (i + step) % size) for i in range(size)])  29.7 us
    pallas_call x1, Pallas kernels, split_weights(): pl.pallas_call(weights_kernel, out_shape=(shape, shape), grid=(slots // s...  12.6 us
    pallas_call x1, Pallas kernels, update(): pl.pallas_call(update_kernel, out_shape=tuple((jax.ShapeDtypeStruct(shape...  10.4 us
    pallas_call x3, Pallas kernels, local_kernel(): pl.pallas_call(kernel, out_shape=jax.ShapeDtypeStruct(shape, jnp.float32)...  10 us
    ppermute x1, waiting for transfers between devices, per_device(): passed = lax.ppermute(first, 'yl', [(0, 1)])  6.03 us
    all_to_all x1, starting transfers between devices, per_device(): lax.all_to_all(copies.reshape(rows * 2, share, BLOCK), ROW + ('yl',), 0,...  5.74 us
    all_to_all x1, starting transfers between devices, per_device(): received = lax.all_to_all(packed, ROW, 0, 0, tiled=True)  4.3 us
  transfers between devices with their start and end apart: 36, of which 14 were waited for; matrix products, arithmetic and copies ran while one was open for 8% of the time, Pallas kernels for 14%

profile of v3, /device:TPU:0, one launch (start us, length us, event | category | flops | bytes accessed | tf_op | source)
XLA Modules:
  0.0 166.0 jit_solution(16174928007989611974)
XLA Ops:
  0.7 1.1 slice.146
  1.8 1.3 slice.143
  3.1 1.1 fusion.5
  4.2 0.9 fusion.4
  5.1 3.4 %collective-permute-start = (f32[2,128,128]{2,1,0:T(8,128)S(1)}, f32[2,128,128]{2,1,0:T(8,128)S(1)}, u32[]{:S(2)}, u32[]{:S(2)}) collective-permute-start(f32[2,128,128]{2,1,0:T(8,128)S(1)} %pad_maximum_fusion.8), channel_id=1, source_target_pairs={{0,16},{16,0},{1,17},{17,1},{2,18},{18,2},{3,19},{19,3},{4,20},{20... | collective-permute-start | bytes 393224 | tf_op jit(solution)/shard_map/ppermute | solution.py:228
  8.5 0.8 add_convert_fusion
  9.3 1.0 copy.10
  10.3 0.8 pad_maximum_fusion.4
  11.2 4.3 %all-to-all-start = ((f32[8,72,128]{2,1,0:T(8,128)}), f32[8,72,128]{2,1,0:T(8,128)S(1)}, u32[]{:S(2)}, u32[]{:S(2)}) async-start(f32[8,72,128]{2,1,0:T(8,128)} %pad_maximum_fusion.4), calls=%async_computation | async-start | bytes 589824 | tf_op jit(solution)/shard_map/all_to_all | solution.py:231
  16.3 1.1 pad_maximum_fusion
  17.5 4.1 %collective-permute-start.9 = (f32[128,128]{1,0:T(8,128)S(1)}, f32[128,128]{1,0:T(8,128)S(1)}, u32[]{:S(2)}, u32[]{:S(2)}) collective-permute-start(f32[128,128]{1,0:T(8,128)S(1)} %get-tuple-element.56), channel_id=1, source_target_pairs={{0,6},{2,0},{4,2},{6,4},{1,7},{3,1},{5,3},{7,5},{8,14},{10,8},{12,... | collective-permute-start | bytes 196616 | tf_op jit(solution)/shard_map/ppermute | solution.py:22
  21.6 1.3 collective-permute-start.7
  22.9 3.3 %collective-permute-start.3 = (f32[3,128,128]{2,1,0:T(8,128)S(1)}, f32[3,128,128]{2,1,0:T(8,128)S(1)}, u32[]{:S(2)}, u32[]{:S(2)}) collective-permute-start(f32[3,128,128]{2,1,0:T(8,128)S(1)} %pad_maximum_fusion.7), channel_id=1, source_target_pairs={{0,96},{32,0},{64,32},{96,64},{1,97},{33,1},{65,33},{97,65},{2,98}... | collective-permute-start | bytes 589832 | tf_op jit(solution)/shard_map/ppermute | solution.py:22
  26.1 0.9 collective-permute-start.2
  27.8 0.9 collective-permute-start.1
  28.7 1.3 collective-permute-start.13
  30.1 2.3 %collective-permute-start.11 = (f32[4,128,128]{2,1,0:T(8,128)S(1)}, f32[4,128,128]{2,1,0:T(8,128)S(1)}, u32[]{:S(2)}, u32[]{:S(2)}) collective-permute-start(f32[4,128,128]{2,1,0:T(8,128)S(1)} %get-tuple-element.50), channel_id=1, source_target_pairs={{0,64},{32,96},{64,0},{96,32},{1,65},{33,97},{65,1},{97,33},{2,66}... | collective-permute-start | bytes 786440 | tf_op jit(solution)/shard_map/ppermute | solution.py:22
  33.0 1.8 %collective-permute-start.10 = (f32[4,128,128]{2,1,0:T(8,128)S(1)}, f32[4,128,128]{2,1,0:T(8,128)S(1)}, u32[]{:S(2)}, u32[]{:S(2)}) collective-permute-start(f32[4,128,128]{2,1,0:T(8,128)S(1)} %get-tuple-element.50), channel_id=1, source_target_pairs={{0,32},{32,64},{64,96},{96,0},{1,33},{33,65},{65,97},{97,1},{2,34}... | collective-permute-start | bytes 786440 | tf_op jit(solution)/shard_map/ppermute | solution.py:22
  34.8 4.5 %collective-permute-done.3 = f32[3,128,128]{2,1,0:T(8,128)S(1)} collective-permute-done((f32[3,128,128]{2,1,0:T(8,128)S(1)}, f32[3,128,128]{2,1,0:T(8,128)S(1)}, u32[]{:S(2)}, u32[]{:S(2)}) %collective-permute-start.3) | collective-permute-done | bytes 196640 | tf_op jit(solution)/shard_map/ppermute | solution.py:22
  39.3 4.1 %collective-permute-start.12 = (f32[4,128,128]{2,1,0:T(8,128)S(1)}, f32[4,128,128]{2,1,0:T(8,128)S(1)}, u32[]{:S(2)}, u32[]{:S(2)}) collective-permute-start(f32[4,128,128]{2,1,0:T(8,128)S(1)} %get-tuple-element.50), channel_id=1, source_target_pairs={{0,96},{32,0},{64,32},{96,64},{1,97},{33,1},{65,33},{97,65},{2,98}... | collective-permute-start | bytes 786440 | tf_op jit(solution)/shard_map/ppermute | solution.py:22
  43.6 1.2 collective-permute-done.14
  44.8 2.3 %collective-permute-start.17 = (f32[8,16,128]{2,1,0:T(8,128)S(1)}, f32[8,16,128]{2,1,0:T(8,128)S(1)}, u32[]{:S(2)}, u32[]{:S(2)}) collective-permute-start(f32[8,16,128]{2,1,0:T(8,128)S(1)} %add.93), channel_id=1, source_target_pairs={{0,6},{2,0},{4,2},{6,4},{1,7},{3,1},{5,3},{7,5},{8,14},{10,8},{12,... | collective-permute-start | bytes 196616 | tf_op jit(solution)/shard_map/ppermute | solution.py:22
  47.1 0.8 pad_maximum_fusion.3.x_ref
  47.9 2.0 %collective-permute-start.16 = (f32[8,16,128]{2,1,0:T(8,128)S(1)}, f32[8,16,128]{2,1,0:T(8,128)S(1)}, u32[]{:S(2)}, u32[]{:S(2)}) collective-permute-start(f32[8,16,128]{2,1,0:T(8,128)S(1)} %add.93), channel_id=1, source_target_pairs={{0,4},{2,6},{4,0},{6,2},{1,5},{3,7},{5,1},{7,3},{8,12},{10,14},{12... | collective-permute-start | bytes 196616 | tf_op jit(solution)/shard_map/ppermute | solution.py:22
  50.0 1.3 collective-permute-start.15
  51.4 2.4 %collective-permute-done.16 = f32[8,16,128]{2,1,0:T(8,128)S(1)} collective-permute-done((f32[8,16,128]{2,1,0:T(8,128)S(1)}, f32[8,16,128]{2,1,0:T(8,128)S(1)}, u32[]{:S(2)}, u32[]{:S(2)}) %collective-permute-start.16) | collective-permute-done | bytes 65568 | tf_op jit(solution)/shard_map/ppermute | solution.py:22
  53.8 2.3 %collective-permute-start.5 = (f32[4,128,128]{2,1,0:T(8,128)S(1)}, f32[4,128,128]{2,1,0:T(8,128)S(1)}, u32[]{:S(2)}, u32[]{:S(2)}) collective-permute-start(f32[4,128,128]{2,1,0:T(8,128)S(1)} %get-tuple-element.52), channel_id=1, source_target_pairs={{0,4},{2,6},{4,0},{6,2},{1,5},{3,7},{5,1},{7,3},{8,12},{10,14},{12... | collective-permute-start | bytes 786440 | tf_op jit(solution)/shard_map/ppermute | solution.py:22
  56.1 3.2 %collective-permute-start.6 = (f32[4,128,128]{2,1,0:T(8,128)S(1)}, f32[4,128,128]{2,1,0:T(8,128)S(1)}, u32[]{:S(2)}, u32[]{:S(2)}) collective-permute-start(f32[4,128,128]{2,1,0:T(8,128)S(1)} %get-tuple-element.52), channel_id=1, source_target_pairs={{0,6},{2,0},{4,2},{6,4},{1,7},{3,1},{5,3},{7,5},{8,14},{10,8},{12,... | collective-permute-start | bytes 786440 | tf_op jit(solution)/shard_map/ppermute | solution.py:22
  59.3 0.6 add_add_fusion.1.start_ref
  60.0 4.5 %collective-permute-done.5 = f32[4,128,128]{2,1,0:T(8,128)S(1)} collective-permute-done((f32[4,128,128]{2,1,0:T(8,128)S(1)}, f32[4,128,128]{2,1,0:T(8,128)S(1)}, u32[]{:S(2)}, u32[]{:S(2)}) %collective-permute-start.5) | collective-permute-done | bytes 262176 | tf_op jit(solution)/shard_map/ppermute | solution.py:22
  64.5 3.3 %collective-permute-done.4 = f32[4,128,128]{2,1,0:T(8,128)S(1)} collective-permute-done((f32[4,128,128]{2,1,0:T(8,128)S(1)}, f32[4,128,128]{2,1,0:T(8,128)S(1)}, u32[]{:S(2)}, u32[]{:S(2)}) %collective-permute-start.4) | collective-permute-done | bytes 262176 | tf_op jit(solution)/shard_map/ppermute | solution.py:22
  68.4 3.9 %all-to-all-start.1 = ((f32[16,136,128]{2,1,0:T(8,128)}), f32[16,136,128]{2,1,0:T(8,128)S(1)}, u32[]{:S(2)}, u32[]{:S(2)}) async-start(f32[16,136,128]{2,1,0:T(8,128)} %pad_maximum_fusion), calls=%async_computation.1 | async-start | bytes 2228224 | tf_op jit(solution)/shard_map/all_to_all | solution.py:269
  72.4 0.7 stack.115.place_ref
  73.1 4.0 %shard_map.59.first_ref = f32[8,16,128]{2,1,0:T(8,128)} custom-call(s32[5]{0:T(128)} %stack.115.place_ref, f32[8,16,128]{2,1,0:T(8,128)} %add_add_fusion.1.start_ref, f32[4,4,128,128]{3,2,1,0:T(8,128)} %copy-done.1, f32[4,4,128,128]{3,2,1,0:T(8,128)} %collective-permute-done.18.e1_ref, f32[4,4,128,128]{3,2,1,0:T(8,128)} %copy-done, ...), custom_call_target="tpu_custom_call" | custom-call | flops 600000000 | bytes 5000000 | tf_op jit(solution)/shard_map/pallas_call | solution.py:161
  77.0 3.8 %collective-permute-start.20 = (f32[8,16,128]{2,1,0:T(8,128)}, f32[8,16,128]{2,1,0:T(8,128)S(1)}, u32[]{:S(2)}, u32[]{:S(2)}) collective-permute-start(f32[8,16,128]{2,1,0:T(8,128)} %shard_map.59.first_ref), channel_id=1, source_target_pairs={{0,8},{1,9},{2,10},{3,11},{4,12},{5,13},{6,14},{7,15},{16,24},{17,... | collective-permute-start | bytes 196616 | tf_op jit(solution)/shard_map/ppermute | solution.py:268
  80.9 6.0 %collective-permute-done.20.passed_ref = f32[8,16,128]{2,1,0:T(8,128)S(1)} collective-permute-done((f32[8,16,128]{2,1,0:T(8,128)}, f32[8,16,128]{2,1,0:T(8,128)S(1)}, u32[]{:S(2)}, u32[]{:S(2)}) %collective-permute-start.20) | collective-permute-done | bytes 65568 | tf_op jit(solution)/shard_map/ppermute | solution.py:268
  87.5 2.0 %shard_map.60 = f32[16,128]{1,0:T(8,128)} custom-call(s32[5]{0:T(128)} %stack.115.place_ref, f32[8,16,128]{2,1,0:T(8,128)} %add_add_fusion.1.start_ref, f32[8,16,128]{2,1,0:T(8,128)} %copy-done.6, f32[4,2,128,128]{3,2,1,0:T(8,128)} %pad_maximum_fusion.3.x_ref), custom_call_target="tpu_custom_call" | custom-call | flops 600000000 | bytes 5000000 | tf_op jit(solution)/shard_map/pallas_call | solution.py:161
  89.5 1.4 collective-permute-done.21
  90.9 0.7 fusion.7
  91.6 3.1 %collective-permute-start.23 = (f32[2,16,128]{2,1,0:T(8,128)S(1)}, f32[2,16,128]{2,1,0:T(8,128)S(1)}, u32[]{:S(2)}, u32[]{:S(2)}) collective-permute-start(f32[2,16,128]{2,1,0:T(8,128)S(1)} %get-tuple-element.59), channel_id=1, source_target_pairs={{0,4},{2,6},{4,0},{6,2},{1,5},{3,7},{5,1},{7,3},{8,12},{10,14},{12... | collective-permute-start | bytes 49160 | tf_op jit(solution)/shard_map/ppermute | solution.py:22
  94.7 0.7 collective-permute-start.22
  95.4 2.6 %collective-permute-start.24 = (f32[2,16,128]{2,1,0:T(8,128)S(1)}, f32[2,16,128]{2,1,0:T(8,128)S(1)}, u32[]{:S(2)}, u32[]{:S(2)}) collective-permute-start(f32[2,16,128]{2,1,0:T(8,128)S(1)} %get-tuple-element.59), channel_id=1, source_target_pairs={{0,6},{2,0},{4,2},{6,4},{1,7},{3,1},{5,3},{7,5},{8,14},{10,8},{12,... | collective-permute-start | bytes 49160 | tf_op jit(solution)/shard_map/ppermute | solution.py:22
  98.5 1.1 collective-permute-done.22
  99.7 0.6 pad_maximum_fusion.9.start_ref
  100.3 4.0 %shard_map.61 = f32[8,2,16,128]{3,2,1,0:T(8,128)} custom-call(s32[5]{0:T(128)} %stack.115.place_ref, f32[4,2,16,128]{3,2,1,0:T(8,128)} %pad_maximum_fusion.9.start_ref, f32[8,16,128]{2,1,0:T(8,128)} %shard_map.59.first_ref, f32[4,4,128,128]{3,2,1,0:T(8,128)} %copy-done.1, f32[4,4,128,128]{3,2,1,0:T(8,128)} %collective-permute-done.18.e1_ref, ...), custom_call_target="tpu_custom_call" | custom-call | flops 600000000 | bytes 5000000 | tf_op jit(solution)/shard_map/pallas_call | solution.py:161
  104.4 5.7 %all-to-all-start.2 = ((f32[16,16,128]{2,1,0:T(8,128)}), f32[16,16,128]{2,1,0:T(8,128)S(1)}, u32[]{:S(2)}, u32[]{:S(2)}) async-start(f32[16,16,128]{2,1,0:T(8,128)} %bitcast.105), calls=%async_computation.2 | async-start | bytes 262144 | tf_op jit(solution)/shard_map/all_to_all | solution.py:278
  110.1 12.6 %shard_map.62 = (bf16[32,256,128]{2,1,0:T(8,128)(2,1)}, bf16[32,256,128]{2,1,0:T(8,128)(2,1)}) custom-call(f32[8,128]{1,0:T(8,128)} %slice_bitcast_fusion.13.after_ref, f32[2,128,32,128]{3,2,1,0:T(8,128)} %bitcast.101), custom_call_target="tpu_custom_call" | custom-call | flops 600000000 | bytes 8000000 | tf_op jit(solution)/shard_map/pallas_call | solution.py:174
  122.7 0.9 convert_reduce_fusion.slot_ref
  123.6 0.6 copy-done.5
  124.3 10.4 %shard_map.63 = (f32[4,15,16,128]{3,2,1,0:T(8,128)}, f32[4,15,16,128]{3,2,1,0:T(8,128)}, f32[2,16,16,128]{3,2,1,0:T(8,128)}, f32[2,16,16,128]{3,2,1,0:T(8,128)},...) custom-call(s32[5]{0:T(128)} %stack.115.place_ref, s32[16]{0:T(128)} %convert_reduce_fusion.slot_ref, ...), custom_call_target="tpu_custom_call" | custom-call | flops 900000000 | bytes 8000000 | tf_op jit(solution)/shard_map/pallas_call | solution.py:192
  134.7 1.9 %collective-permute-start.29 = (f32[2,16,16,128]{3,2,1,0:T(8,128)}, f32[2,16,16,128]{3,2,1,0:T(8,128)S(1)}, u32[]{:S(2)}, u32[]{:S(2)}) collective-permute-start(f32[2,16,16,128]{3,2,1,0:T(8,128)} %get-tuple-element.29), channel_id=1, source_target_pairs={{0,32},{32,64},{64,96},{96,0},{1,33},{33,65},{65,97},{97,1},{2,34}... | collective-permute-start | bytes 786440 | tf_op jit(solution)/shard_map/ppermute | solution.py:22
  136.7 2.7 %collective-permute-start.30 = (f32[2,16,16,128]{3,2,1,0:T(8,128)}, f32[2,16,16,128]{3,2,1,0:T(8,128)S(1)}, u32[]{:S(2)}, u32[]{:S(2)}) collective-permute-start(f32[2,16,16,128]{3,2,1,0:T(8,128)} %get-tuple-element.30), channel_id=1, source_target_pairs={{0,64},{32,96},{64,0},{96,32},{1,65},{33,97},{65,1},{97,33},{2,66}... | collective-permute-start | bytes 786440 | tf_op jit(solution)/shard_map/ppermute | solution.py:22
  139.3 1.5 collective-permute-start.31
  140.8 3.0 %collective-permute-start.25 = (f32[4,15,16,128]{3,2,1,0:T(8,128)}, f32[4,15,16,128]{3,2,1,0:T(8,128)S(1)}, u32[]{:S(2)}, u32[]{:S(2)}) collective-permute-start(f32[4,15,16,128]{3,2,1,0:T(8,128)} %get-tuple-element.27), channel_id=1, source_target_pairs={{0,16},{16,0},{1,17},{17,1},{2,18},{18,2},{3,19},{19,3},{4,20},{20... | collective-permute-start | bytes 1474568 | tf_op jit(solution)/shard_map/ppermute | solution.py:22
  144.5 5.0 %collective-permute-done.30 = f32[2,16,16,128]{3,2,1,0:T(8,128)S(1)} collective-permute-done((f32[2,16,16,128]{3,2,1,0:T(8,128)}, f32[2,16,16,128]{3,2,1,0:T(8,128)S(1)}, u32[]{:S(2)}, u32[]{:S(2)}) %collective-permute-start.30) | collective-permute-done | bytes 262176 | tf_op jit(solution)/shard_map/ppermute | solution.py:22
  149.5 1.0 add_add_fusion
  150.6 3.1 %collective-permute-start.32 = (f32[16,16,128]{2,1,0:T(8,128)S(1)}, f32[16,16,128]{2,1,0:T(8,128)S(1)}, u32[]{:S(2)}, u32[]{:S(2)}) collective-permute-start(f32[16,16,128]{2,1,0:T(8,128)S(1)} %slice_bitcast_fusion), channel_id=1, source_target_pairs={{0,16},{16,0},{1,17},{17,1},{2,18},{18,2},{3,19},{19,3},{4,20},{20... | collective-permute-start | bytes 393224 | tf_op jit(solution)/shard_map/ppermute | solution.py:22
  153.9 1.1 add.99
  155.0 2.5 %collective-permute-start.27 = (f32[15,16,128]{2,1,0:T(8,128)S(1)}, f32[15,16,128]{2,1,0:T(8,128)S(1)}, u32[]{:S(2)}, u32[]{:S(2)}) collective-permute-start(f32[15,16,128]{2,1,0:T(8,128)S(1)} %get-tuple-element.42), channel_id=1, source_target_pairs={{0,64},{32,96},{64,0},{96,32},{1,65},{33,97},{65,1},{97,33},{2,66}... | collective-permute-start | bytes 368648 | tf_op jit(solution)/shard_map/ppermute | solution.py:22
  157.5 1.4 collective-permute-start.28
  158.9 0.6 collective-permute-start.26
  159.6 2.9 %collective-permute-done.27 = f32[15,16,128]{2,1,0:T(8,128)S(1)} collective-permute-done((f32[15,16,128]{2,1,0:T(8,128)S(1)}, f32[15,16,128]{2,1,0:T(8,128)S(1)}, u32[]{:S(2)}, u32[]{:S(2)}) %collective-permute-start.27) | collective-permute-done | bytes 122912 | tf_op jit(solution)/shard_map/ppermute | solution.py:22
  162.5 2.5 %collective-permute-done.26 = f32[15,16,128]{2,1,0:T(8,128)S(1)} collective-permute-done((f32[15,16,128]{2,1,0:T(8,128)S(1)}, f32[15,16,128]{2,1,0:T(8,128)S(1)}, u32[]{:S(2)}, u32[]{:S(2)}) %collective-permute-start.26) | collective-permute-done | bytes 122912 | tf_op jit(solution)/shard_map/ppermute | solution.py:22
  165.1 1.0 copy.11
  (87 shorter events, 5.6 us)
Async XLA Ops:
  0.6 14.8 %copy-start.7 = (s32[1,1,4]{2,1,0:T(1,128)S(1)}, s32[1,1,4]{2,1,0:T(1,128)}, u32[]{:S(2)}) copy-start(s32[1,1,4]{2,1,0:T(1,128)} %param.5) | copy-start | bytes 52
  0.6 14.8 %copy-start.3 = (f32[1,1,4,128,128]{4,3,2,1,0:T(8,128)S(1)}, f32[1,1,4,128,128]{4,3,2,1,0:T(8,128)}, u32[]{:S(2)}) copy-start(f32[1,1,4,128,128]{4,3,2,1,0:T(8,128)} %param.4) | copy-start | bytes 786436
  5.1 12.3 %collective-permute-start = (f32[2,128,128]{2,1,0:T(8,128)S(1)}, f32[2,128,128]{2,1,0:T(8,128)S(1)}, u32[]{:S(2)}, u32[]{:S(2)}) collective-permute-start(f32[2,128,128]{2,1,0:T(8,128)S(1)} %pad_maximum_fusion.8), channel_id=1, source_target_pairs={{0,16},{16,0},{1,17},{17,1},{2,18},{18,2},{3,19},{19,3},{4,20},{20... | collective-permute-start | bytes 393224 | tf_op jit(solution)/shard_map/ppermute | solution.py:228
  11.2 15.9 %all-to-all-start = ((f32[8,72,128]{2,1,0:T(8,128)}), f32[8,72,128]{2,1,0:T(8,128)S(1)}, u32[]{:S(2)}, u32[]{:S(2)}) async-start(f32[8,72,128]{2,1,0:T(8,128)} %pad_maximum_fusion.4), calls=%async_computation | async-start | bytes 589824 | tf_op jit(solution)/shard_map/all_to_all | solution.py:231
  17.5 10.3 %collective-permute-start.9 = (f32[128,128]{1,0:T(8,128)S(1)}, f32[128,128]{1,0:T(8,128)S(1)}, u32[]{:S(2)}, u32[]{:S(2)}) collective-permute-start(f32[128,128]{1,0:T(8,128)S(1)} %get-tuple-element.56), channel_id=1, source_target_pairs={{0,6},{2,0},{4,2},{6,4},{1,7},{3,1},{5,3},{7,5},{8,14},{10,8},{12,... | collective-permute-start | bytes 196616 | tf_op jit(solution)/shard_map/ppermute | solution.py:22
  21.6 7.2 %collective-permute-start.8 = (f32[128,128]{1,0:T(8,128)S(1)}, f32[128,128]{1,0:T(8,128)S(1)}, u32[]{:S(2)}, u32[]{:S(2)}) collective-permute-start(f32[128,128]{1,0:T(8,128)S(1)} %get-tuple-element.56), channel_id=1, source_target_pairs={{0,4},{2,6},{4,0},{6,2},{1,5},{3,7},{5,1},{7,3},{8,12},{10,14},{12... | collective-permute-start | bytes 196616 | tf_op jit(solution)/shard_map/ppermute | solution.py:22
  21.6 8.5 %collective-permute-start.7 = (f32[128,128]{1,0:T(8,128)S(1)}, f32[128,128]{1,0:T(8,128)S(1)}, u32[]{:S(2)}, u32[]{:S(2)}) collective-permute-start(f32[128,128]{1,0:T(8,128)S(1)} %get-tuple-element.56), channel_id=1, source_target_pairs={{0,2},{2,4},{4,6},{6,0},{1,3},{3,5},{5,7},{7,1},{8,10},{10,12},{12... | collective-permute-start | bytes 196616 | tf_op jit(solution)/shard_map/ppermute | solution.py:22
  22.9 16.5 %collective-permute-start.3 = (f32[3,128,128]{2,1,0:T(8,128)S(1)}, f32[3,128,128]{2,1,0:T(8,128)S(1)}, u32[]{:S(2)}, u32[]{:S(2)}) collective-permute-start(f32[3,128,128]{2,1,0:T(8,128)S(1)} %pad_maximum_fusion.7), channel_id=1, source_target_pairs={{0,96},{32,0},{64,32},{96,64},{1,97},{33,1},{65,33},{97,65},{2,98}... | collective-permute-start | bytes 589832 | tf_op jit(solution)/shard_map/ppermute | solution.py:22
  26.1 17.3 %collective-permute-start.2 = (f32[3,128,128]{2,1,0:T(8,128)S(1)}, f32[3,128,128]{2,1,0:T(8,128)S(1)}, u32[]{:S(2)}, u32[]{:S(2)}) collective-permute-start(f32[3,128,128]{2,1,0:T(8,128)S(1)} %pad_maximum_fusion.7), channel_id=1, source_target_pairs={{0,64},{32,96},{64,0},{96,32},{1,65},{33,97},{65,1},{97,33},{2,66}... | collective-permute-start | bytes 589832 | tf_op jit(solution)/shard_map/ppermute | solution.py:22
  27.8 15.7 %collective-permute-start.1 = (f32[3,128,128]{2,1,0:T(8,128)S(1)}, f32[3,128,128]{2,1,0:T(8,128)S(1)}, u32[]{:S(2)}, u32[]{:S(2)}) collective-permute-start(f32[3,128,128]{2,1,0:T(8,128)S(1)} %pad_maximum_fusion.7), channel_id=1, source_target_pairs={{0,32},{32,64},{64,96},{96,0},{1,33},{33,65},{65,97},{97,1},{2,34}... | collective-permute-start | bytes 589832 | tf_op jit(solution)/shard_map/ppermute | solution.py:22
  28.7 4.3 %collective-permute-start.13 = (f32[8,16,128]{2,1,0:T(8,128)S(1)}, f32[8,16,128]{2,1,0:T(8,128)S(1)}, u32[]{:S(2)}, u32[]{:S(2)}) collective-permute-start(f32[8,16,128]{2,1,0:T(8,128)S(1)} %get-tuple-element.40), channel_id=1, source_target_pairs={{0,8},{8,0},{1,9},{9,1},{2,10},{10,2},{3,11},{11,3},{4,12},{12,4},... | collective-permute-start | bytes 196616 | tf_op jit(solution)/shard_map/ppermute | solution.py:22
  30.1 25.9 %collective-permute-start.11 = (f32[4,128,128]{2,1,0:T(8,128)S(1)}, f32[4,128,128]{2,1,0:T(8,128)S(1)}, u32[]{:S(2)}, u32[]{:S(2)}) collective-permute-start(f32[4,128,128]{2,1,0:T(8,128)S(1)} %get-tuple-element.50), channel_id=1, source_target_pairs={{0,64},{32,96},{64,0},{96,32},{1,65},{33,97},{65,1},{97,33},{2,66}... | collective-permute-start | bytes 786440 | tf_op jit(solution)/shard_map/ppermute | solution.py:22
  33.0 26.9 %collective-permute-start.10 = (f32[4,128,128]{2,1,0:T(8,128)S(1)}, f32[4,128,128]{2,1,0:T(8,128)S(1)}, u32[]{:S(2)}, u32[]{:S(2)}) collective-permute-start(f32[4,128,128]{2,1,0:T(8,128)S(1)} %get-tuple-element.50), channel_id=1, source_target_pairs={{0,32},{32,64},{64,96},{96,0},{1,33},{33,65},{65,97},{97,1},{2,34}... | collective-permute-start | bytes 786440 | tf_op jit(solution)/shard_map/ppermute | solution.py:22
  39.3 20.6 %collective-permute-start.12 = (f32[4,128,128]{2,1,0:T(8,128)S(1)}, f32[4,128,128]{2,1,0:T(8,128)S(1)}, u32[]{:S(2)}, u32[]{:S(2)}) collective-permute-start(f32[4,128,128]{2,1,0:T(8,128)S(1)} %get-tuple-element.50), channel_id=1, source_target_pairs={{0,96},{32,0},{64,32},{96,64},{1,97},{33,1},{65,33},{97,65},{2,98}... | collective-permute-start | bytes 786440 | tf_op jit(solution)/shard_map/ppermute | solution.py:22
  43.4 1.3 collective-permute-start.14
  44.8 5.2 %collective-permute-start.17 = (f32[8,16,128]{2,1,0:T(8,128)S(1)}, f32[8,16,128]{2,1,0:T(8,128)S(1)}, u32[]{:S(2)}, u32[]{:S(2)}) collective-permute-start(f32[8,16,128]{2,1,0:T(8,128)S(1)} %add.93), channel_id=1, source_target_pairs={{0,6},{2,0},{4,2},{6,4},{1,7},{3,1},{5,3},{7,5},{8,14},{10,8},{12,... | collective-permute-start | bytes 196616 | tf_op jit(solution)/shard_map/ppermute | solution.py:22
  47.9 5.9 %collective-permute-start.16 = (f32[8,16,128]{2,1,0:T(8,128)S(1)}, f32[8,16,128]{2,1,0:T(8,128)S(1)}, u32[]{:S(2)}, u32[]{:S(2)}) collective-permute-start(f32[8,16,128]{2,1,0:T(8,128)S(1)} %add.93), channel_id=1, source_target_pairs={{0,4},{2,6},{4,0},{6,2},{1,5},{3,7},{5,1},{7,3},{8,12},{10,14},{12... | collective-permute-start | bytes 196616 | tf_op jit(solution)/shard_map/ppermute | solution.py:22
  50.0 6.1 %collective-permute-start.15 = (f32[8,16,128]{2,1,0:T(8,128)S(1)}, f32[8,16,128]{2,1,0:T(8,128)S(1)}, u32[]{:S(2)}, u32[]{:S(2)}) collective-permute-start(f32[8,16,128]{2,1,0:T(8,128)S(1)} %add.93), channel_id=1, source_target_pairs={{0,2},{2,4},{4,6},{6,0},{1,3},{3,5},{5,7},{7,1},{8,10},{10,12},{12... | collective-permute-start | bytes 196616 | tf_op jit(solution)/shard_map/ppermute | solution.py:22
  53.8 10.7 %collective-permute-start.5 = (f32[4,128,128]{2,1,0:T(8,128)S(1)}, f32[4,128,128]{2,1,0:T(8,128)S(1)}, u32[]{:S(2)}, u32[]{:S(2)}) collective-permute-start(f32[4,128,128]{2,1,0:T(8,128)S(1)} %get-tuple-element.52), channel_id=1, source_target_pairs={{0,4},{2,6},{4,0},{6,2},{1,5},{3,7},{5,1},{7,3},{8,12},{10,14},{12... | collective-permute-start | bytes 786440 | tf_op jit(solution)/shard_map/ppermute | solution.py:22
  56.1 11.7 %collective-permute-start.4 = (f32[4,128,128]{2,1,0:T(8,128)S(1)}, f32[4,128,128]{2,1,0:T(8,128)S(1)}, u32[]{:S(2)}, u32[]{:S(2)}) collective-permute-start(f32[4,128,128]{2,1,0:T(8,128)S(1)} %get-tuple-element.52), channel_id=1, source_target_pairs={{0,2},{2,4},{4,6},{6,0},{1,3},{3,5},{5,7},{7,1},{8,10},{10,12},{12... | collective-permute-start | bytes 786440 | tf_op jit(solution)/shard_map/ppermute | solution.py:22
  56.1 11.7 %collective-permute-start.6 = (f32[4,128,128]{2,1,0:T(8,128)S(1)}, f32[4,128,128]{2,1,0:T(8,128)S(1)}, u32[]{:S(2)}, u32[]{:S(2)}) collective-permute-start(f32[4,128,128]{2,1,0:T(8,128)S(1)} %get-tuple-element.52), channel_id=1, source_target_pairs={{0,6},{2,0},{4,2},{6,4},{1,7},{3,1},{5,3},{7,5},{8,14},{10,8},{12,... | collective-permute-start | bytes 786440 | tf_op jit(solution)/shard_map/ppermute | solution.py:22
  60.0 8.4 %copy-start = (f32[4,4,128,128]{3,2,1,0:T(8,128)}, f32[4,4,128,128]{3,2,1,0:T(8,128)S(1)}, u32[]{:S(2)}) copy-start(f32[4,4,128,128]{3,2,1,0:T(8,128)S(1)} %pad_maximum_fusion.2.o0_ref) | copy-start | bytes 3145732
  67.8 5.2 %copy-start.1 = (f32[4,4,128,128]{3,2,1,0:T(8,128)}, f32[4,4,128,128]{3,2,1,0:T(8,128)S(1)}, u32[]{:S(2)}) copy-start(f32[4,4,128,128]{3,2,1,0:T(8,128)S(1)} %pad_maximum_fusion.1.e0_ref) | copy-start | bytes 3145732
  67.8 5.2 %collective-permute-start.18 = (f32[4,4,128,128]{3,2,1,0:T(8,128)S(1)}, f32[4,4,128,128]{3,2,1,0:T(8,128)}, u32[]{:S(2)}, u32[]{:S(2)}) collective-permute-start(f32[4,4,128,128]{3,2,1,0:T(8,128)S(1)} %pad_maximum_fusion.1.e0_ref), channel_id=1, source_target_pairs={{0,1},{1,0},{2,3},{3,2},{4,5},{5,4},{6,7},{7,6},{8,9},{9,8},{10,11... | collective-permute-start | bytes 3145736 | tf_op jit(solution)/shard_map/ppermute | solution.py:22
  67.9 5.1 %collective-permute-start.19 = (f32[4,4,128,128]{3,2,1,0:T(8,128)S(1)}, f32[4,4,128,128]{3,2,1,0:T(8,128)}, u32[]{:S(2)}, u32[]{:S(2)}) collective-permute-start(f32[4,4,128,128]{3,2,1,0:T(8,128)S(1)} %pad_maximum_fusion.2.o0_ref), channel_id=1, source_target_pairs={{0,1},{1,0},{2,3},{3,2},{4,5},{5,4},{6,7},{7,6},{8,9},{9,8},{10,11... | collective-permute-start | bytes 3145736 | tf_op jit(solution)/shard_map/ppermute | solution.py:22
  68.4 35.9 %all-to-all-start.1 = ((f32[16,136,128]{2,1,0:T(8,128)}), f32[16,136,128]{2,1,0:T(8,128)S(1)}, u32[]{:S(2)}, u32[]{:S(2)}) async-start(f32[16,136,128]{2,1,0:T(8,128)} %pad_maximum_fusion), calls=%async_computation.1 | async-start | bytes 2228224 | tf_op jit(solution)/shard_map/all_to_all | solution.py:269
  77.0 9.9 %collective-permute-start.20 = (f32[8,16,128]{2,1,0:T(8,128)}, f32[8,16,128]{2,1,0:T(8,128)S(1)}, u32[]{:S(2)}, u32[]{:S(2)}) collective-permute-start(f32[8,16,128]{2,1,0:T(8,128)} %shard_map.59.first_ref), channel_id=1, source_target_pairs={{0,8},{1,9},{2,10},{3,11},{4,12},{5,13},{6,14},{7,15},{16,24},{17,... | collective-permute-start | bytes 196616 | tf_op jit(solution)/shard_map/ppermute | solution.py:268
  86.9 0.6 copy-start.6
  89.5 1.4 collective-permute-start.21
  91.6 6.9 %collective-permute-start.23 = (f32[2,16,128]{2,1,0:T(8,128)S(1)}, f32[2,16,128]{2,1,0:T(8,128)S(1)}, u32[]{:S(2)}, u32[]{:S(2)}) collective-permute-start(f32[2,16,128]{2,1,0:T(8,128)S(1)} %get-tuple-element.59), channel_id=1, source_target_pairs={{0,4},{2,6},{4,0},{6,2},{1,5},{3,7},{5,1},{7,3},{8,12},{10,14},{12... | collective-permute-start | bytes 49160 | tf_op jit(solution)/shard_map/ppermute | solution.py:22
  94.7 4.9 %collective-permute-start.22 = (f32[2,16,128]{2,1,0:T(8,128)S(1)}, f32[2,16,128]{2,1,0:T(8,128)S(1)}, u32[]{:S(2)}, u32[]{:S(2)}) collective-permute-start(f32[2,16,128]{2,1,0:T(8,128)S(1)} %get-tuple-element.59), channel_id=1, source_target_pairs={{0,2},{2,4},{4,6},{6,0},{1,3},{3,5},{5,7},{7,1},{8,10},{10,12},{12... | collective-permute-start | bytes 49160 | tf_op jit(solution)/shard_map/ppermute | solution.py:22
  95.4 4.3 %collective-permute-start.24 = (f32[2,16,128]{2,1,0:T(8,128)S(1)}, f32[2,16,128]{2,1,0:T(8,128)S(1)}, u32[]{:S(2)}, u32[]{:S(2)}) collective-permute-start(f32[2,16,128]{2,1,0:T(8,128)S(1)} %get-tuple-element.59), channel_id=1, source_target_pairs={{0,6},{2,0},{4,2},{6,4},{1,7},{3,1},{5,3},{7,5},{8,14},{10,8},{12,... | collective-permute-start | bytes 49160 | tf_op jit(solution)/shard_map/ppermute | solution.py:22
  104.3 18.4 %copy-start.2 = (f32[16,136,128]{2,1,0:T(8,128)}, f32[16,136,128]{2,1,0:T(8,128)S(1)}, u32[]{:S(2)}) copy-start(f32[16,136,128]{2,1,0:T(8,128)S(1)} %all-to-all-done.1.held_ref) | copy-start | bytes 3342340
  104.4 19.3 %all-to-all-start.2 = ((f32[16,16,128]{2,1,0:T(8,128)}), f32[16,16,128]{2,1,0:T(8,128)S(1)}, u32[]{:S(2)}, u32[]{:S(2)}) async-start(f32[16,16,128]{2,1,0:T(8,128)} %bitcast.105), calls=%async_computation.2 | async-start | bytes 262144 | tf_op jit(solution)/shard_map/all_to_all | solution.py:278
  123.6 0.7 copy-start.5
  124.3 16.5 %copy-start.4 = (f32[8,2,16,128]{3,2,1,0:T(8,128)S(1)}, f32[8,2,16,128]{3,2,1,0:T(8,128)}, u32[]{:S(2)}) copy-start(f32[8,2,16,128]{3,2,1,0:T(8,128)} %shard_map.61) | copy-start | bytes 393220
  134.7 9.8 %collective-permute-start.29 = (f32[2,16,16,128]{3,2,1,0:T(8,128)}, f32[2,16,16,128]{3,2,1,0:T(8,128)S(1)}, u32[]{:S(2)}, u32[]{:S(2)}) collective-permute-start(f32[2,16,16,128]{3,2,1,0:T(8,128)} %get-tuple-element.29), channel_id=1, source_target_pairs={{0,32},{32,64},{64,96},{96,0},{1,33},{33,65},{65,97},{97,1},{2,34}... | collective-permute-start | bytes 786440 | tf_op jit(solution)/shard_map/ppermute | solution.py:22
  136.7 12.9 %collective-permute-start.30 = (f32[2,16,16,128]{3,2,1,0:T(8,128)}, f32[2,16,16,128]{3,2,1,0:T(8,128)S(1)}, u32[]{:S(2)}, u32[]{:S(2)}) collective-permute-start(f32[2,16,16,128]{3,2,1,0:T(8,128)} %get-tuple-element.30), channel_id=1, source_target_pairs={{0,64},{32,96},{64,0},{96,32},{1,65},{33,97},{65,1},{97,33},{2,66}... | collective-permute-start | bytes 786440 | tf_op jit(solution)/shard_map/ppermute | solution.py:22
  139.3 10.2 %collective-permute-start.31 = (f32[2,16,16,128]{3,2,1,0:T(8,128)}, f32[2,16,16,128]{3,2,1,0:T(8,128)S(1)}, u32[]{:S(2)}, u32[]{:S(2)}) collective-permute-start(f32[2,16,16,128]{3,2,1,0:T(8,128)} %get-tuple-element.31), channel_id=1, source_target_pairs={{0,96},{32,0},{64,32},{96,64},{1,97},{33,1},{65,33},{97,65},{2,98}... | collective-permute-start | bytes 786440 | tf_op jit(solution)/shard_map/ppermute | solution.py:22
  140.8 13.1 %collective-permute-start.25 = (f32[4,15,16,128]{3,2,1,0:T(8,128)}, f32[4,15,16,128]{3,2,1,0:T(8,128)S(1)}, u32[]{:S(2)}, u32[]{:S(2)}) collective-permute-start(f32[4,15,16,128]{3,2,1,0:T(8,128)} %get-tuple-element.27), channel_id=1, source_target_pairs={{0,16},{16,0},{1,17},{17,1},{2,18},{18,2},{3,19},{19,3},{4,20},{20... | collective-permute-start | bytes 1474568 | tf_op jit(solution)/shard_map/ppermute | solution.py:22
  150.6 9.0 %collective-permute-start.32 = (f32[16,16,128]{2,1,0:T(8,128)S(1)}, f32[16,16,128]{2,1,0:T(8,128)S(1)}, u32[]{:S(2)}, u32[]{:S(2)}) collective-permute-start(f32[16,16,128]{2,1,0:T(8,128)S(1)} %slice_bitcast_fusion), channel_id=1, source_target_pairs={{0,16},{16,0},{1,17},{17,1},{2,18},{18,2},{3,19},{19,3},{4,20},{20... | collective-permute-start | bytes 393224 | tf_op jit(solution)/shard_map/ppermute | solution.py:22
  155.0 7.5 %collective-permute-start.27 = (f32[15,16,128]{2,1,0:T(8,128)S(1)}, f32[15,16,128]{2,1,0:T(8,128)S(1)}, u32[]{:S(2)}, u32[]{:S(2)}) collective-permute-start(f32[15,16,128]{2,1,0:T(8,128)S(1)} %get-tuple-element.42), channel_id=1, source_target_pairs={{0,64},{32,96},{64,0},{96,32},{1,65},{33,97},{65,1},{97,33},{2,66}... | collective-permute-start | bytes 368648 | tf_op jit(solution)/shard_map/ppermute | solution.py:22
  157.5 5.0 %collective-permute-start.28 = (f32[15,16,128]{2,1,0:T(8,128)S(1)}, f32[15,16,128]{2,1,0:T(8,128)S(1)}, u32[]{:S(2)}, u32[]{:S(2)}) collective-permute-start(f32[15,16,128]{2,1,0:T(8,128)S(1)} %get-tuple-element.43), channel_id=1, source_target_pairs={{0,96},{32,0},{64,32},{96,64},{1,97},{33,1},{65,33},{97,65},{2,98}... | collective-permute-start | bytes 368648 | tf_op jit(solution)/shard_map/ppermute | solution.py:22
  158.9 6.1 %collective-permute-start.26 = (f32[15,16,128]{2,1,0:T(8,128)S(1)}, f32[15,16,128]{2,1,0:T(8,128)S(1)}, u32[]{:S(2)}, u32[]{:S(2)}) collective-permute-start(f32[15,16,128]{2,1,0:T(8,128)S(1)} %get-tuple-element.44), channel_id=1, source_target_pairs={{0,32},{32,64},{64,96},{96,0},{1,33},{33,65},{65,97},{97,1},{2,34}... | collective-permute-start | bytes 368648 | tf_op jit(solution)/shard_map/ppermute | solution.py:22

commit v4 on v3

--- a/solution.py
+++ b/solution.py
@@ -2,6 +2,7 @@
 import jax.numpy as jnp
 from jax import lax
 from jax.experimental import pallas as pl
+from jax.experimental.layout import Layout, with_layout_constraint
 from jax.experimental.pallas import tpu as pltpu
 from jax.sharding import Mesh
 from jax.sharding import PartitionSpec as P
@@ -92,19 +93,12 @@
         out_ref[i, 1] = block
 
 
-def weights_kernel(after_ref, upper_ref, high_ref, low_ref):
-    for s in range(upper_ref.shape[2]):
-        high, low = split_bf16(upper_ref[:, :, s, :].reshape(2 * BLOCK, BLOCK))
-        high_ref[s] = high
-        low_ref[s] = low
-
-
 def update_kernel(
-    place_ref, slot_ref, rows_ref, held_ref, high_ref, low_ref,
+    place_ref, slot_ref, rows_ref, held_ref, factor_ref,
     a_keep, a_send, b_keep, b_one, b_two, b_three, left_high, left_low,
 ):
     step = pl.program_id(0)
-    count = high_ref.shape[0]
+    count = factor_ref.shape[1]
     last = pl.num_programs(0) - 1
     groups = [(yh, dx) for yh in range(2) for dx in range(4)]
     share = BLOCK // len(groups)
@@ -134,12 +128,16 @@
                 ref = (b_keep, b_one, b_two, b_three)[dx].at[yh, jnp.maximum(slot - 16, 0)]
                 ref[...] = values(g) + ref[...] if add else values(g)
 
-    for i in range(count):
+    for i in range(0, count, 2):
+        halves = [jnp.concatenate([factor_ref[t, i], factor_ref[t, i + 1]], axis=1) for t in range(2)]
+        high, low = split_bf16(jnp.concatenate(halves, axis=0))
         both = jnp.concatenate([left_high[...], left_low[...]], axis=0)
-        first = jnp.dot(both, high_ref[i], preferred_element_type=jnp.float32)
-        second = jnp.dot(left_high[...], low_ref[i], preferred_element_type=jnp.float32)
+        first = jnp.dot(both, high, preferred_element_type=jnp.float32)
+        second = jnp.dot(left_high[...], low, preferred_element_type=jnp.float32)
         total = first[:BLOCK] + first[BLOCK:] + second
-        put(step * count + i, lambda g: total[g * share : (g + 1) * share], False)
+        for k in range(2):
+            part = total[:, k * BLOCK : (k + 1) * BLOCK]
+            put(step * count + i + k, lambda g: part[g * share : (g + 1) * share], False)
 
     @pl.when(step == last)
     def _():
@@ -167,37 +165,20 @@
     )(*args)
 
 
-def split_weights(after, upper):
-    slots, step = upper.shape[2], 8
-    shape = jax.ShapeDtypeStruct((slots, 2 * BLOCK, BLOCK), jnp.bfloat16)
-    spec = pl.BlockSpec((step, 2 * BLOCK, BLOCK), lambda i: (i, 0, 0))
-    return pl.pallas_call(
-        weights_kernel,
-        out_shape=(shape, shape),
-        grid=(slots // step,),
-        in_specs=[
-            pl.BlockSpec((8, BLOCK), lambda i: (0, 0)),
-            pl.BlockSpec((2, BLOCK, step, BLOCK), lambda i: (0, 0, i, 0)),
-        ],
-        out_specs=(spec, spec),
-        cost_estimate=pl.CostEstimate(flops=600_000_000, bytes_accessed=8_000_000, transcendentals=0),
-    )(after, upper)
-
-
-def update(place, slot_of, own_rows, arrived, high, low):
-    slots, step = high.shape[0], 8
+def update(place, slot_of, own_rows, arrived, factor):
+    slots, step = factor.shape[1], 8
     share = own_rows.shape[2]
-    spec = pl.BlockSpec((step, 2 * BLOCK, BLOCK), lambda i: (i, 0, 0))
+    spec = pl.BlockSpec((2, step, BLOCK, BLOCK), lambda i: (0, i, 0, 0))
     shapes = [(4, 15, share, BLOCK)] * 2 + [(2, 16, share, BLOCK)] * 4
     return pl.pallas_call(
         update_kernel,
         out_shape=tuple(jax.ShapeDtypeStruct(shape, jnp.float32) for shape in shapes),
         grid=(slots // step,),
-        in_specs=[SMEM, SMEM, VMEM, VMEM, spec, spec],
+        in_specs=[SMEM, SMEM, VMEM, VMEM, spec],
         out_specs=(VMEM,) * 6,
         scratch_shapes=[pltpu.VMEM((BLOCK, 2 * BLOCK), jnp.bfloat16)] * 2,
         cost_estimate=pl.CostEstimate(flops=900_000_000, bytes_accessed=8_000_000, transcendentals=0),
-    )(place, slot_of, own_rows, arrived, high, low)
+    )(place, slot_of, own_rows, arrived, factor)
 
 
 def per_device(incoming, block_map, panel_row, diag_inverse):
@@ -233,7 +214,9 @@
     by_z = around(odd[0], "z")
     coupling = jnp.stack([p[1:] for p in by_x])
     even = jnp.stack([p[0] for p in by_x])
-    weights = split_weights(by_x[1][0, :8], upper)
+    upper, even = lax.optimization_barrier((upper, even))
+    upper = with_layout_constraint(upper, Layout(major_to_minor=(0, 1, 2, 3)))
+    factor = upper.transpose(0, 2, 1, 3)
     even = jnp.stack(around(even, "z"))
     odd = jnp.stack(around(jnp.stack(by_z), "x"))
 
@@ -279,7 +262,7 @@
         copies.reshape(rows * 2, share, BLOCK), ROW + ("yl",), 0, 0, tiled=True
     ).reshape(rows, 2, share, BLOCK)
     slot_of = arrived[:, BLOCK, 0].astype(jnp.int32)
-    a_keep, a_send, b_keep, *b_sends = update(place, slot_of, own_rows, arrived, *weights)
+    a_keep, a_send, b_keep, *b_sends = update(place, slot_of, own_rows, arrived, factor)
     a_part = a_keep + rotated(a_send, "yh", 1)
     b_part = b_keep
     for step, b_send in zip((1, 2, 3), b_sends):

time: 167 us -> 159 us (0.952)
  Pallas kernels: 33.1 us -> 17.9 us
  local copies, waits for them, and re-layouts: 7.83 us -> 13.7 us
  waiting for transfers between devices: 35.8 us -> 41.3 us
  starting transfers between devices: 76 us -> 72.3 us
    pallas_call x1 -> x0, Pallas kernels: 12.6 us -> none  [split_weights(): pl.pallas_call(weights_kernel, out_shape=(shape, shape), grid=(slots // s...]
    another operation x0 -> x1, local copies, waits for them, and re-layouts: none -> 6.58 us  [per_device(): upper = with_layout_constraint(upper, Layout(major_to_minor=(0, 1, 2, 3)))]
    ppermute x31, waiting for transfers between devices: 29.7 us -> 34.8 us  [rotated(): lax.ppermute(array, axis, [(i, (i + step) % size) for i in range(size)])]
    ppermute x31, starting transfers between devices: 54.8 us -> 51.8 us  [rotated(): lax.ppermute(array, axis, [(i, (i + step) % size) for i in range(size)])]
    pallas_call x1, Pallas kernels: 10.4 us -> 7.84 us  [update(): pl.pallas_call(update_kernel, out_shape=tuple((jax.ShapeDtypeStruct(shape...]
  transfers between devices with their start and end apart: 36 -> 36, of which waited for: 14 -> 17; matrix products, arithmetic and copies ran while one was open for 8% -> 12% of each run, Pallas kernels for 14% -> 6%
where the time goes in v4:
time: 159 us; the launch traced here: 158 us
  starting transfers between devices  72.3 us (45%)
  waiting for transfers between devices  41.3 us (26%)
  Pallas kernels  17.9 us (11%)
  local copies, waits for them, and re-layouts  13.7 us (9%)
  other arithmetic  11.2 us (7%)
    ppermute x31, starting transfers between devices, rotated(): lax.ppermute(array, axis, [(i, (i + step) % size) for i in range(size)])  51.8 us
    ppermute x31, waiting for transfers between devices, rotated(): lax.ppermute(array, axis, [(i, (i + step) % size) for i in range(size)])  34.8 us
    pallas_call x3, Pallas kernels, local_kernel(): pl.pallas_call(kernel, out_shape=jax.ShapeDtypeStruct(shape, jnp.float32)...  10 us
    pallas_call x1, Pallas kernels, update(): pl.pallas_call(update_kernel, out_shape=tuple((jax.ShapeDtypeStruct(shape...  7.84 us
    another operation x1, local copies, waits for them, and re-layouts, per_device(): upper = with_layout_constraint(upper, Layout(major_to_minor=(0, 1, 2, 3)))  6.58 us
    ppermute x1, waiting for transfers between devices, per_device(): passed = lax.ppermute(first, 'yl', [(0, 1)])  6.1 us
    all_to_all x1, starting transfers between devices, per_device(): lax.all_to_all(copies.reshape(rows * 2, share, BLOCK), ROW + ('yl',), 0,...  5.39 us
    all_to_all x1, starting transfers between devices, per_device(): received = lax.all_to_all(packed, ROW, 0, 0, tiled=True)  4.3 us
  transfers between devices with their start and end apart: 36, of which 17 were waited for; matrix products, arithmetic and copies ran while one was open for 12% of the time, Pallas kernels for 6%

profile of v4, /device:TPU:0, one launch (start us, length us, event | category | flops | bytes accessed | tf_op | source)
XLA Modules:
  0.0 158.5 jit_solution(6667444083591146595)
XLA Ops:
  0.7 1.1 slice.142
  1.8 1.3 slice.139
  3.1 1.1 fusion.5
  4.2 0.9 fusion.4
  5.1 3.4 %collective-permute-start = (f32[2,128,128]{2,1,0:T(8,128)S(1)}, f32[2,128,128]{2,1,0:T(8,128)S(1)}, u32[]{:S(2)}, u32[]{:S(2)}) collective-permute-start(f32[2,128,128]{2,1,0:T(8,128)S(1)} %pad_maximum_fusion.8), channel_id=1, source_target_pairs={{0,16},{16,0},{1,17},{17,1},{2,18},{18,2},{3,19},{19,3},{4,20},{20... | collective-permute-start | bytes 393224 | tf_op jit(solution)/shard_map/ppermute | solution.py:209
  8.5 0.8 add_convert_fusion
  9.3 1.0 copy.13
  10.3 0.8 pad_maximum_fusion.4
  11.1 4.3 %all-to-all-start = ((f32[8,72,128]{2,1,0:T(8,128)}), f32[8,72,128]{2,1,0:T(8,128)S(1)}, u32[]{:S(2)}, u32[]{:S(2)}) async-start(f32[8,72,128]{2,1,0:T(8,128)} %pad_maximum_fusion.4), calls=%async_computation | async-start | bytes 589824 | tf_op jit(solution)/shard_map/all_to_all | solution.py:212
  16.3 1.1 pad_maximum_fusion
  17.4 4.1 %collective-permute-start.9 = (f32[128,128]{1,0:T(8,128)S(1)}, f32[128,128]{1,0:T(8,128)S(1)}, u32[]{:S(2)}, u32[]{:S(2)}) collective-permute-start(f32[128,128]{1,0:T(8,128)S(1)} %get-tuple-element.54), channel_id=1, source_target_pairs={{0,6},{2,0},{4,2},{6,4},{1,7},{3,1},{5,3},{7,5},{8,14},{10,8},{12,... | collective-permute-start | bytes 196616 | tf_op jit(solution)/shard_map/ppermute | solution.py:23
  21.6 1.3 collective-permute-start.7
  22.8 3.3 %collective-permute-start.3 = (f32[3,128,128]{2,1,0:T(8,128)S(1)}, f32[3,128,128]{2,1,0:T(8,128)S(1)}, u32[]{:S(2)}, u32[]{:S(2)}) collective-permute-start(f32[3,128,128]{2,1,0:T(8,128)S(1)} %pad_maximum_fusion.7), channel_id=1, source_target_pairs={{0,96},{32,0},{64,32},{96,64},{1,97},{33,1},{65,33},{97,65},{2,98}... | collective-permute-start | bytes 589832 | tf_op jit(solution)/shard_map/ppermute | solution.py:23
  26.1 0.9 collective-permute-start.2
  27.8 0.9 collective-permute-start.1
  28.7 1.3 collective-permute-start.13
  30.1 2.3 %collective-permute-start.11 = (f32[4,128,128]{2,1,0:T(8,128)S(1)}, f32[4,128,128]{2,1,0:T(8,128)S(1)}, u32[]{:S(2)}, u32[]{:S(2)}) collective-permute-start(f32[4,128,128]{2,1,0:T(8,128)S(1)} %get-tuple-element.50), channel_id=1, source_target_pairs={{0,64},{32,96},{64,0},{96,32},{1,65},{33,97},{65,1},{97,33},{2,66}... | collective-permute-start | bytes 786440 | tf_op jit(solution)/shard_map/ppermute | solution.py:23
  33.0 1.8 %collective-permute-start.10 = (f32[4,128,128]{2,1,0:T(8,128)S(1)}, f32[4,128,128]{2,1,0:T(8,128)S(1)}, u32[]{:S(2)}, u32[]{:S(2)}) collective-permute-start(f32[4,128,128]{2,1,0:T(8,128)S(1)} %get-tuple-element.50), channel_id=1, source_target_pairs={{0,32},{32,64},{64,96},{96,0},{1,33},{33,65},{65,97},{97,1},{2,34}... | collective-permute-start | bytes 786440 | tf_op jit(solution)/shard_map/ppermute | solution.py:23
  34.8 4.5 %collective-permute-done.3 = f32[3,128,128]{2,1,0:T(8,128)S(1)} collective-permute-done((f32[3,128,128]{2,1,0:T(8,128)S(1)}, f32[3,128,128]{2,1,0:T(8,128)S(1)}, u32[]{:S(2)}, u32[]{:S(2)}) %collective-permute-start.3) | collective-permute-done | bytes 196640 | tf_op jit(solution)/shard_map/ppermute | solution.py:23
  39.3 4.1 %collective-permute-start.12 = (f32[4,128,128]{2,1,0:T(8,128)S(1)}, f32[4,128,128]{2,1,0:T(8,128)S(1)}, u32[]{:S(2)}, u32[]{:S(2)}) collective-permute-start(f32[4,128,128]{2,1,0:T(8,128)S(1)} %get-tuple-element.50), channel_id=1, source_target_pairs={{0,96},{32,0},{64,32},{96,64},{1,97},{33,1},{65,33},{97,65},{2,98}... | collective-permute-start | bytes 786440 | tf_op jit(solution)/shard_map/ppermute | solution.py:23
  43.6 1.2 collective-permute-done.14
  44.7 2.3 %collective-permute-start.17 = (f32[8,16,128]{2,1,0:T(8,128)S(1)}, f32[8,16,128]{2,1,0:T(8,128)S(1)}, u32[]{:S(2)}, u32[]{:S(2)}) collective-permute-start(f32[8,16,128]{2,1,0:T(8,128)S(1)} %add.93), channel_id=1, source_target_pairs={{0,6},{2,0},{4,2},{6,4},{1,7},{3,1},{5,3},{7,5},{8,14},{10,8},{12,... | collective-permute-start | bytes 196616 | tf_op jit(solution)/shard_map/ppermute | solution.py:23
  47.1 0.9 pad_maximum_fusion.3.x_ref
  47.9 2.0 %collective-permute-start.16 = (f32[8,16,128]{2,1,0:T(8,128)S(1)}, f32[8,16,128]{2,1,0:T(8,128)S(1)}, u32[]{:S(2)}, u32[]{:S(2)}) collective-permute-start(f32[8,16,128]{2,1,0:T(8,128)S(1)} %add.93), channel_id=1, source_target_pairs={{0,4},{2,6},{4,0},{6,2},{1,5},{3,7},{5,1},{7,3},{8,12},{10,14},{12... | collective-permute-start | bytes 196616 | tf_op jit(solution)/shard_map/ppermute | solution.py:23
  50.0 1.3 collective-permute-start.15
  51.3 2.5 %collective-permute-done.16 = f32[8,16,128]{2,1,0:T(8,128)S(1)} collective-permute-done((f32[8,16,128]{2,1,0:T(8,128)S(1)}, f32[8,16,128]{2,1,0:T(8,128)S(1)}, u32[]{:S(2)}, u32[]{:S(2)}) %collective-permute-start.16) | collective-permute-done | bytes 65568 | tf_op jit(solution)/shard_map/ppermute | solution.py:23
  53.8 0.8 collective-permute-start.6
  54.6 0.9 collective-permute-done.15
  55.4 1.1 collective-permute-start.5
  56.5 1.1 collective-permute-start.4
  57.7 0.6 add_add_fusion.1.start_ref
  58.4 4.6 %collective-permute-done.6 = f32[4,128,128]{2,1,0:T(8,128)S(1)} collective-permute-done((f32[4,128,128]{2,1,0:T(8,128)S(1)}, f32[4,128,128]{2,1,0:T(8,128)S(1)}, u32[]{:S(2)}, u32[]{:S(2)}) %collective-permute-start.6) | collective-permute-done | bytes 262176 | tf_op jit(solution)/shard_map/ppermute | solution.py:23
  63.0 3.2 %collective-permute-done.5 = f32[4,128,128]{2,1,0:T(8,128)S(1)} collective-permute-done((f32[4,128,128]{2,1,0:T(8,128)S(1)}, f32[4,128,128]{2,1,0:T(8,128)S(1)}, u32[]{:S(2)}, u32[]{:S(2)}) %collective-permute-start.5) | collective-permute-done | bytes 262176 | tf_op jit(solution)/shard_map/ppermute | solution.py:23
  66.1 3.4 %collective-permute-done.4 = f32[4,128,128]{2,1,0:T(8,128)S(1)} collective-permute-done((f32[4,128,128]{2,1,0:T(8,128)S(1)}, f32[4,128,128]{2,1,0:T(8,128)S(1)}, u32[]{:S(2)}, u32[]{:S(2)}) %collective-permute-start.4) | collective-permute-done | bytes 262176 | tf_op jit(solution)/shard_map/ppermute | solution.py:23
  70.2 3.7 %all-to-all-start.1 = ((f32[16,136,128]{2,1,0:T(8,128)}), f32[16,136,128]{2,1,0:T(8,128)S(1)}, u32[]{:S(2)}, u32[]{:S(2)}) async-start(f32[16,136,128]{2,1,0:T(8,128)} %pad_maximum_fusion), calls=%async_computation.1 | async-start | bytes 2228224 | tf_op jit(solution)/shard_map/all_to_all | solution.py:252
  74.5 4.0 %shard_map.59.first_ref = f32[8,16,128]{2,1,0:T(8,128)} custom-call(s32[5]{0:T(128)} %stack.115.place_ref, f32[8,16,128]{2,1,0:T(8,128)} %add_add_fusion.1.start_ref, f32[4,4,128,128]{3,2,1,0:T(8,128)} %copy-done.1, f32[4,4,128,128]{3,2,1,0:T(8,128)} %collective-permute-done.18.e1_ref, f32[4,4,128,128]{3,2,1,0:T(8,128)} %copy-done, ...), custom_call_target="tpu_custom_call" | custom-call | flops 600000000 | bytes 5000000 | tf_op jit(solution)/shard_map/pallas_call | solution.py:159
  78.5 3.7 %collective-permute-start.20 = (f32[8,16,128]{2,1,0:T(8,128)}, f32[8,16,128]{2,1,0:T(8,128)S(1)}, u32[]{:S(2)}, u32[]{:S(2)}) collective-permute-start(f32[8,16,128]{2,1,0:T(8,128)} %shard_map.59.first_ref), channel_id=1, source_target_pairs={{0,8},{1,9},{2,10},{3,11},{4,12},{5,13},{6,14},{7,15},{16,24},{17,... | collective-permute-start | bytes 196616 | tf_op jit(solution)/shard_map/ppermute | solution.py:251
  82.2 6.1 %collective-permute-done.20.passed_ref = f32[8,16,128]{2,1,0:T(8,128)S(1)} collective-permute-done((f32[8,16,128]{2,1,0:T(8,128)}, f32[8,16,128]{2,1,0:T(8,128)S(1)}, u32[]{:S(2)}, u32[]{:S(2)}) %collective-permute-start.20) | collective-permute-done | bytes 65568 | tf_op jit(solution)/shard_map/ppermute | solution.py:251
  89.0 2.0 %shard_map.60 = f32[16,128]{1,0:T(8,128)} custom-call(s32[5]{0:T(128)} %stack.115.place_ref, f32[8,16,128]{2,1,0:T(8,128)} %add_add_fusion.1.start_ref, f32[8,16,128]{2,1,0:T(8,128)} %copy-done.6, f32[4,2,128,128]{3,2,1,0:T(8,128)} %pad_maximum_fusion.3.x_ref), custom_call_target="tpu_custom_call" | custom-call | flops 600000000 | bytes 5000000 | tf_op jit(solution)/shard_map/pallas_call | solution.py:159
  91.0 1.4 collective-permute-done.21
  92.3 0.7 fusion.7
  93.0 3.1 %collective-permute-start.23 = (f32[2,16,128]{2,1,0:T(8,128)S(1)}, f32[2,16,128]{2,1,0:T(8,128)S(1)}, u32[]{:S(2)}, u32[]{:S(2)}) collective-permute-start(f32[2,16,128]{2,1,0:T(8,128)S(1)} %get-tuple-element.57), channel_id=1, source_target_pairs={{0,4},{2,6},{4,0},{6,2},{1,5},{3,7},{5,1},{7,3},{8,12},{10,14},{12... | collective-permute-start | bytes 49160 | tf_op jit(solution)/shard_map/ppermute | solution.py:23
  96.2 0.7 collective-permute-start.22
  96.8 2.6 %collective-permute-start.24 = (f32[2,16,128]{2,1,0:T(8,128)S(1)}, f32[2,16,128]{2,1,0:T(8,128)S(1)}, u32[]{:S(2)}, u32[]{:S(2)}) collective-permute-start(f32[2,16,128]{2,1,0:T(8,128)S(1)} %get-tuple-element.57), channel_id=1, source_target_pairs={{0,6},{2,0},{4,2},{6,4},{1,7},{3,1},{5,3},{7,5},{8,14},{10,8},{12,... | collective-permute-start | bytes 49160 | tf_op jit(solution)/shard_map/ppermute | solution.py:23
  99.4 1.7 %collective-permute-done.22 = f32[2,16,128]{2,1,0:T(8,128)S(1)} collective-permute-done((f32[2,16,128]{2,1,0:T(8,128)S(1)}, f32[2,16,128]{2,1,0:T(8,128)S(1)}, u32[]{:S(2)}, u32[]{:S(2)}) %collective-permute-start.22) | collective-permute-done | bytes 16416 | tf_op jit(solution)/shard_map/ppermute | solution.py:23
  101.1 0.6 pad_maximum_fusion.9.start_ref
  101.8 4.0 %shard_map.61 = f32[8,2,16,128]{3,2,1,0:T(8,128)} custom-call(s32[5]{0:T(128)} %stack.115.place_ref, f32[4,2,16,128]{3,2,1,0:T(8,128)} %pad_maximum_fusion.9.start_ref, f32[8,16,128]{2,1,0:T(8,128)} %shard_map.59.first_ref, f32[4,4,128,128]{3,2,1,0:T(8,128)} %copy-done.1, f32[4,4,128,128]{3,2,1,0:T(8,128)} %collective-permute-done.18.e1_ref, ...), custom_call_target="tpu_custom_call" | custom-call | flops 600000000 | bytes 5000000 | tf_op jit(solution)/shard_map/pallas_call | solution.py:159
  105.8 5.4 %all-to-all-start.2 = ((f32[16,16,128]{2,1,0:T(8,128)}), f32[16,16,128]{2,1,0:T(8,128)S(1)}, u32[]{:S(2)}, u32[]{:S(2)}) async-start(f32[16,16,128]{2,1,0:T(8,128)} %bitcast.107), calls=%async_computation.2 | async-start | bytes 262144 | tf_op jit(solution)/shard_map/all_to_all | solution.py:261
  111.2 6.6 %copy.17 = f32[2,128,32,128]{3,1,2,0:T(8,128)} copy(f32[2,128,32,128]{3,2,1,0:T(8,128)} %bitcast.102) | data formatting | bytes 8388608 | tf_op jit(solution)/shard_map/layout_constraint | solution.py:218
  117.8 0.9 convert_reduce_fusion.slot_ref
  119.7 7.8 %shard_map.62 = (f32[4,15,16,128]{3,2,1,0:T(8,128)}, f32[4,15,16,128]{3,2,1,0:T(8,128)}, f32[2,16,16,128]{3,2,1,0:T(8,128)}, f32[2,16,16,128]{3,2,1,0:T(8,128)},...) custom-call(s32[5]{0:T(128)} %stack.115.place_ref, s32[16]{0:T(128)} %convert_reduce_fusion.slot_ref, ...), custom_call_target="tpu_custom_call" | custom-call | flops 900000000 | bytes 8000000 | tf_op jit(solution)/shard_map/pallas_call | solution.py:173
  127.5 1.6 collective-permute-start.29
  129.1 2.7 %collective-permute-start.30 = (f32[2,16,16,128]{3,2,1,0:T(8,128)}, f32[2,16,16,128]{3,2,1,0:T(8,128)S(1)}, u32[]{:S(2)}, u32[]{:S(2)}) collective-permute-start(f32[2,16,16,128]{3,2,1,0:T(8,128)} %get-tuple-element.30), channel_id=1, source_target_pairs={{0,64},{32,96},{64,0},{96,32},{1,65},{33,97},{65,1},{97,33},{2,66}... | collective-permute-start | bytes 786440 | tf_op jit(solution)/shard_map/ppermute | solution.py:23
  131.8 1.5 collective-permute-start.31
  133.3 3.0 %collective-permute-start.25 = (f32[4,15,16,128]{3,2,1,0:T(8,128)}, f32[4,15,16,128]{3,2,1,0:T(8,128)S(1)}, u32[]{:S(2)}, u32[]{:S(2)}) collective-permute-start(f32[4,15,16,128]{3,2,1,0:T(8,128)} %get-tuple-element.27), channel_id=1, source_target_pairs={{0,16},{16,0},{1,17},{17,1},{2,18},{18,2},{3,19},{19,3},{4,20},{20... | collective-permute-start | bytes 1474568 | tf_op jit(solution)/shard_map/ppermute | solution.py:23
  137.1 4.9 %collective-permute-done.30 = f32[2,16,16,128]{3,2,1,0:T(8,128)S(1)} collective-permute-done((f32[2,16,16,128]{3,2,1,0:T(8,128)}, f32[2,16,16,128]{3,2,1,0:T(8,128)S(1)}, u32[]{:S(2)}, u32[]{:S(2)}) %collective-permute-start.30) | collective-permute-done | bytes 262176 | tf_op jit(solution)/shard_map/ppermute | solution.py:23
  142.0 1.0 add_add_fusion
  143.0 3.0 %collective-permute-start.32 = (f32[16,16,128]{2,1,0:T(8,128)S(1)}, f32[16,16,128]{2,1,0:T(8,128)S(1)}, u32[]{:S(2)}, u32[]{:S(2)}) collective-permute-start(f32[16,16,128]{2,1,0:T(8,128)S(1)} %slice_bitcast_fusion), channel_id=1, source_target_pairs={{0,16},{16,0},{1,17},{17,1},{2,18},{18,2},{3,19},{19,3},{4,20},{20... | collective-permute-start | bytes 393224 | tf_op jit(solution)/shard_map/ppermute | solution.py:23
  146.5 1.1 add.99
  147.6 2.4 %collective-permute-start.27 = (f32[15,16,128]{2,1,0:T(8,128)S(1)}, f32[15,16,128]{2,1,0:T(8,128)S(1)}, u32[]{:S(2)}, u32[]{:S(2)}) collective-permute-start(f32[15,16,128]{2,1,0:T(8,128)S(1)} %get-tuple-element.42), channel_id=1, source_target_pairs={{0,64},{32,96},{64,0},{96,32},{1,65},{33,97},{65,1},{97,33},{2,66}... | collective-permute-start | bytes 368648 | tf_op jit(solution)/shard_map/ppermute | solution.py:23
  150.0 1.4 collective-permute-start.28
  152.0 2.9 %collective-permute-done.27 = f32[15,16,128]{2,1,0:T(8,128)S(1)} collective-permute-done((f32[15,16,128]{2,1,0:T(8,128)S(1)}, f32[15,16,128]{2,1,0:T(8,128)S(1)}, u32[]{:S(2)}, u32[]{:S(2)}) %collective-permute-start.27) | collective-permute-done | bytes 122912 | tf_op jit(solution)/shard_map/ppermute | solution.py:23
  155.0 2.5 %collective-permute-done.26 = f32[15,16,128]{2,1,0:T(8,128)S(1)} collective-permute-done((f32[15,16,128]{2,1,0:T(8,128)S(1)}, f32[15,16,128]{2,1,0:T(8,128)S(1)}, u32[]{:S(2)}, u32[]{:S(2)}) %collective-permute-start.26) | collective-permute-done | bytes 122912 | tf_op jit(solution)/shard_map/ppermute | solution.py:23
  157.5 1.0 copy.15
  (86 shorter events, 7.5 us)
Async XLA Ops:
  0.6 14.8 %copy-start.7 = (s32[1,1,4]{2,1,0:T(1,128)S(1)}, s32[1,1,4]{2,1,0:T(1,128)}, u32[]{:S(2)}) copy-start(s32[1,1,4]{2,1,0:T(1,128)} %param.5) | copy-start | bytes 52
  0.6 14.8 %copy-start.3 = (f32[1,1,4,128,128]{4,3,2,1,0:T(8,128)S(1)}, f32[1,1,4,128,128]{4,3,2,1,0:T(8,128)}, u32[]{:S(2)}) copy-start(f32[1,1,4,128,128]{4,3,2,1,0:T(8,128)} %param.4) | copy-start | bytes 786436
  5.1 12.3 %collective-permute-start = (f32[2,128,128]{2,1,0:T(8,128)S(1)}, f32[2,128,128]{2,1,0:T(8,128)S(1)}, u32[]{:S(2)}, u32[]{:S(2)}) collective-permute-start(f32[2,128,128]{2,1,0:T(8,128)S(1)} %pad_maximum_fusion.8), channel_id=1, source_target_pairs={{0,16},{16,0},{1,17},{17,1},{2,18},{18,2},{3,19},{19,3},{4,20},{20... | collective-permute-start | bytes 393224 | tf_op jit(solution)/shard_map/ppermute | solution.py:209
  11.1 15.9 %all-to-all-start = ((f32[8,72,128]{2,1,0:T(8,128)}), f32[8,72,128]{2,1,0:T(8,128)S(1)}, u32[]{:S(2)}, u32[]{:S(2)}) async-start(f32[8,72,128]{2,1,0:T(8,128)} %pad_maximum_fusion.4), calls=%async_computation | async-start | bytes 589824 | tf_op jit(solution)/shard_map/all_to_all | solution.py:212
  17.4 10.3 %collective-permute-start.9 = (f32[128,128]{1,0:T(8,128)S(1)}, f32[128,128]{1,0:T(8,128)S(1)}, u32[]{:S(2)}, u32[]{:S(2)}) collective-permute-start(f32[128,128]{1,0:T(8,128)S(1)} %get-tuple-element.54), channel_id=1, source_target_pairs={{0,6},{2,0},{4,2},{6,4},{1,7},{3,1},{5,3},{7,5},{8,14},{10,8},{12,... | collective-permute-start | bytes 196616 | tf_op jit(solution)/shard_map/ppermute | solution.py:23
  21.6 7.2 %collective-permute-start.8 = (f32[128,128]{1,0:T(8,128)S(1)}, f32[128,128]{1,0:T(8,128)S(1)}, u32[]{:S(2)}, u32[]{:S(2)}) collective-permute-start(f32[128,128]{1,0:T(8,128)S(1)} %get-tuple-element.54), channel_id=1, source_target_pairs={{0,4},{2,6},{4,0},{6,2},{1,5},{3,7},{5,1},{7,3},{8,12},{10,14},{12... | collective-permute-start | bytes 196616 | tf_op jit(solution)/shard_map/ppermute | solution.py:23
  21.6 8.5 %collective-permute-start.7 = (f32[128,128]{1,0:T(8,128)S(1)}, f32[128,128]{1,0:T(8,128)S(1)}, u32[]{:S(2)}, u32[]{:S(2)}) collective-permute-start(f32[128,128]{1,0:T(8,128)S(1)} %get-tuple-element.54), channel_id=1, source_target_pairs={{0,2},{2,4},{4,6},{6,0},{1,3},{3,5},{5,7},{7,1},{8,10},{10,12},{12... | collective-permute-start | bytes 196616 | tf_op jit(solution)/shard_map/ppermute | solution.py:23
  22.8 16.5 %collective-permute-start.3 = (f32[3,128,128]{2,1,0:T(8,128)S(1)}, f32[3,128,128]{2,1,0:T(8,128)S(1)}, u32[]{:S(2)}, u32[]{:S(2)}) collective-permute-start(f32[3,128,128]{2,1,0:T(8,128)S(1)} %pad_maximum_fusion.7), channel_id=1, source_target_pairs={{0,96},{32,0},{64,32},{96,64},{1,97},{33,1},{65,33},{97,65},{2,98}... | collective-permute-start | bytes 589832 | tf_op jit(solution)/shard_map/ppermute | solution.py:23
  26.1 17.3 %collective-permute-start.2 = (f32[3,128,128]{2,1,0:T(8,128)S(1)}, f32[3,128,128]{2,1,0:T(8,128)S(1)}, u32[]{:S(2)}, u32[]{:S(2)}) collective-permute-start(f32[3,128,128]{2,1,0:T(8,128)S(1)} %pad_maximum_fusion.7), channel_id=1, source_target_pairs={{0,64},{32,96},{64,0},{96,32},{1,65},{33,97},{65,1},{97,33},{2,66}... | collective-permute-start | bytes 589832 | tf_op jit(solution)/shard_map/ppermute | solution.py:23
  27.8 15.7 %collective-permute-start.1 = (f32[3,128,128]{2,1,0:T(8,128)S(1)}, f32[3,128,128]{2,1,0:T(8,128)S(1)}, u32[]{:S(2)}, u32[]{:S(2)}) collective-permute-start(f32[3,128,128]{2,1,0:T(8,128)S(1)} %pad_maximum_fusion.7), channel_id=1, source_target_pairs={{0,32},{32,64},{64,96},{96,0},{1,33},{33,65},{65,97},{97,1},{2,34}... | collective-permute-start | bytes 589832 | tf_op jit(solution)/shard_map/ppermute | solution.py:23
  28.7 4.3 %collective-permute-start.13 = (f32[8,16,128]{2,1,0:T(8,128)S(1)}, f32[8,16,128]{2,1,0:T(8,128)S(1)}, u32[]{:S(2)}, u32[]{:S(2)}) collective-permute-start(f32[8,16,128]{2,1,0:T(8,128)S(1)} %get-tuple-element.40), channel_id=1, source_target_pairs={{0,8},{8,0},{1,9},{9,1},{2,10},{10,2},{3,11},{11,3},{4,12},{12,4},... | collective-permute-start | bytes 196616 | tf_op jit(solution)/shard_map/ppermute | solution.py:23
  30.1 26.4 %collective-permute-start.11 = (f32[4,128,128]{2,1,0:T(8,128)S(1)}, f32[4,128,128]{2,1,0:T(8,128)S(1)}, u32[]{:S(2)}, u32[]{:S(2)}) collective-permute-start(f32[4,128,128]{2,1,0:T(8,128)S(1)} %get-tuple-element.50), channel_id=1, source_target_pairs={{0,64},{32,96},{64,0},{96,32},{1,65},{33,97},{65,1},{97,33},{2,66}... | collective-permute-start | bytes 786440 | tf_op jit(solution)/shard_map/ppermute | solution.py:23
  33.0 25.3 %collective-permute-start.10 = (f32[4,128,128]{2,1,0:T(8,128)S(1)}, f32[4,128,128]{2,1,0:T(8,128)S(1)}, u32[]{:S(2)}, u32[]{:S(2)}) collective-permute-start(f32[4,128,128]{2,1,0:T(8,128)S(1)} %get-tuple-element.50), channel_id=1, source_target_pairs={{0,32},{32,64},{64,96},{96,0},{1,33},{33,65},{65,97},{97,1},{2,34}... | collective-permute-start | bytes 786440 | tf_op jit(solution)/shard_map/ppermute | solution.py:23
  39.3 19.0 %collective-permute-start.12 = (f32[4,128,128]{2,1,0:T(8,128)S(1)}, f32[4,128,128]{2,1,0:T(8,128)S(1)}, u32[]{:S(2)}, u32[]{:S(2)}) collective-permute-start(f32[4,128,128]{2,1,0:T(8,128)S(1)} %get-tuple-element.50), channel_id=1, source_target_pairs={{0,96},{32,0},{64,32},{96,64},{1,97},{33,1},{65,33},{97,65},{2,98}... | collective-permute-start | bytes 786440 | tf_op jit(solution)/shard_map/ppermute | solution.py:23
  43.4 1.3 collective-permute-start.14
  44.7 5.2 %collective-permute-start.17 = (f32[8,16,128]{2,1,0:T(8,128)S(1)}, f32[8,16,128]{2,1,0:T(8,128)S(1)}, u32[]{:S(2)}, u32[]{:S(2)}) collective-permute-start(f32[8,16,128]{2,1,0:T(8,128)S(1)} %add.93), channel_id=1, source_target_pairs={{0,6},{2,0},{4,2},{6,4},{1,7},{3,1},{5,3},{7,5},{8,14},{10,8},{12,... | collective-permute-start | bytes 196616 | tf_op jit(solution)/shard_map/ppermute | solution.py:23
  47.9 5.9 %collective-permute-start.16 = (f32[8,16,128]{2,1,0:T(8,128)S(1)}, f32[8,16,128]{2,1,0:T(8,128)S(1)}, u32[]{:S(2)}, u32[]{:S(2)}) collective-permute-start(f32[8,16,128]{2,1,0:T(8,128)S(1)} %add.93), channel_id=1, source_target_pairs={{0,4},{2,6},{4,0},{6,2},{1,5},{3,7},{5,1},{7,3},{8,12},{10,14},{12... | collective-permute-start | bytes 196616 | tf_op jit(solution)/shard_map/ppermute | solution.py:23
  50.0 5.5 %collective-permute-start.15 = (f32[8,16,128]{2,1,0:T(8,128)S(1)}, f32[8,16,128]{2,1,0:T(8,128)S(1)}, u32[]{:S(2)}, u32[]{:S(2)}) collective-permute-start(f32[8,16,128]{2,1,0:T(8,128)S(1)} %add.93), channel_id=1, source_target_pairs={{0,2},{2,4},{4,6},{6,0},{1,3},{3,5},{5,7},{7,1},{8,10},{10,12},{12... | collective-permute-start | bytes 196616 | tf_op jit(solution)/shard_map/ppermute | solution.py:23
  53.8 9.2 %collective-permute-start.6 = (f32[4,128,128]{2,1,0:T(8,128)S(1)}, f32[4,128,128]{2,1,0:T(8,128)S(1)}, u32[]{:S(2)}, u32[]{:S(2)}) collective-permute-start(f32[4,128,128]{2,1,0:T(8,128)S(1)} %pad_maximum_fusion.5), channel_id=1, source_target_pairs={{0,6},{2,0},{4,2},{6,4},{1,7},{3,1},{5,3},{7,5},{8,14},{10,8},{12,... | collective-permute-start | bytes 786440 | tf_op jit(solution)/shard_map/ppermute | solution.py:23
  55.4 10.7 %collective-permute-start.5 = (f32[4,128,128]{2,1,0:T(8,128)S(1)}, f32[4,128,128]{2,1,0:T(8,128)S(1)}, u32[]{:S(2)}, u32[]{:S(2)}) collective-permute-start(f32[4,128,128]{2,1,0:T(8,128)S(1)} %pad_maximum_fusion.5), channel_id=1, source_target_pairs={{0,4},{2,6},{4,0},{6,2},{1,5},{3,7},{5,1},{7,3},{8,12},{10,14},{12... | collective-permute-start | bytes 786440 | tf_op jit(solution)/shard_map/ppermute | solution.py:23
  56.5 13.0 %collective-permute-start.4 = (f32[4,128,128]{2,1,0:T(8,128)S(1)}, f32[4,128,128]{2,1,0:T(8,128)S(1)}, u32[]{:S(2)}, u32[]{:S(2)}) collective-permute-start(f32[4,128,128]{2,1,0:T(8,128)S(1)} %pad_maximum_fusion.5), channel_id=1, source_target_pairs={{0,2},{2,4},{4,6},{6,0},{1,3},{3,5},{5,7},{7,1},{8,10},{10,12},{12... | collective-permute-start | bytes 786440 | tf_op jit(solution)/shard_map/ppermute | solution.py:23
  58.4 11.8 %copy-start = (f32[4,4,128,128]{3,2,1,0:T(8,128)}, f32[4,4,128,128]{3,2,1,0:T(8,128)S(1)}, u32[]{:S(2)}) copy-start(f32[4,4,128,128]{3,2,1,0:T(8,128)S(1)} %pad_maximum_fusion.2.o0_ref) | copy-start | bytes 3145732
  69.6 4.9 %copy-start.1 = (f32[4,4,128,128]{3,2,1,0:T(8,128)}, f32[4,4,128,128]{3,2,1,0:T(8,128)S(1)}, u32[]{:S(2)}) copy-start(f32[4,4,128,128]{3,2,1,0:T(8,128)S(1)} %pad_maximum_fusion.1.e0_ref) | copy-start | bytes 3145732
  69.6 4.9 %collective-permute-start.18 = (f32[4,4,128,128]{3,2,1,0:T(8,128)S(1)}, f32[4,4,128,128]{3,2,1,0:T(8,128)}, u32[]{:S(2)}, u32[]{:S(2)}) collective-permute-start(f32[4,4,128,128]{3,2,1,0:T(8,128)S(1)} %pad_maximum_fusion.1.e0_ref), channel_id=1, source_target_pairs={{0,1},{1,0},{2,3},{3,2},{4,5},{5,4},{6,7},{7,6},{8,9},{9,8},{10,11... | collective-permute-start | bytes 3145736 | tf_op jit(solution)/shard_map/ppermute | solution.py:23
  69.7 4.8 %collective-permute-start.19 = (f32[4,4,128,128]{3,2,1,0:T(8,128)S(1)}, f32[4,4,128,128]{3,2,1,0:T(8,128)}, u32[]{:S(2)}, u32[]{:S(2)}) collective-permute-start(f32[4,4,128,128]{3,2,1,0:T(8,128)S(1)} %pad_maximum_fusion.2.o0_ref), channel_id=1, source_target_pairs={{0,1},{1,0},{2,3},{3,2},{4,5},{5,4},{6,7},{7,6},{8,9},{9,8},{10,11... | collective-permute-start | bytes 3145736 | tf_op jit(solution)/shard_map/ppermute | solution.py:23
  70.2 35.6 %all-to-all-start.1 = ((f32[16,136,128]{2,1,0:T(8,128)}), f32[16,136,128]{2,1,0:T(8,128)S(1)}, u32[]{:S(2)}, u32[]{:S(2)}) async-start(f32[16,136,128]{2,1,0:T(8,128)} %pad_maximum_fusion), calls=%async_computation.1 | async-start | bytes 2228224 | tf_op jit(solution)/shard_map/all_to_all | solution.py:252
  78.5 9.9 %collective-permute-start.20 = (f32[8,16,128]{2,1,0:T(8,128)}, f32[8,16,128]{2,1,0:T(8,128)S(1)}, u32[]{:S(2)}, u32[]{:S(2)}) collective-permute-start(f32[8,16,128]{2,1,0:T(8,128)} %shard_map.59.first_ref), channel_id=1, source_target_pairs={{0,8},{1,9},{2,10},{3,11},{4,12},{5,13},{6,14},{7,15},{16,24},{17,... | collective-permute-start | bytes 196616 | tf_op jit(solution)/shard_map/ppermute | solution.py:251
  88.3 0.6 copy-start.6
  91.0 1.4 collective-permute-start.21
  93.0 6.4 %collective-permute-start.23 = (f32[2,16,128]{2,1,0:T(8,128)S(1)}, f32[2,16,128]{2,1,0:T(8,128)S(1)}, u32[]{:S(2)}, u32[]{:S(2)}) collective-permute-start(f32[2,16,128]{2,1,0:T(8,128)S(1)} %get-tuple-element.57), channel_id=1, source_target_pairs={{0,4},{2,6},{4,0},{6,2},{1,5},{3,7},{5,1},{7,3},{8,12},{10,14},{12... | collective-permute-start | bytes 49160 | tf_op jit(solution)/shard_map/ppermute | solution.py:23
  96.2 4.9 %collective-permute-start.22 = (f32[2,16,128]{2,1,0:T(8,128)S(1)}, f32[2,16,128]{2,1,0:T(8,128)S(1)}, u32[]{:S(2)}, u32[]{:S(2)}) collective-permute-start(f32[2,16,128]{2,1,0:T(8,128)S(1)} %get-tuple-element.57), channel_id=1, source_target_pairs={{0,2},{2,4},{4,6},{6,0},{1,3},{3,5},{5,7},{7,1},{8,10},{10,12},{12... | collective-permute-start | bytes 49160 | tf_op jit(solution)/shard_map/ppermute | solution.py:23
  96.8 4.3 %collective-permute-start.24 = (f32[2,16,128]{2,1,0:T(8,128)S(1)}, f32[2,16,128]{2,1,0:T(8,128)S(1)}, u32[]{:S(2)}, u32[]{:S(2)}) collective-permute-start(f32[2,16,128]{2,1,0:T(8,128)S(1)} %get-tuple-element.57), channel_id=1, source_target_pairs={{0,6},{2,0},{4,2},{6,4},{1,7},{3,1},{5,3},{7,5},{8,14},{10,8},{12,... | collective-permute-start | bytes 49160 | tf_op jit(solution)/shard_map/ppermute | solution.py:23
  105.8 12.0 %copy-start.2 = (f32[16,136,128]{2,1,0:T(8,128)}, f32[16,136,128]{2,1,0:T(8,128)S(1)}, u32[]{:S(2)}) copy-start(f32[16,136,128]{2,1,0:T(8,128)S(1)} %all-to-all-done.1.held_ref) | copy-start | bytes 3342340
  105.8 13.2 %all-to-all-start.2 = ((f32[16,16,128]{2,1,0:T(8,128)}), f32[16,16,128]{2,1,0:T(8,128)S(1)}, u32[]{:S(2)}, u32[]{:S(2)}) async-start(f32[16,16,128]{2,1,0:T(8,128)} %bitcast.107), calls=%async_computation.2 | async-start | bytes 262144 | tf_op jit(solution)/shard_map/all_to_all | solution.py:261
  119.1 0.6 copy-start.5
  119.7 13.5 %copy-start.4 = (f32[8,2,16,128]{3,2,1,0:T(8,128)S(1)}, f32[8,2,16,128]{3,2,1,0:T(8,128)}, u32[]{:S(2)}) copy-start(f32[8,2,16,128]{3,2,1,0:T(8,128)} %shard_map.61) | copy-start | bytes 393220
  127.5 9.6 %collective-permute-start.29 = (f32[2,16,16,128]{3,2,1,0:T(8,128)}, f32[2,16,16,128]{3,2,1,0:T(8,128)S(1)}, u32[]{:S(2)}, u32[]{:S(2)}) collective-permute-start(f32[2,16,16,128]{3,2,1,0:T(8,128)} %get-tuple-element.29), channel_id=1, source_target_pairs={{0,32},{32,64},{64,96},{96,0},{1,33},{33,65},{65,97},{97,1},{2,34}... | collective-permute-start | bytes 786440 | tf_op jit(solution)/shard_map/ppermute | solution.py:23
  129.1 12.9 %collective-permute-start.30 = (f32[2,16,16,128]{3,2,1,0:T(8,128)}, f32[2,16,16,128]{3,2,1,0:T(8,128)S(1)}, u32[]{:S(2)}, u32[]{:S(2)}) collective-permute-start(f32[2,16,16,128]{3,2,1,0:T(8,128)} %get-tuple-element.30), channel_id=1, source_target_pairs={{0,64},{32,96},{64,0},{96,32},{1,65},{33,97},{65,1},{97,33},{2,66}... | collective-permute-start | bytes 786440 | tf_op jit(solution)/shard_map/ppermute | solution.py:23
  131.8 10.2 %collective-permute-start.31 = (f32[2,16,16,128]{3,2,1,0:T(8,128)}, f32[2,16,16,128]{3,2,1,0:T(8,128)S(1)}, u32[]{:S(2)}, u32[]{:S(2)}) collective-permute-start(f32[2,16,16,128]{3,2,1,0:T(8,128)} %get-tuple-element.31), channel_id=1, source_target_pairs={{0,96},{32,0},{64,32},{96,64},{1,97},{33,1},{65,33},{97,65},{2,98}... | collective-permute-start | bytes 786440 | tf_op jit(solution)/shard_map/ppermute | solution.py:23
  133.3 13.2 %collective-permute-start.25 = (f32[4,15,16,128]{3,2,1,0:T(8,128)}, f32[4,15,16,128]{3,2,1,0:T(8,128)S(1)}, u32[]{:S(2)}, u32[]{:S(2)}) collective-permute-start(f32[4,15,16,128]{3,2,1,0:T(8,128)} %get-tuple-element.27), channel_id=1, source_target_pairs={{0,16},{16,0},{1,17},{17,1},{2,18},{18,2},{3,19},{19,3},{4,20},{20... | collective-permute-start | bytes 1474568 | tf_op jit(solution)/shard_map/ppermute | solution.py:23
  143.0 9.0 %collective-permute-start.32 = (f32[16,16,128]{2,1,0:T(8,128)S(1)}, f32[16,16,128]{2,1,0:T(8,128)S(1)}, u32[]{:S(2)}, u32[]{:S(2)}) collective-permute-start(f32[16,16,128]{2,1,0:T(8,128)S(1)} %slice_bitcast_fusion), channel_id=1, source_target_pairs={{0,16},{16,0},{1,17},{17,1},{2,18},{18,2},{3,19},{19,3},{4,20},{20... | collective-permute-start | bytes 393224 | tf_op jit(solution)/shard_map/ppermute | solution.py:23
  147.6 7.4 %collective-permute-start.27 = (f32[15,16,128]{2,1,0:T(8,128)S(1)}, f32[15,16,128]{2,1,0:T(8,128)S(1)}, u32[]{:S(2)}, u32[]{:S(2)}) collective-permute-start(f32[15,16,128]{2,1,0:T(8,128)S(1)} %get-tuple-element.42), channel_id=1, source_target_pairs={{0,64},{32,96},{64,0},{96,32},{1,65},{33,97},{65,1},{97,33},{2,66}... | collective-permute-start | bytes 368648 | tf_op jit(solution)/shard_map/ppermute | solution.py:23
  150.0 5.0 %collective-permute-start.28 = (f32[15,16,128]{2,1,0:T(8,128)S(1)}, f32[15,16,128]{2,1,0:T(8,128)S(1)}, u32[]{:S(2)}, u32[]{:S(2)}) collective-permute-start(f32[15,16,128]{2,1,0:T(8,128)S(1)} %get-tuple-element.43), channel_id=1, source_target_pairs={{0,96},{32,0},{64,32},{96,64},{1,97},{33,1},{65,33},{97,65},{2,98}... | collective-permute-start | bytes 368648 | tf_op jit(solution)/shard_map/ppermute | solution.py:23
  151.4 6.1 %collective-permute-start.26 = (f32[15,16,128]{2,1,0:T(8,128)S(1)}, f32[15,16,128]{2,1,0:T(8,128)S(1)}, u32[]{:S(2)}, u32[]{:S(2)}) collective-permute-start(f32[15,16,128]{2,1,0:T(8,128)S(1)} %get-tuple-element.44), channel_id=1, source_target_pairs={{0,32},{32,64},{64,96},{96,0},{1,33},{33,65},{65,97},{97,1},{2,34}... | collective-permute-start | bytes 368648 | tf_op jit(solution)/shard_map/ppermute | solution.py:23

commit v5 on v2

--- a/solution.py
+++ b/solution.py
@@ -2,6 +2,7 @@
 import jax.numpy as jnp
 from jax import lax
 from jax.experimental import pallas as pl
+from jax.experimental.layout import Layout, with_layout_constraint
 from jax.experimental.pallas import tpu as pltpu
 from jax.sharding import Mesh
 from jax.sharding import PartitionSpec as P
@@ -72,11 +73,10 @@
 
 def coupling_kernel(place_ref, start_ref, passed_ref, x_ref, out_ref):
     my_x, my_z, my_core = place_ref[0], place_ref[1], place_ref[2]
-    total = start_ref[my_z * 2 + my_core]
-    for j in range(HALF):
-        dx = lax.rem(my_x - j // 2 + 4, 4)
-        total = total - product(split_bf16(passed_ref[j]), x_ref[dx, j % 2])
-    out_ref[...] = total
+    left = jnp.concatenate([passed_ref[j] for j in range(HALF)], axis=1)
+    right = [x_ref[lax.rem(my_x - j // 2 + 4, 4), j % 2] for j in range(HALF)]
+    carried = product(split_bf16(left), jnp.concatenate(right, axis=0))
+    out_ref[...] = start_ref[my_z * 2 + my_core] - carried
 
 
 def second_kernel(place_ref, start_ref, first_ref, e0_ref, e1_ref, o0_ref, o1_ref, out_ref):
@@ -90,6 +90,58 @@
         block = jnp.where(place_ref[3] == 0, first_ref[i], solved[i])
         out_ref[i, 0] = block
         out_ref[i, 1] = block
+
+
+def update_kernel(
+    place_ref, rows_ref, factor_ref, a_keep, a_send, b_keep, b_one, b_two, b_three, left_high, left_low
+):
+    step = pl.program_id(0)
+    count = factor_ref.shape[1]
+    groups = [(yh, dx) for yh in range(2) for dx in range(4)]
+    share = BLOCK // len(groups)
+
+    @pl.when(step == 0)
+    def _():
+        for g, (yh, dx) in enumerate(groups):
+            row = lax.rem(place_ref[0] + dx, 4) * 2 + lax.rem(place_ref[4] + yh, 2)
+            for t in range(2):
+                high, low = split_bf16(-rows_ref[row, t])
+                at = (pl.ds(g * share, share), pl.ds(t * BLOCK, BLOCK))
+                left_high[at] = high
+                left_low[at] = low
+
+    def fill(target):
+        both = jnp.concatenate([left_high[...], left_low[...]], axis=0)
+        for i in range(0, count, 2):
+            halves = [
+                jnp.concatenate([factor_ref[t, i], factor_ref[t, i + 1]], axis=1) for t in range(2)
+            ]
+            high, low = split_bf16(jnp.concatenate(halves, axis=0))
+            first = jnp.dot(both, high, preferred_element_type=jnp.float32)
+            second = jnp.dot(left_high[...], low, preferred_element_type=jnp.float32)
+            total = first[:BLOCK] + first[BLOCK:] + second
+            for k in range(2):
+                for g, (yh, dx) in enumerate(groups):
+                    target(i + k, yh, dx, total[g * share : (g + 1) * share, k * BLOCK : (k + 1) * BLOCK])
+
+    def fill_a(slot, yh, dx, values):
+        if slot > 0:
+            (a_keep, a_send)[yh][dx, slot - 1] = values
+
+    def fill_b(slot, yh, dx, values):
+        (b_keep, b_one, b_two, b_three)[dx][yh, slot] = values
+
+    pl.when(step == 0)(lambda: fill(fill_a))
+    pl.when(step == 1)(lambda: fill(fill_b))
+
+
+def place_kernel(slot_ref, arrived_ref, out_ref):
+    spare = out_ref.shape[0] - 1
+    share = out_ref.shape[1]
+    for q in range(slot_ref.shape[0]):
+        slot = slot_ref[q]
+        rows = pl.ds(q % 8 * share, share)
+        out_ref[jnp.where(slot < 0, spare, slot)] = arrived_ref[q // 8, rows, :]
 
 
 def local_kernel(kernel, shape, *args):
@@ -102,6 +154,22 @@
     )(*args)
 
 
+def update(place, own_rows, factor):
+    slots, step = factor.shape[1], 16
+    share = own_rows.shape[2]
+    spec = pl.BlockSpec((2, step, BLOCK, BLOCK), lambda i: (0, i, 0, 0))
+    shapes = [(4, 15, share, BLOCK)] * 2 + [(2, 16, share, BLOCK)] * 4
+    return pl.pallas_call(
+        update_kernel,
+        out_shape=tuple(jax.ShapeDtypeStruct(shape, jnp.float32) for shape in shapes),
+        grid=(slots // step,),
+        in_specs=[SMEM, VMEM, spec],
+        out_specs=(VMEM,) * 6,
+        scratch_shapes=[pltpu.VMEM((BLOCK, 2 * BLOCK), jnp.bfloat16)] * 2,
+        cost_estimate=pl.CostEstimate(flops=900_000_000, bytes_accessed=8_000_000, transcendentals=0),
+    )(place, own_rows, factor)
+
+
 def per_device(incoming, block_map, panel_row, diag_inverse):
     my_x, my_yh, my_yl, my_z, my_core = (lax.axis_index(a) for a in ("x", "yh", "yl", "z", "core"))
     my_row = lax.axis_index(ROW)
@@ -110,7 +178,7 @@
     sources = incoming.shape[2]
     share = BLOCK // rows
     slots = panel_row.shape[3]
-    place = jnp.stack([my_x, my_z, my_core, my_yl]).astype(jnp.int32)
+    place = jnp.stack([my_x, my_z, my_core, my_yl, my_yh]).astype(jnp.int32)
 
     targets = block_map.reshape(sources)
     blocks = incoming.reshape(sources, BLOCK, BLOCK)
@@ -131,11 +199,9 @@
     even = jnp.where(my_yh == 0, pair, other)
     odd = jnp.where(my_yh == 0, other, pair)
     received = lax.all_to_all(packed, ROW, 0, 0, tiled=True)
-    by_x = around(jnp.stack([even[0], even[1], odd[1]]), "x")
+    column = jnp.stack([even[1], odd[1]])
     by_z = around(odd[0], "z")
-    coupling = jnp.stack([p[1:] for p in by_x])
-    even = jnp.stack([p[0] for p in by_x])
-    upper, even = lax.optimization_barrier((upper, even))
+    even = jnp.stack(around(even[0], "x"))
     even = jnp.stack(around(even, "z"))
     odd = jnp.stack(around(jnp.stack(by_z), "x"))
 
@@ -152,46 +218,59 @@
     start = start + rotated(start, "core", 1)
     start = sum(around(start, "z"))
 
-    even_other = rotated(even, "core", 1)
-    odd_other = rotated(odd, "core", 1)
-    factors = (even, even_other, odd, odd_other)
-
-    chosen = (targets[None, :] % cols) == jnp.arange(cols, dtype=jnp.int32)[:, None]
-    outgoing = jnp.zeros((cols, BLOCK, BLOCK), jnp.float32)
+    goal = received[:, sources * share : sources * share + sources, 0].astype(jnp.int32)
+    chosen = (goal[None] % cols) == jnp.arange(cols, dtype=jnp.int32)[:, None, None]
+    outgoing = jnp.zeros((cols, rows, share, BLOCK), jnp.float32)
     for u in range(sources):
-        outgoing = jnp.where(chosen[:, u, None, None], blocks[u][None], outgoing)
-    slot_label = jnp.max(jnp.where(chosen, targets[None, :] // cols, -1), axis=1)
-    slot_label = jnp.broadcast_to(slot_label.astype(jnp.float32)[:, None, None], (cols, 8, BLOCK))
-    outgoing = jnp.concatenate([outgoing, slot_label], axis=1)
+        outgoing = jnp.where(chosen[:, :, u, None, None], data[None, :, u], outgoing)
+    slot_label = jnp.max(jnp.where(chosen, goal[None] // cols, -1), axis=2).astype(jnp.float32)
+    slot_label = jnp.broadcast_to(slot_label[:, :, None], (cols, rows, BLOCK))
+    outgoing = jnp.concatenate([outgoing.reshape(cols, BLOCK, BLOCK), slot_label], axis=1)
+
+    even, odd, start = lax.optimization_barrier((even, odd, start))
+    factors = (even, rotated(even, "core", 1), odd, rotated(odd, "core", 1))
+    column, even = lax.optimization_barrier((column, even))
+    coupling = jnp.stack(around(column, "x"))
 
     shape = (HALF, share, BLOCK)
     first = local_kernel(first_kernel, shape, place, start, *factors)
     passed = lax.ppermute(first, "yl", [(0, 1)])
-    arrived = lax.all_to_all(outgoing, COL, 0, 0, tiled=True)
+    passed, outgoing = lax.optimization_barrier((passed, outgoing))
     residual = local_kernel(
         coupling_kernel, (share, BLOCK), place, start, passed, coupling
     )
-    residual = jnp.stack(around(jnp.stack(around(residual, "core")), "z"))
+    residual = jnp.stack(around(residual, "core"))
+    upper, residual = lax.optimization_barrier((upper, residual))
+    upper = with_layout_constraint(upper, Layout(major_to_minor=(0, 1, 2, 3)))
+    factor = upper.transpose(0, 2, 1, 3)
+    residual = jnp.stack(around(residual, "z"))
     copies = local_kernel(
         second_kernel, (HALF, 2, share, BLOCK), place, residual, first, *factors
     )
-    copies, arrived = lax.optimization_barrier((copies, arrived))
     panel_solution = lax.dynamic_index_in_dim(copies[:, 0], my_plane, 0, keepdims=False)
 
     own_rows = lax.all_to_all(
         copies.reshape(rows * 2, share, BLOCK), ROW + ("yl",), 0, 0, tiled=True
     ).reshape(rows, 2, share, BLOCK)
-    slot_of = arrived[:, BLOCK, 0].astype(jnp.int32)
-    matches = (slot_of[None, :] == jnp.arange(1, slots, dtype=jnp.int32)[:, None]).astype(jnp.float32)
-    held = arrived[:, :BLOCK].reshape(cols, rows, share, BLOCK)
-    held = jnp.einsum("sq,qrke->rkse", matches, held, precision=HIGHEST)
-    partial = held - jnp.einsum(
-        "rtkp,tpse->rkse", own_rows, upper[:, :, 1:, :], precision=lax.Precision.HIGH
-    )
-    trailing = lax.dynamic_index_in_dim(partial, my_row, 0, keepdims=False)
-    for step in range(1, rows):
-        part = lax.dynamic_index_in_dim(partial, my_row ^ step, 0, keepdims=False)
-        trailing = trailing + lax.ppermute(part, ROW, [(i, i ^ step) for i in range(rows)])
+    a_keep, a_send, b_keep, *b_sends = update(place, own_rows, factor)
+    outgoing, a_keep = lax.optimization_barrier((outgoing, a_keep))
+    a_part = a_keep + rotated(a_send, "yh", 1)
+    b_part = b_keep
+    for step, b_send in zip((1, 2, 3), b_sends):
+        b_part = b_part + rotated(b_send, "x", step)
+    arrived = lax.all_to_all(outgoing, COL, 0, 0, tiled=True)
+    b_part = b_part[0] + rotated(b_part[1], "yh", 1)
+    a_part = a_part[0] + sum(rotated(a_part[step], "x", step) for step in (1, 2, 3))
+    slot_of = arrived[:, BLOCK:, 0].astype(jnp.int32).reshape(cols * rows)
+    held = pl.pallas_call(
+        place_kernel,
+        out_shape=jax.ShapeDtypeStruct((slots + 1, share, BLOCK), jnp.float32),
+        in_specs=[SMEM, VMEM],
+        out_specs=VMEM,
+        cost_estimate=pl.CostEstimate(flops=100_000_000, bytes_accessed=2_000_000, transcendentals=0),
+    )(slot_of, arrived)
+    trailing = held[1:slots] + jnp.concatenate([a_part, b_part], axis=0)
+    trailing = trailing.transpose(1, 0, 2)
     return panel_solution[:, None, None, :], trailing[:, :, None, :]
 
 

time: 163 us -> 163 us (level)
  waiting for transfers between devices: 56.6 us -> 31.9 us
  local copies, waits for them, and re-layouts: 14.5 us -> 26.4 us
  Pallas kernels: 10 us -> 16.3 us
  starting transfers between devices: 67.4 us -> 72.9 us
  matrix products: 5.44 us -> 1.12 us
  other arithmetic: 7.74 us -> 11.9 us
    ppermute x23 -> x34, starting transfers between devices: 31.5 us -> 49.8 us  [rotated(): lax.ppermute(array, axis, [(i, (i + step) % size) for i in range(size)])]
    ppermute x7 -> x0, waiting for transfers between devices: 16.3 us -> none  [per_device(): lax.ppermute(part, ROW, [(i, i ^ step) for i in range(rows)])]
    ppermute x7 -> x0, starting transfers between devices: 14.6 us -> none  [per_device(): lax.ppermute(part, ROW, [(i, i ^ step) for i in range(rows)])]
    broadcast_in_dim x3 -> x14, local copies, waits for them, and re-layouts: 0.11 us -> 10.4 us  [the longest x13 9.64 us: per_device(): jnp.where(chosen[:, :, u, None, None], data[None, :, u], outgoing)]
    another operation x3, local copies, waits for them, and re-layouts: 0.94 us -> 8.16 us  [the longest x1 6.59 us: per_device(): upper = with_layout_constraint(upper, Layout(major_to_minor=(0, 1, 2, 3)))]
    pallas_call x0 -> x2, Pallas kernels: none -> 6.38 us  [the longest x1 4.23 us: update(): pl.pallas_call(update_kernel, out_shape=tuple((jax.ShapeDtypeStruct(shape...]
    unnamed x22 -> x20, local copies, waits for them, and re-layouts: 9.17 us -> 3.38 us
    all_to_all x1, waiting for transfers between devices: 6.69 us -> 1.26 us  [per_device(): lax.all_to_all(copies.reshape(rows * 2, share, BLOCK), ROW + ('yl',), 0,...]
  transfers between devices with their start and end apart: 35 -> 39, of which waited for: 20 -> 17; matrix products, arithmetic and copies ran while one was open for 8% -> 18% of each run, Pallas kernels for 6% -> 2%
where the time goes in v5:
time: 163 us; the launch traced here: 162 us
  starting transfers between devices  72.9 us (45%)
  waiting for transfers between devices  31.9 us (20%)
  local copies, waits for them, and re-layouts  26.4 us (16%)
  Pallas kernels  16.3 us (10%)
  other arithmetic  11.9 us (7%)
    ppermute x34, starting transfers between devices, rotated(): lax.ppermute(array, axis, [(i, (i + step) % size) for i in range(size)])  49.8 us
    ppermute x34, waiting for transfers between devices, rotated(): lax.ppermute(array, axis, [(i, (i + step) % size) for i in range(size)])  30.3 us
    pallas_call x3, Pallas kernels, local_kernel(): pl.pallas_call(kernel, out_shape=jax.ShapeDtypeStruct(shape, jnp.float32)...  9.97 us
    broadcast_in_dim x13, local copies, waits for them, and re-layouts, per_device(): jnp.where(chosen[:, :, u, None, None], data[None, :, u], outgoing)  9.64 us
    all_to_all x1, starting transfers between devices, per_device(): lax.all_to_all(copies.reshape(rows * 2, share, BLOCK), ROW + ('yl',), 0,...  8.71 us
    another operation x1, local copies, waits for them, and re-layouts, per_device(): upper = with_layout_constraint(upper, Layout(major_to_minor=(0, 1, 2, 3)))  6.59 us
    all_to_all x1, starting transfers between devices, per_device(): received = lax.all_to_all(packed, ROW, 0, 0, tiled=True)  4.3 us
    pallas_call x1, Pallas kernels, update(): pl.pallas_call(update_kernel, out_shape=tuple((jax.ShapeDtypeStruct(shape...  4.23 us
  transfers between devices with their start and end apart: 39, of which 17 were waited for; matrix products, arithmetic and copies ran while one was open for 18% of the time, Pallas kernels for 2%

profile of v5, /device:TPU:0, one launch (start us, length us, event | category | flops | bytes accessed | tf_op | source)
XLA Modules:
  0.0 161.7 jit_solution(8366290101082337877)
XLA Ops:
  0.6 1.1 slice.120
  1.7 1.3 slice.117
  3.0 1.1 fusion.5
  4.2 0.9 fusion.4
  5.0 3.4 %collective-permute-start = (f32[2,128,128]{2,1,0:T(8,128)S(1)}, f32[2,128,128]{2,1,0:T(8,128)S(1)}, u32[]{:S(2)}, u32[]{:S(2)}) collective-permute-start(f32[2,128,128]{2,1,0:T(8,128)S(1)} %pad_maximum_fusion.7), channel_id=1, source_target_pairs={{0,16},{16,0},{1,17},{17,1},{2,18},{18,2},{3,19},{19,3},{4,20},{20... | collective-permute-start | bytes 393224 | tf_op jit(solution)/shard_map/ppermute | solution.py:198
  8.4 0.8 add_convert_fusion
  9.2 1.0 copy.50
  10.3 0.8 pad_maximum_fusion.4
  11.1 4.3 %all-to-all-start = ((f32[8,72,128]{2,1,0:T(8,128)}), f32[8,72,128]{2,1,0:T(8,128)S(1)}, u32[]{:S(2)}, u32[]{:S(2)}) async-start(f32[8,72,128]{2,1,0:T(8,128)} %pad_maximum_fusion.4), calls=%async_computation | async-start | bytes 589824 | tf_op jit(solution)/shard_map/all_to_all | solution.py:201
  16.1 4.1 %collective-permute-start.9 = (f32[128,128]{1,0:T(8,128)S(1)}, f32[128,128]{1,0:T(8,128)S(1)}, u32[]{:S(2)}, u32[]{:S(2)}) collective-permute-start(f32[128,128]{1,0:T(8,128)S(1)} %get-tuple-element.63), channel_id=1, source_target_pairs={{0,6},{2,0},{4,2},{6,4},{1,7},{3,1},{5,3},{7,5},{8,14},{10,8},{12,... | collective-permute-start | bytes 196616 | tf_op jit(solution)/shard_map/ppermute | solution.py:23
  20.2 1.3 collective-permute-start.7
  21.4 3.3 %collective-permute-start.3 = (f32[128,128]{1,0:T(8,128)S(1)}, f32[128,128]{1,0:T(8,128)S(1)}, u32[]{:S(2)}, u32[]{:S(2)}) collective-permute-start(f32[128,128]{1,0:T(8,128)S(1)} %get-tuple-element.60), channel_id=1, source_target_pairs={{0,96},{32,0},{64,32},{96,64},{1,97},{33,1},{65,33},{97,65},{2,98}... | collective-permute-start | bytes 196616 | tf_op jit(solution)/shard_map/ppermute | solution.py:23
  24.7 0.9 collective-permute-start.2
  26.4 0.9 collective-permute-start.1
  27.3 1.3 collective-permute-start.13
  28.7 2.3 %collective-permute-start.11 = (f32[4,128,128]{2,1,0:T(8,128)S(1)}, f32[4,128,128]{2,1,0:T(8,128)S(1)}, u32[]{:S(2)}, u32[]{:S(2)}) collective-permute-start(f32[4,128,128]{2,1,0:T(8,128)S(1)} %get-tuple-element.54), channel_id=1, source_target_pairs={{0,64},{32,96},{64,0},{96,32},{1,65},{33,97},{65,1},{97,33},{2,66}... | collective-permute-start | bytes 786440 | tf_op jit(solution)/shard_map/ppermute | solution.py:23
  31.6 1.8 %collective-permute-start.10 = (f32[4,128,128]{2,1,0:T(8,128)S(1)}, f32[4,128,128]{2,1,0:T(8,128)S(1)}, u32[]{:S(2)}, u32[]{:S(2)}) collective-permute-start(f32[4,128,128]{2,1,0:T(8,128)S(1)} %get-tuple-element.54), channel_id=1, source_target_pairs={{0,32},{32,64},{64,96},{96,0},{1,33},{33,65},{65,97},{97,1},{2,34}... | collective-permute-start | bytes 786440 | tf_op jit(solution)/shard_map/ppermute | solution.py:23
  33.4 1.5 collective-permute-start.12
  35.3 0.9 collective-permute-done.14
  36.2 2.2 %collective-permute-start.17 = (f32[8,16,128]{2,1,0:T(8,128)S(1)}, f32[8,16,128]{2,1,0:T(8,128)S(1)}, u32[]{:S(2)}, u32[]{:S(2)}) collective-permute-start(f32[8,16,128]{2,1,0:T(8,128)S(1)} %add.96), channel_id=1, source_target_pairs={{0,6},{2,0},{4,2},{6,4},{1,7},{3,1},{5,3},{7,5},{8,14},{10,8},{12,... | collective-permute-start | bytes 196616 | tf_op jit(solution)/shard_map/ppermute | solution.py:23
  38.4 2.2 %collective-permute-start.16 = (f32[8,16,128]{2,1,0:T(8,128)S(1)}, f32[8,16,128]{2,1,0:T(8,128)S(1)}, u32[]{:S(2)}, u32[]{:S(2)}) collective-permute-start(f32[8,16,128]{2,1,0:T(8,128)S(1)} %add.96), channel_id=1, source_target_pairs={{0,4},{2,6},{4,0},{6,2},{1,5},{3,7},{5,1},{7,3},{8,12},{10,14},{12... | collective-permute-start | bytes 196616 | tf_op jit(solution)/shard_map/ppermute | solution.py:23
  40.7 1.0 collective-permute-done.17
  41.6 1.1 collective-permute-start.15
  42.9 1.4 collective-permute-done.16
  44.3 2.7 %collective-permute-start.5 = (f32[4,128,128]{2,1,0:T(8,128)S(1)}, f32[4,128,128]{2,1,0:T(8,128)S(1)}, u32[]{:S(2)}, u32[]{:S(2)}) collective-permute-start(f32[4,128,128]{2,1,0:T(8,128)S(1)} %get-tuple-element.58), channel_id=1, source_target_pairs={{0,4},{2,6},{4,0},{6,2},{1,5},{3,7},{5,1},{7,3},{8,12},{10,14},{12... | collective-permute-start | bytes 786440 | tf_op jit(solution)/shard_map/ppermute | solution.py:23
  46.9 2.5 %collective-permute-done.15 = f32[8,16,128]{2,1,0:T(8,128)S(1)} collective-permute-done((f32[8,16,128]{2,1,0:T(8,128)S(1)}, f32[8,16,128]{2,1,0:T(8,128)S(1)}, u32[]{:S(2)}, u32[]{:S(2)}) %collective-permute-start.15) | collective-permute-done | bytes 65568 | tf_op jit(solution)/shard_map/ppermute | solution.py:23
  49.4 3.2 %collective-permute-start.6 = (f32[4,128,128]{2,1,0:T(8,128)S(1)}, f32[4,128,128]{2,1,0:T(8,128)S(1)}, u32[]{:S(2)}, u32[]{:S(2)}) collective-permute-start(f32[4,128,128]{2,1,0:T(8,128)S(1)} %get-tuple-element.58), channel_id=1, source_target_pairs={{0,6},{2,0},{4,2},{6,4},{1,7},{3,1},{5,3},{7,5},{8,14},{10,8},{12,... | collective-permute-start | bytes 786440 | tf_op jit(solution)/shard_map/ppermute | solution.py:23
  53.4 1.9 %collective-permute-done.5 = f32[4,128,128]{2,1,0:T(8,128)S(1)} collective-permute-done((f32[4,128,128]{2,1,0:T(8,128)S(1)}, f32[4,128,128]{2,1,0:T(8,128)S(1)}, u32[]{:S(2)}, u32[]{:S(2)}) %collective-permute-start.5) | collective-permute-done | bytes 262176 | tf_op jit(solution)/shard_map/ppermute | solution.py:23
  55.3 3.5 %collective-permute-done.4 = f32[4,128,128]{2,1,0:T(8,128)S(1)} collective-permute-done((f32[4,128,128]{2,1,0:T(8,128)S(1)}, f32[4,128,128]{2,1,0:T(8,128)S(1)}, u32[]{:S(2)}, u32[]{:S(2)}) %collective-permute-start.4) | collective-permute-done | bytes 262176 | tf_op jit(solution)/shard_map/ppermute | solution.py:23
  60.1 1.3 copy.52
  67.0 0.8 broadcast_in_dim.172
  69.9 1.9 %select_select_fusion = f32[16,128,128]{2,1,0:T(8,128)S(1)} fusion(f32[128,128]{1,0:T(8,128)S(1)} %bitcast.127, f32[128,128]{1,0:T(8,128)S(1)} %bitcast.128, f32[128,128]{1,0:T(8,128)S(1)} %bitcast.129, f32[128,128]{1,0:T(8,128)S(1)} %bitcast.126, pred[16,128]{1,0:T(8,128)(4,1)} %broadcast_in_dim.173, pred[16,128]{1,0:T(8,128)(4,1)} %broadcast_in_dim.167, ...), kind=kLoop, calls=%fused_computation.6 | loop fusion | flops 1048576 | bytes 1318912 | tf_op jit(solution)/shard_map/jit(_where)/select_n | solution.py:225
  71.7 1.5 collective-permute-start.23
  73.3 1.0 collective-permute-start.22
  74.5 0.8 broadcast_in_dim.180
  75.3 1.1 pad_maximum_fusion
  76.4 1.0 copy-done.3
  77.3 4.0 %shard_map.59.first_ref = f32[8,16,128]{2,1,0:T(8,128)} custom-call(s32[5]{0:T(128)} %stack.123.place_ref, f32[8,16,128]{2,1,0:T(8,128)} %add_add_fusion.1.start_ref, f32[4,4,128,128]{3,2,1,0:T(8,128)} %copy-done.1, f32[4,4,128,128]{3,2,1,0:T(8,128)} %collective-permute-done.18.e1_ref, f32[4,4,128,128]{3,2,1,0:T(8,128)} %copy-done, f32[4,4,128,128]{3,2,1,0:T(8,128)} %copy-done.3), custom_call_target="tpu_custom_call" | custom-call | flops 600000000 | bytes 5000000 | tf_op jit(solution)/shard_map/pallas_call | solution.py:148
  81.3 3.0 %collective-permute-start.20 = (f32[8,16,128]{2,1,0:T(8,128)}, f32[8,16,128]{2,1,0:T(8,128)S(1)}, u32[]{:S(2)}, u32[]{:S(2)}) collective-permute-start(f32[8,16,128]{2,1,0:T(8,128)} %shard_map.59.first_ref), channel_id=1, source_target_pairs={{0,8},{1,9},{2,10},{3,11},{4,12},{5,13},{6,14},{7,15},{16,24},{17,... | collective-permute-start | bytes 196616 | tf_op jit(solution)/shard_map/ppermute | solution.py:237
  84.4 1.8 %pad_maximum_fusion.3.x_ref = f32[4,2,128,128]{3,2,1,0:T(8,128)} fusion(f32[1,2,128,128]{3,2,1,0:T(8,128)S(1)} %bitcast.136, f32[1,2,128,128]{3,2,1,0:T(8,128)} %bitcast.43, f32[1,2,128,128]{3,2,1,0:T(8,128)} %bitcast.42, f32[1,2,128,128]{3,2,1,0:T(8,128)S(1)} %bitcast.124), kind=kLoop, calls=%fused_computation.7 | loop fusion | flops 393216 | bytes 1048576 | tf_op jit(solution)/shard_map/stack | solution.py:233
  87.2 1.9 %shard_map.60 = f32[16,128]{1,0:T(8,128)} custom-call(s32[5]{0:T(128)} %stack.123.place_ref, f32[8,16,128]{2,1,0:T(8,128)} %add_add_fusion.1.start_ref, f32[8,16,128]{2,1,0:T(8,128)} %copy-done.8, f32[4,2,128,128]{3,2,1,0:T(8,128)} %pad_maximum_fusion.3.x_ref), custom_call_target="tpu_custom_call" | custom-call | flops 600000000 | bytes 5000000 | tf_op jit(solution)/shard_map/pallas_call | solution.py:148
  89.1 1.4 collective-permute-done.24
  91.2 1.3 collective-permute-start.27
  92.5 1.2 collective-permute-start.26
  93.7 0.8 collective-permute-start.25
  94.9 2.9 %collective-permute-done.26 = f32[2,16,128]{2,1,0:T(8,128)S(1)} collective-permute-done((f32[2,16,128]{2,1,0:T(8,128)S(1)}, f32[2,16,128]{2,1,0:T(8,128)S(1)}, u32[]{:S(2)}, u32[]{:S(2)}) %collective-permute-start.26) | collective-permute-done | bytes 16416 | tf_op jit(solution)/shard_map/ppermute | solution.py:23
  97.9 0.8 collective-permute-done.25
  99.3 4.0 %shard_map.61 = f32[8,2,16,128]{3,2,1,0:T(8,128)} custom-call(s32[5]{0:T(128)} %stack.123.place_ref, f32[4,2,16,128]{3,2,1,0:T(8,128)} %pad_maximum_fusion.9.start_ref, f32[8,16,128]{2,1,0:T(8,128)} %shard_map.59.first_ref, f32[4,4,128,128]{3,2,1,0:T(8,128)} %copy-done.1, f32[4,4,128,128]{3,2,1,0:T(8,128)} %collective-permute-done.18.e1_ref, ...), custom_call_target="tpu_custom_call" | custom-call | flops 600000000 | bytes 5000000 | tf_op jit(solution)/shard_map/pallas_call | solution.py:148
  103.4 8.7 %all-to-all-start.1 = ((f32[16,16,128]{2,1,0:T(8,128)}), f32[16,16,128]{2,1,0:T(8,128)S(1)}, u32[]{:S(2)}, u32[]{:S(2)}) async-start(f32[16,16,128]{2,1,0:T(8,128)} %bitcast.119), calls=%async_computation.1 | async-start | bytes 262144 | tf_op jit(solution)/shard_map/all_to_all | solution.py:252
  112.1 6.6 %copy.61 = f32[2,128,32,128]{3,1,2,0:T(8,128)} copy(f32[2,128,32,128]{3,2,1,0:T(8,128)} %bitcast.115) | data formatting | bytes 8388608 | tf_op jit(solution)/shard_map/layout_constraint | solution.py:244
  118.7 1.3 all-to-all-done.1
  120.6 4.2 %shard_map.62 = (f32[4,15,16,128]{3,2,1,0:T(8,128)}, f32[4,15,16,128]{3,2,1,0:T(8,128)}, f32[2,16,16,128]{3,2,1,0:T(8,128)}, f32[2,16,16,128]{3,2,1,0:T(8,128)},...) custom-call(s32[5]{0:T(128)} %stack.123.place_ref, f32[8,2,16,128]{3,2,1,0:T(8,128)} %bitcast.122, ...), custom_call_target="tpu_custom_call" | custom-call | flops 900000000 | bytes 8000000 | tf_op jit(solution)/shard_map/pallas_call | solution.py:162
  125.5 2.7 %collective-permute-start.33 = (f32[2,16,16,128]{3,2,1,0:T(8,128)}, f32[2,16,16,128]{3,2,1,0:T(8,128)S(1)}, u32[]{:S(2)}, u32[]{:S(2)}) collective-permute-start(f32[2,16,16,128]{3,2,1,0:T(8,128)} %get-tuple-element.32), channel_id=1, source_target_pairs={{0,64},{32,96},{64,0},{96,32},{1,65},{33,97},{65,1},{97,33},{2,66}... | collective-permute-start | bytes 786440 | tf_op jit(solution)/shard_map/ppermute | solution.py:23
  128.2 1.5 collective-permute-start.34
  129.7 3.0 %collective-permute-start.28 = (f32[4,15,16,128]{3,2,1,0:T(8,128)}, f32[4,15,16,128]{3,2,1,0:T(8,128)S(1)}, u32[]{:S(2)}, u32[]{:S(2)}) collective-permute-start(f32[4,15,16,128]{3,2,1,0:T(8,128)} %get-tuple-element.29), channel_id=1, source_target_pairs={{0,16},{16,0},{1,17},{17,1},{2,18},{18,2},{3,19},{19,3},{4,20},{20... | collective-permute-start | bytes 1474568 | tf_op jit(solution)/shard_map/ppermute | solution.py:23
  133.3 3.7 %all-to-all-start.2 = ((f32[16,136,128]{2,1,0:T(8,128)}), f32[16,136,128]{2,1,0:T(8,128)S(1)}, u32[]{:S(2)}, u32[]{:S(2)}) async-start(f32[16,136,128]{2,1,0:T(8,128)} %pad_maximum_fusion), calls=%async_computation.2 | async-start | bytes 2228224 | tf_op jit(solution)/shard_map/all_to_all | solution.py:261
  137.0 1.1 collective-permute-done.33
  138.2 3.0 %collective-permute-start.35 = (f32[16,16,128]{2,1,0:T(8,128)S(1)}, f32[16,16,128]{2,1,0:T(8,128)S(1)}, u32[]{:S(2)}, u32[]{:S(2)}) collective-permute-start(f32[16,16,128]{2,1,0:T(8,128)S(1)} %slice_bitcast_fusion), channel_id=1, source_target_pairs={{0,16},{16,0},{1,17},{17,1},{2,18},{18,2},{3,19},{19,3},{4,20},{20... | collective-permute-start | bytes 393224 | tf_op jit(solution)/shard_map/ppermute | solution.py:23
  141.3 2.7 %collective-permute-done.28 = f32[4,15,16,128]{3,2,1,0:T(8,128)S(1)} collective-permute-done((f32[4,15,16,128]{3,2,1,0:T(8,128)}, f32[4,15,16,128]{3,2,1,0:T(8,128)S(1)}, u32[]{:S(2)}, u32[]{:S(2)}) %collective-permute-start.28) | collective-permute-done | bytes 491552 | tf_op jit(solution)/shard_map/ppermute | solution.py:23
  144.2 3.2 %collective-permute-start.31 = (f32[15,16,128]{2,1,0:T(8,128)S(1)}, f32[15,16,128]{2,1,0:T(8,128)S(1)}, u32[]{:S(2)}, u32[]{:S(2)}) collective-permute-start(f32[15,16,128]{2,1,0:T(8,128)S(1)} %get-tuple-element.47), channel_id=1, source_target_pairs={{0,96},{32,0},{64,32},{96,64},{1,97},{33,1},{65,33},{97,65},{2,98}... | collective-permute-start | bytes 368648 | tf_op jit(solution)/shard_map/ppermute | solution.py:23
  147.4 9.1 %collective-permute-done.35 = f32[16,16,128]{2,1,0:T(8,128)S(1)} collective-permute-done((f32[16,16,128]{2,1,0:T(8,128)S(1)}, f32[16,16,128]{2,1,0:T(8,128)S(1)}, u32[]{:S(2)}, u32[]{:S(2)}) %collective-permute-start.35) | collective-permute-done | bytes 131104 | tf_op jit(solution)/shard_map/ppermute | solution.py:23
  157.6 2.1 %shard_map.63 = f32[33,16,128]{2,1,0:T(8,128)} custom-call(s32[128]{0:T(128)} %convert_element_type.55.slot_ref, f32[16,136,128]{2,1,0:T(8,128)} %copy-done.2), custom_call_target="tpu_custom_call" | custom-call | flops 100000000 | bytes 2000000 | tf_op jit(solution)/shard_map/pallas_call | solution.py:265
  159.7 1.0 fusion
  160.7 1.0 copy.58
  (104 shorter events, 18.6 us)
Async XLA Ops:
  5.0 11.0 %collective-permute-start = (f32[2,128,128]{2,1,0:T(8,128)S(1)}, f32[2,128,128]{2,1,0:T(8,128)S(1)}, u32[]{:S(2)}, u32[]{:S(2)}) collective-permute-start(f32[2,128,128]{2,1,0:T(8,128)S(1)} %pad_maximum_fusion.7), channel_id=1, source_target_pairs={{0,16},{16,0},{1,17},{17,1},{2,18},{18,2},{3,19},{19,3},{4,20},{20... | collective-permute-start | bytes 393224 | tf_op jit(solution)/shard_map/ppermute | solution.py:198
  11.1 14.5 %all-to-all-start = ((f32[8,72,128]{2,1,0:T(8,128)}), f32[8,72,128]{2,1,0:T(8,128)S(1)}, u32[]{:S(2)}, u32[]{:S(2)}) async-start(f32[8,72,128]{2,1,0:T(8,128)} %pad_maximum_fusion.4), calls=%async_computation | async-start | bytes 589824 | tf_op jit(solution)/shard_map/all_to_all | solution.py:201
  16.1 10.3 %collective-permute-start.9 = (f32[128,128]{1,0:T(8,128)S(1)}, f32[128,128]{1,0:T(8,128)S(1)}, u32[]{:S(2)}, u32[]{:S(2)}) collective-permute-start(f32[128,128]{1,0:T(8,128)S(1)} %get-tuple-element.63), channel_id=1, source_target_pairs={{0,6},{2,0},{4,2},{6,4},{1,7},{3,1},{5,3},{7,5},{8,14},{10,8},{12,... | collective-permute-start | bytes 196616 | tf_op jit(solution)/shard_map/ppermute | solution.py:23
  20.2 7.2 %collective-permute-start.8 = (f32[128,128]{1,0:T(8,128)S(1)}, f32[128,128]{1,0:T(8,128)S(1)}, u32[]{:S(2)}, u32[]{:S(2)}) collective-permute-start(f32[128,128]{1,0:T(8,128)S(1)} %get-tuple-element.63), channel_id=1, source_target_pairs={{0,4},{2,6},{4,0},{6,2},{1,5},{3,7},{5,1},{7,3},{8,12},{10,14},{12... | collective-permute-start | bytes 196616 | tf_op jit(solution)/shard_map/ppermute | solution.py:23
  20.2 8.5 %collective-permute-start.7 = (f32[128,128]{1,0:T(8,128)S(1)}, f32[128,128]{1,0:T(8,128)S(1)}, u32[]{:S(2)}, u32[]{:S(2)}) collective-permute-start(f32[128,128]{1,0:T(8,128)S(1)} %get-tuple-element.63), channel_id=1, source_target_pairs={{0,2},{2,4},{4,6},{6,0},{1,3},{3,5},{5,7},{7,1},{8,10},{10,12},{12... | collective-permute-start | bytes 196616 | tf_op jit(solution)/shard_map/ppermute | solution.py:23
  21.4 11.9 %collective-permute-start.3 = (f32[128,128]{1,0:T(8,128)S(1)}, f32[128,128]{1,0:T(8,128)S(1)}, u32[]{:S(2)}, u32[]{:S(2)}) collective-permute-start(f32[128,128]{1,0:T(8,128)S(1)} %get-tuple-element.60), channel_id=1, source_target_pairs={{0,96},{32,0},{64,32},{96,64},{1,97},{33,1},{65,33},{97,65},{2,98}... | collective-permute-start | bytes 196616 | tf_op jit(solution)/shard_map/ppermute | solution.py:23
  24.7 10.2 %collective-permute-start.2 = (f32[128,128]{1,0:T(8,128)S(1)}, f32[128,128]{1,0:T(8,128)S(1)}, u32[]{:S(2)}, u32[]{:S(2)}) collective-permute-start(f32[128,128]{1,0:T(8,128)S(1)} %get-tuple-element.60), channel_id=1, source_target_pairs={{0,64},{32,96},{64,0},{96,32},{1,65},{33,97},{65,1},{97,33},{2,66}... | collective-permute-start | bytes 196616 | tf_op jit(solution)/shard_map/ppermute | solution.py:23
  26.4 8.7 %collective-permute-start.1 = (f32[128,128]{1,0:T(8,128)S(1)}, f32[128,128]{1,0:T(8,128)S(1)}, u32[]{:S(2)}, u32[]{:S(2)}) collective-permute-start(f32[128,128]{1,0:T(8,128)S(1)} %get-tuple-element.60), channel_id=1, source_target_pairs={{0,32},{32,64},{64,96},{96,0},{1,33},{33,65},{65,97},{97,1},{2,34}... | collective-permute-start | bytes 196616 | tf_op jit(solution)/shard_map/ppermute | solution.py:23
  27.3 4.3 %collective-permute-start.13 = (f32[8,16,128]{2,1,0:T(8,128)S(1)}, f32[8,16,128]{2,1,0:T(8,128)S(1)}, u32[]{:S(2)}, u32[]{:S(2)}) collective-permute-start(f32[8,16,128]{2,1,0:T(8,128)S(1)} %get-tuple-element.44), channel_id=1, source_target_pairs={{0,8},{8,0},{1,9},{9,1},{2,10},{10,2},{3,11},{11,3},{4,12},{12,4},... | collective-permute-start | bytes 196616 | tf_op jit(solution)/shard_map/ppermute | solution.py:23
  28.7 20.7 %collective-permute-start.11 = (f32[4,128,128]{2,1,0:T(8,128)S(1)}, f32[4,128,128]{2,1,0:T(8,128)S(1)}, u32[]{:S(2)}, u32[]{:S(2)}) collective-permute-start(f32[4,128,128]{2,1,0:T(8,128)S(1)} %get-tuple-element.54), channel_id=1, source_target_pairs={{0,64},{32,96},{64,0},{96,32},{1,65},{33,97},{65,1},{97,33},{2,66}... | collective-permute-start | bytes 786440 | tf_op jit(solution)/shard_map/ppermute | solution.py:23
  31.6 21.7 %collective-permute-start.10 = (f32[4,128,128]{2,1,0:T(8,128)S(1)}, f32[4,128,128]{2,1,0:T(8,128)S(1)}, u32[]{:S(2)}, u32[]{:S(2)}) collective-permute-start(f32[4,128,128]{2,1,0:T(8,128)S(1)} %get-tuple-element.54), channel_id=1, source_target_pairs={{0,32},{32,64},{64,96},{96,0},{1,33},{33,65},{65,97},{97,1},{2,34}... | collective-permute-start | bytes 786440 | tf_op jit(solution)/shard_map/ppermute | solution.py:23
  33.4 19.9 %collective-permute-start.12 = (f32[4,128,128]{2,1,0:T(8,128)S(1)}, f32[4,128,128]{2,1,0:T(8,128)S(1)}, u32[]{:S(2)}, u32[]{:S(2)}) collective-permute-start(f32[4,128,128]{2,1,0:T(8,128)S(1)} %get-tuple-element.54), channel_id=1, source_target_pairs={{0,96},{32,0},{64,32},{96,64},{1,97},{33,1},{65,33},{97,65},{2,98}... | collective-permute-start | bytes 786440 | tf_op jit(solution)/shard_map/ppermute | solution.py:23
  34.9 1.3 collective-permute-start.14
  36.2 5.4 %collective-permute-start.17 = (f32[8,16,128]{2,1,0:T(8,128)S(1)}, f32[8,16,128]{2,1,0:T(8,128)S(1)}, u32[]{:S(2)}, u32[]{:S(2)}) collective-permute-start(f32[8,16,128]{2,1,0:T(8,128)S(1)} %add.96), channel_id=1, source_target_pairs={{0,6},{2,0},{4,2},{6,4},{1,7},{3,1},{5,3},{7,5},{8,14},{10,8},{12,... | collective-permute-start | bytes 196616 | tf_op jit(solution)/shard_map/ppermute | solution.py:23
  38.4 5.8 %collective-permute-start.16 = (f32[8,16,128]{2,1,0:T(8,128)S(1)}, f32[8,16,128]{2,1,0:T(8,128)S(1)}, u32[]{:S(2)}, u32[]{:S(2)}) collective-permute-start(f32[8,16,128]{2,1,0:T(8,128)S(1)} %add.96), channel_id=1, source_target_pairs={{0,4},{2,6},{4,0},{6,2},{1,5},{3,7},{5,1},{7,3},{8,12},{10,14},{12... | collective-permute-start | bytes 196616 | tf_op jit(solution)/shard_map/ppermute | solution.py:23
  41.6 7.8 %collective-permute-start.15 = (f32[8,16,128]{2,1,0:T(8,128)S(1)}, f32[8,16,128]{2,1,0:T(8,128)S(1)}, u32[]{:S(2)}, u32[]{:S(2)}) collective-permute-start(f32[8,16,128]{2,1,0:T(8,128)S(1)} %add.96), channel_id=1, source_target_pairs={{0,2},{2,4},{4,6},{6,0},{1,3},{3,5},{5,7},{7,1},{8,10},{10,12},{12... | collective-permute-start | bytes 196616 | tf_op jit(solution)/shard_map/ppermute | solution.py:23
  44.3 11.0 %collective-permute-start.5 = (f32[4,128,128]{2,1,0:T(8,128)S(1)}, f32[4,128,128]{2,1,0:T(8,128)S(1)}, u32[]{:S(2)}, u32[]{:S(2)}) collective-permute-start(f32[4,128,128]{2,1,0:T(8,128)S(1)} %get-tuple-element.58), channel_id=1, source_target_pairs={{0,4},{2,6},{4,0},{6,2},{1,5},{3,7},{5,1},{7,3},{8,12},{10,14},{12... | collective-permute-start | bytes 786440 | tf_op jit(solution)/shard_map/ppermute | solution.py:23
  49.4 9.4 %collective-permute-start.4 = (f32[4,128,128]{2,1,0:T(8,128)S(1)}, f32[4,128,128]{2,1,0:T(8,128)S(1)}, u32[]{:S(2)}, u32[]{:S(2)}) collective-permute-start(f32[4,128,128]{2,1,0:T(8,128)S(1)} %get-tuple-element.58), channel_id=1, source_target_pairs={{0,2},{2,4},{4,6},{6,0},{1,3},{3,5},{5,7},{7,1},{8,10},{10,12},{12... | collective-permute-start | bytes 786440 | tf_op jit(solution)/shard_map/ppermute | solution.py:23
  49.4 9.4 %collective-permute-start.6 = (f32[4,128,128]{2,1,0:T(8,128)S(1)}, f32[4,128,128]{2,1,0:T(8,128)S(1)}, u32[]{:S(2)}, u32[]{:S(2)}) collective-permute-start(f32[4,128,128]{2,1,0:T(8,128)S(1)} %get-tuple-element.58), channel_id=1, source_target_pairs={{0,6},{2,0},{4,2},{6,4},{1,7},{3,1},{5,3},{7,5},{8,14},{10,8},{12,... | collective-permute-start | bytes 786440 | tf_op jit(solution)/shard_map/ppermute | solution.py:23
  53.4 21.9 %copy-start = (f32[4,4,128,128]{3,2,1,0:T(8,128)}, f32[4,4,128,128]{3,2,1,0:T(8,128)S(1)}, u32[]{:S(2)}) copy-start(f32[4,4,128,128]{3,2,1,0:T(8,128)S(1)} %pad_maximum_fusion.2.o0_ref) | copy-start | bytes 3145732
  58.8 17.5 %copy-start.1 = (f32[4,4,128,128]{3,2,1,0:T(8,128)}, f32[4,4,128,128]{3,2,1,0:T(8,128)S(1)}, u32[]{:S(2)}) copy-start(f32[4,4,128,128]{3,2,1,0:T(8,128)S(1)} %pad_maximum_fusion.1.e0_ref) | copy-start | bytes 3145732
  58.9 17.5 %collective-permute-start.19 = (f32[4,4,128,128]{3,2,1,0:T(8,128)S(1)}, f32[4,4,128,128]{3,2,1,0:T(8,128)S(1)}, u32[]{:S(2)}, u32[]{:S(2)}) collective-permute-start(f32[4,4,128,128]{3,2,1,0:T(8,128)S(1)} %pad_maximum_fusion.2.o0_ref), channel_id=1, source_target_pairs={{0,1},{1,0},{2,3},{3,2},{4,5},{5,4},{6,7},{7,6},{8,9},{9,8},{10,11... | collective-permute-start | bytes 3145736 | tf_op jit(solution)/shard_map/ppermute | solution.py:23
  59.0 17.4 %collective-permute-start.18 = (f32[4,4,128,128]{3,2,1,0:T(8,128)S(1)}, f32[4,4,128,128]{3,2,1,0:T(8,128)}, u32[]{:S(2)}, u32[]{:S(2)}) collective-permute-start(f32[4,4,128,128]{3,2,1,0:T(8,128)S(1)} %pad_maximum_fusion.1.e0_ref), channel_id=1, source_target_pairs={{0,1},{1,0},{2,3},{3,2},{4,5},{5,4},{6,7},{7,6},{8,9},{9,8},{10,11... | collective-permute-start | bytes 3145736 | tf_op jit(solution)/shard_map/ppermute | solution.py:23
  71.7 12.6 %collective-permute-start.23 = (f32[2,128,128]{2,1,0:T(8,128)S(1)}, f32[2,128,128]{2,1,0:T(8,128)S(1)}, u32[]{:S(2)}, u32[]{:S(2)}) collective-permute-start(f32[2,128,128]{2,1,0:T(8,128)S(1)} %pad_maximum_fusion.8), channel_id=1, source_target_pairs={{0,96},{32,0},{64,32},{96,64},{1,97},{33,1},{65,33},{97,65},{2,98}... | collective-permute-start | bytes 393224 | tf_op jit(solution)/shard_map/ppermute | solution.py:23
  73.3 11.1 %collective-permute-start.22 = (f32[2,128,128]{2,1,0:T(8,128)S(1)}, f32[2,128,128]{2,1,0:T(8,128)}, u32[]{:S(2)}, u32[]{:S(2)}) collective-permute-start(f32[2,128,128]{2,1,0:T(8,128)S(1)} %pad_maximum_fusion.8), channel_id=1, source_target_pairs={{0,64},{32,96},{64,0},{96,32},{1,65},{33,97},{65,1},{97,33},{2,66}... | collective-permute-start | bytes 393224 | tf_op jit(solution)/shard_map/ppermute | solution.py:23
  74.3 10.1 %collective-permute-start.21 = (f32[2,128,128]{2,1,0:T(8,128)S(1)}, f32[2,128,128]{2,1,0:T(8,128)}, u32[]{:S(2)}, u32[]{:S(2)}) collective-permute-start(f32[2,128,128]{2,1,0:T(8,128)S(1)} %pad_maximum_fusion.8), channel_id=1, source_target_pairs={{0,32},{32,64},{64,96},{96,0},{1,33},{33,65},{65,97},{97,1},{2,34}... | collective-permute-start | bytes 393224 | tf_op jit(solution)/shard_map/ppermute | solution.py:23
  76.4 1.0 copy-start.3
  81.3 5.3 %collective-permute-start.20 = (f32[8,16,128]{2,1,0:T(8,128)}, f32[8,16,128]{2,1,0:T(8,128)S(1)}, u32[]{:S(2)}, u32[]{:S(2)}) collective-permute-start(f32[8,16,128]{2,1,0:T(8,128)} %shard_map.59.first_ref), channel_id=1, source_target_pairs={{0,8},{1,9},{2,10},{3,11},{4,12},{5,13},{6,14},{7,15},{16,24},{17,... | collective-permute-start | bytes 196616 | tf_op jit(solution)/shard_map/ppermute | solution.py:237
  86.6 0.6 copy-start.8
  89.1 1.4 collective-permute-start.24
  91.2 3.7 %collective-permute-start.27 = (f32[2,16,128]{2,1,0:T(8,128)S(1)}, f32[2,16,128]{2,1,0:T(8,128)S(1)}, u32[]{:S(2)}, u32[]{:S(2)}) collective-permute-start(f32[2,16,128]{2,1,0:T(8,128)S(1)} %pad_maximum_fusion.10), channel_id=1, source_target_pairs={{0,6},{2,0},{4,2},{6,4},{1,7},{3,1},{5,3},{7,5},{8,14},{10,8},{12,... | collective-permute-start | bytes 49160 | tf_op jit(solution)/shard_map/ppermute | solution.py:23
  92.5 5.4 %collective-permute-start.26 = (f32[2,16,128]{2,1,0:T(8,128)S(1)}, f32[2,16,128]{2,1,0:T(8,128)S(1)}, u32[]{:S(2)}, u32[]{:S(2)}) collective-permute-start(f32[2,16,128]{2,1,0:T(8,128)S(1)} %pad_maximum_fusion.10), channel_id=1, source_target_pairs={{0,4},{2,6},{4,0},{6,2},{1,5},{3,7},{5,1},{7,3},{8,12},{10,14},{12... | collective-permute-start | bytes 49160 | tf_op jit(solution)/shard_map/ppermute | solution.py:23
  93.7 4.9 %collective-permute-start.25 = (f32[2,16,128]{2,1,0:T(8,128)S(1)}, f32[2,16,128]{2,1,0:T(8,128)S(1)}, u32[]{:S(2)}, u32[]{:S(2)}) collective-permute-start(f32[2,16,128]{2,1,0:T(8,128)S(1)} %pad_maximum_fusion.10), channel_id=1, source_target_pairs={{0,2},{2,4},{4,6},{6,0},{1,3},{3,5},{5,7},{7,1},{8,10},{10,12},{12... | collective-permute-start | bytes 49160 | tf_op jit(solution)/shard_map/ppermute | solution.py:23
  103.4 16.6 %all-to-all-start.1 = ((f32[16,16,128]{2,1,0:T(8,128)}), f32[16,16,128]{2,1,0:T(8,128)S(1)}, u32[]{:S(2)}, u32[]{:S(2)}) async-start(f32[16,16,128]{2,1,0:T(8,128)} %bitcast.119), calls=%async_computation.1 | async-start | bytes 262144 | tf_op jit(solution)/shard_map/all_to_all | solution.py:252
  119.9 0.6 copy-start.5
  120.6 9.1 %copy-start.4 = (f32[8,2,16,128]{3,2,1,0:T(8,128)S(1)}, f32[8,2,16,128]{3,2,1,0:T(8,128)}, u32[]{:S(2)}) copy-start(f32[8,2,16,128]{3,2,1,0:T(8,128)} %shard_map.61) | copy-start | bytes 393220
  124.8 13.3 %copy-start.7 = (f32[2,16,16,128]{3,2,1,0:T(8,128)S(1)}, f32[2,16,16,128]{3,2,1,0:T(8,128)}, u32[]{:S(2)}) copy-start(f32[2,16,16,128]{3,2,1,0:T(8,128)} %get-tuple-element.30) | copy-start | bytes 786436
  124.8 19.2 %copy-start.6 = (f32[4,15,16,128]{3,2,1,0:T(8,128)S(1)}, f32[4,15,16,128]{3,2,1,0:T(8,128)}, u32[]{:S(2)}) copy-start(f32[4,15,16,128]{3,2,1,0:T(8,128)} %get-tuple-element.28) | copy-start | bytes 1474564
  124.8 12.2 %collective-permute-start.32 = (f32[2,16,16,128]{3,2,1,0:T(8,128)}, f32[2,16,16,128]{3,2,1,0:T(8,128)S(1)}, u32[]{:S(2)}, u32[]{:S(2)}) collective-permute-start(f32[2,16,16,128]{3,2,1,0:T(8,128)} %get-tuple-element.31), channel_id=1, source_target_pairs={{0,32},{32,64},{64,96},{96,0},{1,33},{33,65},{65,97},{97,1},{2,34}... | collective-permute-start | bytes 786440 | tf_op jit(solution)/shard_map/ppermute | solution.py:23
  125.5 12.6 %collective-permute-start.33 = (f32[2,16,16,128]{3,2,1,0:T(8,128)}, f32[2,16,16,128]{3,2,1,0:T(8,128)S(1)}, u32[]{:S(2)}, u32[]{:S(2)}) collective-permute-start(f32[2,16,16,128]{3,2,1,0:T(8,128)} %get-tuple-element.32), channel_id=1, source_target_pairs={{0,64},{32,96},{64,0},{96,32},{1,65},{33,97},{65,1},{97,33},{2,66}... | collective-permute-start | bytes 786440 | tf_op jit(solution)/shard_map/ppermute | solution.py:23
  128.2 9.9 %collective-permute-start.34 = (f32[2,16,16,128]{3,2,1,0:T(8,128)}, f32[2,16,16,128]{3,2,1,0:T(8,128)S(1)}, u32[]{:S(2)}, u32[]{:S(2)}) collective-permute-start(f32[2,16,16,128]{3,2,1,0:T(8,128)} %get-tuple-element.33), channel_id=1, source_target_pairs={{0,96},{32,0},{64,32},{96,64},{1,97},{33,1},{65,33},{97,65},{2,98}... | collective-permute-start | bytes 786440 | tf_op jit(solution)/shard_map/ppermute | solution.py:23
  129.7 14.3 %collective-permute-start.28 = (f32[4,15,16,128]{3,2,1,0:T(8,128)}, f32[4,15,16,128]{3,2,1,0:T(8,128)S(1)}, u32[]{:S(2)}, u32[]{:S(2)}) collective-permute-start(f32[4,15,16,128]{3,2,1,0:T(8,128)} %get-tuple-element.29), channel_id=1, source_target_pairs={{0,16},{16,0},{1,17},{17,1},{2,18},{18,2},{3,19},{19,3},{4,20},{20... | collective-permute-start | bytes 1474568 | tf_op jit(solution)/shard_map/ppermute | solution.py:23
  133.3 23.2 %all-to-all-start.2 = ((f32[16,136,128]{2,1,0:T(8,128)}), f32[16,136,128]{2,1,0:T(8,128)S(1)}, u32[]{:S(2)}, u32[]{:S(2)}) async-start(f32[16,136,128]{2,1,0:T(8,128)} %pad_maximum_fusion), calls=%async_computation.2 | async-start | bytes 2228224 | tf_op jit(solution)/shard_map/all_to_all | solution.py:261
  138.2 18.2 %collective-permute-start.35 = (f32[16,16,128]{2,1,0:T(8,128)S(1)}, f32[16,16,128]{2,1,0:T(8,128)S(1)}, u32[]{:S(2)}, u32[]{:S(2)}) collective-permute-start(f32[16,16,128]{2,1,0:T(8,128)S(1)} %slice_bitcast_fusion), channel_id=1, source_target_pairs={{0,16},{16,0},{1,17},{17,1},{2,18},{18,2},{3,19},{19,3},{4,20},{20... | collective-permute-start | bytes 393224 | tf_op jit(solution)/shard_map/ppermute | solution.py:23
  144.1 12.4 %collective-permute-start.30 = (f32[15,16,128]{2,1,0:T(8,128)S(1)}, f32[15,16,128]{2,1,0:T(8,128)S(1)}, u32[]{:S(2)}, u32[]{:S(2)}) collective-permute-start(f32[15,16,128]{2,1,0:T(8,128)S(1)} %get-tuple-element.46), channel_id=1, source_target_pairs={{0,64},{32,96},{64,0},{96,32},{1,65},{33,97},{65,1},{97,33},{2,66}... | collective-permute-start | bytes 368648 | tf_op jit(solution)/shard_map/ppermute | solution.py:23
  144.2 12.3 %collective-permute-start.31 = (f32[15,16,128]{2,1,0:T(8,128)S(1)}, f32[15,16,128]{2,1,0:T(8,128)S(1)}, u32[]{:S(2)}, u32[]{:S(2)}) collective-permute-start(f32[15,16,128]{2,1,0:T(8,128)S(1)} %get-tuple-element.47), channel_id=1, source_target_pairs={{0,96},{32,0},{64,32},{96,64},{1,97},{33,1},{65,33},{97,65},{2,98}... | collective-permute-start | bytes 368648 | tf_op jit(solution)/shard_map/ppermute | solution.py:23
  147.4 9.1 %collective-permute-start.29 = (f32[15,16,128]{2,1,0:T(8,128)S(1)}, f32[15,16,128]{2,1,0:T(8,128)S(1)}, u32[]{:S(2)}, u32[]{:S(2)}) collective-permute-start(f32[15,16,128]{2,1,0:T(8,128)S(1)} %get-tuple-element.48), channel_id=1, source_target_pairs={{0,32},{32,64},{64,96},{96,0},{1,33},{33,65},{65,97},{97,1},{2,34}... | collective-permute-start | bytes 368648 | tf_op jit(solution)/shard_map/ppermute | solution.py:23
  156.6 1.0 copy-start.2

commit v6 on v5

--- a/solution.py
+++ b/solution.py
@@ -14,6 +14,7 @@
 PLANE = ("z", "core")
 BLOCK = 128
 HALF = 8
+GRANT = 24 * 2**20
 VMEM = pl.BlockSpec(memory_space=pltpu.VMEM)
 SMEM = pl.BlockSpec(memory_space=pltpu.SMEM)
 
@@ -93,7 +94,8 @@
 
 
 def update_kernel(
-    place_ref, rows_ref, factor_ref, a_keep, a_send, b_keep, b_one, b_two, b_three, left_high, left_low
+    place_ref, rows_ref, factor_ref,
+    a_keep, a_send, b_keep, b_one, b_two, b_three, left_high, left_low,
 ):
     step = pl.program_id(0)
     count = factor_ref.shape[1]
@@ -135,6 +137,20 @@
     pl.when(step == 1)(lambda: fill(fill_b))
 
 
+def pack_kernel(goal_ref, received_ref, out_ref):
+    cols, share = out_ref.shape[0], 16
+    sources = goal_ref.shape[0] // 8
+    out_ref[:, :BLOCK] = jnp.zeros((cols, BLOCK, BLOCK), jnp.float32)
+    out_ref[:, BLOCK:] = jnp.full((cols, 8, BLOCK), -1.0, jnp.float32)
+    for r in range(8):
+        for u in range(sources):
+            goal = goal_ref[r * sources + u]
+            col = lax.rem(goal, cols)
+            slot = lax.div(goal, cols).astype(jnp.float32)
+            out_ref[col, r * share : (r + 1) * share] = received_ref[r, u * share : (u + 1) * share]
+            out_ref[col, BLOCK + r : BLOCK + r + 1] = jnp.full((1, BLOCK), slot, jnp.float32)
+
+
 def place_kernel(slot_ref, arrived_ref, out_ref):
     spare = out_ref.shape[0] - 1
     share = out_ref.shape[1]
@@ -150,6 +166,7 @@
         out_shape=jax.ShapeDtypeStruct(shape, jnp.float32),
         in_specs=[SMEM] + [VMEM] * (len(args) - 1),
         out_specs=VMEM,
+        compiler_params=pltpu.CompilerParams(vmem_limit_bytes=GRANT),
         cost_estimate=pl.CostEstimate(flops=600_000_000, bytes_accessed=5_000_000, transcendentals=0),
     )(*args)
 
@@ -166,6 +183,7 @@
         in_specs=[SMEM, VMEM, spec],
         out_specs=(VMEM,) * 6,
         scratch_shapes=[pltpu.VMEM((BLOCK, 2 * BLOCK), jnp.bfloat16)] * 2,
+        compiler_params=pltpu.CompilerParams(vmem_limit_bytes=GRANT),
         cost_estimate=pl.CostEstimate(flops=900_000_000, bytes_accessed=8_000_000, transcendentals=0),
     )(place, own_rows, factor)
 
@@ -189,7 +207,7 @@
 
     inverse = diag_inverse.reshape(BLOCK, BLOCK)
     upper = panel_row.reshape(2, BLOCK, slots, BLOCK)
-    panel = upper[:, :, 0, :]
+    panel = lax.optimization_barrier(upper[:, :, 0, :])
     scaled = jnp.einsum("tpf,ef->tpe", panel, inverse, precision=HIGHEST)
     mine = jnp.where(my_yl == 0, scaled[0], scaled[1])
     mine = jnp.where(my_row == my_plane, inverse, mine)
@@ -203,7 +221,9 @@
     by_z = around(odd[0], "z")
     even = jnp.stack(around(even[0], "x"))
     even = jnp.stack(around(even, "z"))
-    odd = jnp.stack(around(jnp.stack(by_z), "x"))
+    by_x = around(jnp.concatenate([jnp.stack(by_z), column]), "x")
+    odd = jnp.stack([p[:4] for p in by_x])
+    coupling = jnp.stack([p[4:] for p in by_x])
 
     data = received[:, : sources * share].reshape(rows, sources, share, BLOCK)
     label = received[:, sources * share : sources * share + sources, None, :]
@@ -219,18 +239,12 @@
     start = sum(around(start, "z"))
 
     goal = received[:, sources * share : sources * share + sources, 0].astype(jnp.int32)
-    chosen = (goal[None] % cols) == jnp.arange(cols, dtype=jnp.int32)[:, None, None]
-    outgoing = jnp.zeros((cols, rows, share, BLOCK), jnp.float32)
-    for u in range(sources):
-        outgoing = jnp.where(chosen[:, :, u, None, None], data[None, :, u], outgoing)
-    slot_label = jnp.max(jnp.where(chosen, goal[None] // cols, -1), axis=2).astype(jnp.float32)
-    slot_label = jnp.broadcast_to(slot_label[:, :, None], (cols, rows, BLOCK))
-    outgoing = jnp.concatenate([outgoing.reshape(cols, BLOCK, BLOCK), slot_label], axis=1)
+    outgoing = local_kernel(
+        pack_kernel, (cols, BLOCK + 8, BLOCK), goal.reshape(rows * sources), received
+    )
 
     even, odd, start = lax.optimization_barrier((even, odd, start))
     factors = (even, rotated(even, "core", 1), odd, rotated(odd, "core", 1))
-    column, even = lax.optimization_barrier((column, even))
-    coupling = jnp.stack(around(column, "x"))
 
     shape = (HALF, share, BLOCK)
     first = local_kernel(first_kernel, shape, place, start, *factors)
@@ -244,9 +258,7 @@
     upper = with_layout_constraint(upper, Layout(major_to_minor=(0, 1, 2, 3)))
     factor = upper.transpose(0, 2, 1, 3)
     residual = jnp.stack(around(residual, "z"))
-    copies = local_kernel(
-        second_kernel, (HALF, 2, share, BLOCK), place, residual, first, *factors
-    )
+    copies = local_kernel(second_kernel, (HALF, 2, share, BLOCK), place, residual, first, *factors)
     panel_solution = lax.dynamic_index_in_dim(copies[:, 0], my_plane, 0, keepdims=False)
 
     own_rows = lax.all_to_all(
@@ -262,13 +274,7 @@
     b_part = b_part[0] + rotated(b_part[1], "yh", 1)
     a_part = a_part[0] + sum(rotated(a_part[step], "x", step) for step in (1, 2, 3))
     slot_of = arrived[:, BLOCK:, 0].astype(jnp.int32).reshape(cols * rows)
-    held = pl.pallas_call(
-        place_kernel,
-        out_shape=jax.ShapeDtypeStruct((slots + 1, share, BLOCK), jnp.float32),
-        in_specs=[SMEM, VMEM],
-        out_specs=VMEM,
-        cost_estimate=pl.CostEstimate(flops=100_000_000, bytes_accessed=2_000_000, transcendentals=0),
-    )(slot_of, arrived)
+    held = local_kernel(place_kernel, (slots + 1, share, BLOCK), slot_of, arrived)
     trailing = held[1:slots] + jnp.concatenate([a_part, b_part], axis=0)
     trailing = trailing.transpose(1, 0, 2)
     return panel_solution[:, None, None, :], trailing[:, :, None, :]
@@ -283,4 +289,6 @@
         P(None, COL, None, None),
     )
     out_specs = (P(ROW, None, COL, None), P(ROW, None, COL, None))
-    return jax.shard_map(per_device, mesh=fine, in_specs=in_specs, out_specs=out_specs, check_vma=False)
+    return jax.shard_map(
+        per_device, mesh=fine, in_specs=in_specs, out_specs=out_specs, check_vma=False
+    )

time: 163 us -> 159 us (0.975)
  waiting for transfers between devices: 31.9 us -> 51.8 us
  starting transfers between devices: 72.9 us -> 63.2 us
  Pallas kernels: 16.3 us -> 10.6 us
  local copies, waits for them, and re-layouts: 26.4 us -> 22 us
  other arithmetic: 11.9 us -> 7.97 us
    ppermute x34 -> x31, waiting for transfers between devices: 30.3 us -> 48.7 us  [rotated(): lax.ppermute(array, axis, [(i, (i + step) % size) for i in range(size)])]
    broadcast_in_dim x14 -> x0, local copies, waits for them, and re-layouts: 10.4 us -> none  [the longest x13 9.64 us: per_device(): jnp.where(chosen[:, :, u, None, None], data[None, :, u], outgoing)]
    ppermute x34 -> x31, starting transfers between devices: 49.8 us -> 43.1 us  [rotated(): lax.ppermute(array, axis, [(i, (i + step) % size) for i in range(size)])]
    unnamed x20 -> x14, local copies, waits for them, and re-layouts: 3.38 us -> 6.52 us
    another operation x0 -> x6, local copies, waits for them, and re-layouts: none -> 2.8 us  [the longest x3 2.74 us: per_device(): coupling = jnp.stack([p[4:] for p in by_x])]
    all_to_all x1, starting transfers between devices: 8.71 us -> 6.15 us  [per_device(): lax.all_to_all(copies.reshape(rows * 2, share, BLOCK), ROW + ('yl',), 0,...]
    pallas_call x1, Pallas kernels: 4.23 us -> 1.94 us  [update(): pl.pallas_call(update_kernel, out_shape=tuple((jax.ShapeDtypeStruct(shape...]
    pallas_call x1 -> x0, Pallas kernels: 2.14 us -> none  [per_device(): pl.pallas_call(place_kernel, out_shape=jax.ShapeDtypeStruct((slots + 1, s...]
  transfers between devices with their start and end apart: 39 -> 36, of which waited for: 17 -> 15; matrix products, arithmetic and copies ran while one was open for 18% -> 14% of each run, Pallas kernels for 2% -> 1%
where the time goes in v6:
time: 159 us; the launch traced here: 158 us
  starting transfers between devices  63.2 us (40%)
  waiting for transfers between devices  51.8 us (33%)
  local copies, waits for them, and re-layouts  22 us (14%)
  Pallas kernels  10.6 us (7%)
  other arithmetic  7.97 us (5%)
    ppermute x31, waiting for transfers between devices, rotated(): lax.ppermute(array, axis, [(i, (i + step) % size) for i in range(size)])  48.7 us
    ppermute x31, starting transfers between devices, rotated(): lax.ppermute(array, axis, [(i, (i + step) % size) for i in range(size)])  43.1 us
    pallas_call x5, Pallas kernels, local_kernel(): pl.pallas_call(kernel, out_shape=jax.ShapeDtypeStruct(shape, jnp.float32)...  8.69 us
    another operation x1, local copies, waits for them, and re-layouts, per_device(): upper = with_layout_constraint(upper, Layout(major_to_minor=(0, 1, 2, 3)))  6.6 us
    unnamed x14, local copies, waits for them, and re-layouts  6.52 us
    all_to_all x1, starting transfers between devices, per_device(): lax.all_to_all(copies.reshape(rows * 2, share, BLOCK), ROW + ('yl',), 0,...  6.15 us
    all_to_all x1, starting transfers between devices, per_device(): received = lax.all_to_all(packed, ROW, 0, 0, tiled=True)  4.3 us
    all_to_all x1, starting transfers between devices, per_device(): arrived = lax.all_to_all(outgoing, COL, 0, 0, tiled=True)  3.7 us
  transfers between devices with their start and end apart: 36, of which 15 were waited for; matrix products, arithmetic and copies ran while one was open for 14% of the time, Pallas kernels for 1%

profile of v6, /device:TPU:0, one launch (start us, length us, event | category | flops | bytes accessed | tf_op | source)
XLA Modules:
  0.0 157.8 jit_solution(13763607466595814442)
XLA Ops:
  0.6 1.3 slice.104
  2.0 1.1 fusion.5
  3.1 0.9 fusion.4
  4.0 3.4 %collective-permute-start = (f32[2,128,128]{2,1,0:T(8,128)S(1)}, f32[2,128,128]{2,1,0:T(8,128)S(1)}, u32[]{:S(2)}, u32[]{:S(2)}) collective-permute-start(f32[2,128,128]{2,1,0:T(8,128)S(1)} %pad_maximum_fusion.5), channel_id=1, source_target_pairs={{0,16},{16,0},{1,17},{17,1},{2,18},{18,2},{3,19},{19,3},{4,20},{20... | collective-permute-start | bytes 393224 | tf_op jit(solution)/shard_map/ppermute | solution.py:216
  7.4 0.8 add_convert_fusion
  8.2 1.0 copy.12
  9.2 0.8 pad_maximum_fusion.3
  10.0 4.3 %all-to-all-start = ((f32[8,72,128]{2,1,0:T(8,128)}), f32[8,72,128]{2,1,0:T(8,128)S(1)}, u32[]{:S(2)}, u32[]{:S(2)}) async-start(f32[8,72,128]{2,1,0:T(8,128)} %pad_maximum_fusion.3), calls=%async_computation | async-start | bytes 589824 | tf_op jit(solution)/shard_map/all_to_all | solution.py:219
  15.0 1.9 %collective-permute-start.7 = (f32[128,128]{1,0:T(8,128)S(1)}, f32[128,128]{1,0:T(8,128)S(1)}, u32[]{:S(2)}, u32[]{:S(2)}) collective-permute-start(f32[128,128]{1,0:T(8,128)S(1)} %get-tuple-element.52), channel_id=1, source_target_pairs={{0,2},{2,4},{4,6},{6,0},{1,3},{3,5},{5,7},{7,1},{8,10},{10,12},{12... | collective-permute-start | bytes 196616 | tf_op jit(solution)/shard_map/ppermute | solution.py:24
  16.9 2.2 %collective-permute-start.9 = (f32[128,128]{1,0:T(8,128)S(1)}, f32[128,128]{1,0:T(8,128)S(1)}, u32[]{:S(2)}, u32[]{:S(2)}) collective-permute-start(f32[128,128]{1,0:T(8,128)S(1)} %get-tuple-element.52), channel_id=1, source_target_pairs={{0,6},{2,0},{4,2},{6,4},{1,7},{3,1},{5,3},{7,5},{8,14},{10,8},{12,... | collective-permute-start | bytes 196616 | tf_op jit(solution)/shard_map/ppermute | solution.py:24
  19.1 1.8 %collective-permute-start.8 = (f32[128,128]{1,0:T(8,128)S(1)}, f32[128,128]{1,0:T(8,128)S(1)}, u32[]{:S(2)}, u32[]{:S(2)}) collective-permute-start(f32[128,128]{1,0:T(8,128)S(1)} %get-tuple-element.52), channel_id=1, source_target_pairs={{0,4},{2,6},{4,0},{6,2},{1,5},{3,7},{5,1},{7,3},{8,12},{10,14},{12... | collective-permute-start | bytes 196616 | tf_op jit(solution)/shard_map/ppermute | solution.py:24
  21.9 3.0 %collective-permute-done.8 = f32[128,128]{1,0:T(8,128)S(1)} collective-permute-done((f32[128,128]{1,0:T(8,128)S(1)}, f32[128,128]{1,0:T(8,128)S(1)}, u32[]{:S(2)}, u32[]{:S(2)}) %collective-permute-start.8) | collective-permute-done | bytes 65568 | tf_op jit(solution)/shard_map/ppermute | solution.py:24
  26.9 1.4 collective-permute-start.13
  28.4 0.7 fusion.9
  29.0 3.2 %collective-permute-start.3 = (f32[128,128]{1,0:T(8,128)S(1)}, f32[128,128]{1,0:T(8,128)S(1)}, u32[]{:S(2)}, u32[]{:S(2)}) collective-permute-start(f32[128,128]{1,0:T(8,128)S(1)} %get-tuple-element.48), channel_id=1, source_target_pairs={{0,96},{32,0},{64,32},{96,64},{1,97},{33,1},{65,33},{97,65},{2,98}... | collective-permute-start | bytes 196616 | tf_op jit(solution)/shard_map/ppermute | solution.py:24
  32.3 0.9 collective-permute-start.2
  33.1 0.9 collective-permute-start.1
  34.7 2.4 %collective-permute-start.12 = (f32[6,128,128]{2,1,0:T(8,128)}, f32[6,128,128]{2,1,0:T(8,128)S(1)}, u32[]{:S(2)}, u32[]{:S(2)}) collective-permute-start(f32[6,128,128]{2,1,0:T(8,128)} %constant_dynamic-update-slice_fusion), channel_id=1, source_target_pairs={{0,96},{32,0},{64,32},{96,64},{1,97},{33,1},{65,33},{97,65},{2,98}... | collective-permute-start | bytes 1179656 | tf_op jit(solution)/shard_map/ppermute | solution.py:24
  37.1 2.0 %collective-permute-start.17 = (f32[8,16,128]{2,1,0:T(8,128)S(1)}, f32[8,16,128]{2,1,0:T(8,128)S(1)}, u32[]{:S(2)}, u32[]{:S(2)}) collective-permute-start(f32[8,16,128]{2,1,0:T(8,128)S(1)} %add.79), channel_id=1, source_target_pairs={{0,6},{2,0},{4,2},{6,4},{1,7},{3,1},{5,3},{7,5},{8,14},{10,8},{12,... | collective-permute-start | bytes 196616 | tf_op jit(solution)/shard_map/ppermute | solution.py:24
  39.3 3.5 %collective-permute-start.5 = (f32[4,128,128]{2,1,0:T(8,128)S(1)}, f32[4,128,128]{2,1,0:T(8,128)S(1)}, u32[]{:S(2)}, u32[]{:S(2)}) collective-permute-start(f32[4,128,128]{2,1,0:T(8,128)S(1)} %get-tuple-element.46), channel_id=1, source_target_pairs={{0,4},{2,6},{4,0},{6,2},{1,5},{3,7},{5,1},{7,3},{8,12},{10,14},{12... | collective-permute-start | bytes 786440 | tf_op jit(solution)/shard_map/ppermute | solution.py:24
  42.9 3.8 %collective-permute-done.17 = f32[8,16,128]{2,1,0:T(8,128)S(1)} collective-permute-done((f32[8,16,128]{2,1,0:T(8,128)S(1)}, f32[8,16,128]{2,1,0:T(8,128)S(1)}, u32[]{:S(2)}, u32[]{:S(2)}) %collective-permute-start.17) | collective-permute-done | bytes 65568 | tf_op jit(solution)/shard_map/ppermute | solution.py:24
  46.7 4.2 %collective-permute-start.6 = (f32[4,128,128]{2,1,0:T(8,128)S(1)}, f32[4,128,128]{2,1,0:T(8,128)S(1)}, u32[]{:S(2)}, u32[]{:S(2)}) collective-permute-start(f32[4,128,128]{2,1,0:T(8,128)S(1)} %get-tuple-element.46), channel_id=1, source_target_pairs={{0,6},{2,0},{4,2},{6,4},{1,7},{3,1},{5,3},{7,5},{8,14},{10,8},{12,... | collective-permute-start | bytes 786440 | tf_op jit(solution)/shard_map/ppermute | solution.py:24
  50.9 6.3 %collective-permute-done.15 = f32[8,16,128]{2,1,0:T(8,128)S(1)} collective-permute-done((f32[8,16,128]{2,1,0:T(8,128)S(1)}, f32[8,16,128]{2,1,0:T(8,128)S(1)}, u32[]{:S(2)}, u32[]{:S(2)}) %collective-permute-start.15) | collective-permute-done | bytes 65568 | tf_op jit(solution)/shard_map/ppermute | solution.py:24
  57.2 1.5 collective-permute-start.11
  59.0 0.7 copy-done.2
  59.7 11.3 %collective-permute-done.11 = f32[6,128,128]{2,1,0:T(8,128)S(1)} collective-permute-done((f32[6,128,128]{2,1,0:T(8,128)}, f32[6,128,128]{2,1,0:T(8,128)S(1)}, u32[]{:S(2)}, u32[]{:S(2)}) %collective-permute-start.11) | collective-permute-done | bytes 393248 | tf_op jit(solution)/shard_map/ppermute | solution.py:24
  71.0 7.4 %collective-permute-done.10 = f32[6,128,128]{2,1,0:T(8,128)S(1)} collective-permute-done((f32[6,128,128]{2,1,0:T(8,128)}, f32[6,128,128]{2,1,0:T(8,128)S(1)}, u32[]{:S(2)}, u32[]{:S(2)}) %collective-permute-start.10) | collective-permute-done | bytes 393248 | tf_op jit(solution)/shard_map/ppermute | solution.py:24
  78.4 0.8 copy-done.4
  80.0 1.5 maximum_bitcast_fusion.1
  81.8 1.8 %shard_map.60 = f32[16,136,128]{2,1,0:T(8,128)} custom-call(s32[32]{0:T(128)S(1)} %convert_element_type.39.goal_ref, f32[8,72,128]{2,1,0:T(8,128)S(1)} %all-to-all-done.received_ref), custom_call_target="tpu_custom_call" | custom-call | flops 600000000 | bytes 5000000 | tf_op jit(solution)/shard_map/pallas_call | solution.py:164
  83.5 0.9 slice_bitcast_fusion.5
  84.5 0.9 slice_bitcast_fusion.6
  85.4 0.9 slice_bitcast_fusion.7
  86.3 2.4 %shard_map.59.first_ref = f32[8,16,128]{2,1,0:T(8,128)S(1)} custom-call(s32[5]{0:T(128)S(1)} %stack.123.place_ref, f32[8,16,128]{2,1,0:T(8,128)S(1)} %add_add_fusion.1.start_ref, f32[4,4,128,128]{3,2,1,0:T(8,128)S(1)} %pad_maximum_fusion.e0_ref, f32[4,4,128,128]{3,2,1,0:T(8,128)S(1)} %collective-permute-done.18.e1_ref, ...), custom_call_target="tpu_custom_call" | custom-call | flops 600000000 | bytes 5000000 | tf_op jit(solution)/shard_map/pallas_call | solution.py:164
  88.7 2.6 %collective-permute-start.20 = (f32[8,16,128]{2,1,0:T(8,128)S(1)}, f32[8,16,128]{2,1,0:T(8,128)S(1)}, u32[]{:S(2)}, u32[]{:S(2)}) collective-permute-start(f32[8,16,128]{2,1,0:T(8,128)S(1)} %shard_map.59.first_ref), channel_id=1, source_target_pairs={{0,8},{1,9},{2,10},{3,11},{4,12},{5,13},{6,14},{7,15},{16,24},{17,... | collective-permute-start | bytes 196616 | tf_op jit(solution)/shard_map/ppermute | solution.py:251
  91.4 1.8 %collective-permute-done.20.passed_ref = f32[8,16,128]{2,1,0:T(8,128)S(1)} collective-permute-done((f32[8,16,128]{2,1,0:T(8,128)S(1)}, f32[8,16,128]{2,1,0:T(8,128)S(1)}, u32[]{:S(2)}, u32[]{:S(2)}) %collective-permute-start.20) | collective-permute-done | bytes 65568 | tf_op jit(solution)/shard_map/ppermute | solution.py:251
  93.2 0.8 shard_map.61
  94.1 1.2 collective-permute-done.21
  95.2 1.4 collective-permute-start.23
  97.3 1.7 %collective-permute-done.24 = f32[2,16,128]{2,1,0:T(8,128)S(1)} collective-permute-done((f32[2,16,128]{2,1,0:T(8,128)S(1)}, f32[2,16,128]{2,1,0:T(8,128)S(1)}, u32[]{:S(2)}, u32[]{:S(2)}) %collective-permute-start.24) | collective-permute-done | bytes 16416 | tf_op jit(solution)/shard_map/ppermute | solution.py:24
  99.0 1.5 collective-permute-done.23
  100.5 1.2 collective-permute-done.22
  101.7 3.1 %shard_map.62 = f32[8,2,16,128]{3,2,1,0:T(8,128)} custom-call(s32[5]{0:T(128)S(1)} %stack.123.place_ref, f32[4,2,16,128]{3,2,1,0:T(8,128)S(1)} %pad_maximum_fusion.6.start_ref, f32[8,16,128]{2,1,0:T(8,128)S(1)} %shard_map.59.first_ref, f32[4,4,128,128]{3,2,1,0:T(8,128)S(1)} %pad_maximum_fusion.e0_ref, f32[4,4,128,128]{3,2,1,0:T(8,128)S(1)} %collective-permute-done.18.e1_ref, ...), custom_call_target="tpu_custom_call" | custom-call | flops 600000000 | bytes 5000000 | tf_op jit(solution)/shard_map/pallas_call | solution.py:164
  104.7 6.1 %all-to-all-start.1 = ((f32[16,16,128]{2,1,0:T(8,128)}), f32[16,16,128]{2,1,0:T(8,128)S(1)}, u32[]{:S(2)}, u32[]{:S(2)}) async-start(f32[16,16,128]{2,1,0:T(8,128)} %bitcast.42), calls=%async_computation.1 | async-start | bytes 262144 | tf_op jit(solution)/shard_map/all_to_all | solution.py:264
  110.9 6.6 %copy.16 = f32[2,128,32,128]{3,1,2,0:T(8,128)} copy(f32[2,128,32,128]{3,2,1,0:T(8,128)} %bitcast.91) | data formatting | bytes 8388608 | tf_op jit(solution)/shard_map/layout_constraint | solution.py:258
  117.5 1.2 all-to-all-done.1
  118.7 2.2 %copy-done = f32[2,128,32,128]{3,1,2,0:T(8,128)S(1)} copy-done((f32[2,128,32,128]{3,1,2,0:T(8,128)S(1)}, f32[2,128,32,128]{3,1,2,0:T(8,128)}, u32[]{:S(2)}) %copy-start) | copy-done | bytes 4194328
  120.9 1.9 %shard_map.63 = (f32[4,15,16,128]{3,2,1,0:T(8,128)S(1)}, f32[4,15,16,128]{3,2,1,0:T(8,128)S(1)}, f32[2,16,16,128]{3,2,1,0:T(8,128)S(1)}, f32[2,16,16,128]{3,2,1,...) custom-call(s32[5]{0:T(128)S(1)} %stack.123.place_ref, f32[8,2,16,128]{3,2,1,0:T(8,128)S(1)} %bitcast.88, ...), custom_call_target="tpu_custom_call" | custom-call | flops 900000000 | bytes 8000000 | tf_op jit(solution)/shard_map/pallas_call | solution.py:179
  122.8 0.8 collective-permute-start.29
  123.6 2.7 %collective-permute-start.30 = (f32[2,16,16,128]{3,2,1,0:T(8,128)S(1)}, f32[2,16,16,128]{3,2,1,0:T(8,128)}, u32[]{:S(2)}, u32[]{:S(2)}) collective-permute-start(f32[2,16,16,128]{3,2,1,0:T(8,128)S(1)} %get-tuple-element.30), channel_id=1, source_target_pairs={{0,64},{32,96},{64,0},{96,32},{1,65},{33,97},{65,1},{97,33},{2,66}... | collective-permute-start | bytes 786440 | tf_op jit(solution)/shard_map/ppermute | solution.py:24
  126.3 1.5 collective-permute-start.31
  127.7 0.8 slice.121
  128.6 3.0 %collective-permute-start.25 = (f32[4,15,16,128]{3,2,1,0:T(8,128)S(1)}, f32[4,15,16,128]{3,2,1,0:T(8,128)}, u32[]{:S(2)}, u32[]{:S(2)}) collective-permute-start(f32[4,15,16,128]{3,2,1,0:T(8,128)S(1)} %get-tuple-element.27), channel_id=1, source_target_pairs={{0,16},{16,0},{1,17},{17,1},{2,18},{18,2},{3,19},{19,3},{4,20},{20... | collective-permute-start | bytes 1474568 | tf_op jit(solution)/shard_map/ppermute | solution.py:24
  132.1 3.7 %all-to-all-start.2 = ((f32[16,136,128]{2,1,0:T(8,128)}), f32[16,136,128]{2,1,0:T(8,128)S(1)}, u32[]{:S(2)}, u32[]{:S(2)}) async-start(f32[16,136,128]{2,1,0:T(8,128)} %shard_map.60), calls=%async_computation.2 | async-start | bytes 2228224 | tf_op jit(solution)/shard_map/all_to_all | solution.py:273
  135.9 0.7 collective-permute-done.30
  136.6 1.2 add_add_fusion
  137.8 3.0 %collective-permute-start.32 = (f32[16,16,128]{2,1,0:T(8,128)S(1)}, f32[16,16,128]{2,1,0:T(8,128)S(1)}, u32[]{:S(2)}, u32[]{:S(2)}) collective-permute-start(f32[16,16,128]{2,1,0:T(8,128)S(1)} %slice_bitcast_fusion.3), channel_id=1, source_target_pairs={{0,16},{16,0},{1,17},{17,1},{2,18},{18,2},{3,19},{19,3},{4,20},{20... | collective-permute-start | bytes 393224 | tf_op jit(solution)/shard_map/ppermute | solution.py:24
  140.8 1.9 %collective-permute-done.25 = f32[4,15,16,128]{3,2,1,0:T(8,128)} collective-permute-done((f32[4,15,16,128]{3,2,1,0:T(8,128)S(1)}, f32[4,15,16,128]{3,2,1,0:T(8,128)}, u32[]{:S(2)}, u32[]{:S(2)}) %collective-permute-start.25) | collective-permute-done | bytes 491552 | tf_op jit(solution)/shard_map/ppermute | solution.py:24
  142.7 1.1 add.84
  143.9 0.8 collective-permute-start.27
  144.7 2.5 %collective-permute-start.28 = (f32[15,16,128]{2,1,0:T(8,128)S(1)}, f32[15,16,128]{2,1,0:T(8,128)S(1)}, u32[]{:S(2)}, u32[]{:S(2)}) collective-permute-start(f32[15,16,128]{2,1,0:T(8,128)S(1)} %get-tuple-element.41), channel_id=1, source_target_pairs={{0,96},{32,0},{64,32},{96,64},{1,97},{33,1},{65,33},{97,65},{2,98}... | collective-permute-start | bytes 368648 | tf_op jit(solution)/shard_map/ppermute | solution.py:24
  147.2 8.3 %collective-permute-done.32 = f32[16,16,128]{2,1,0:T(8,128)S(1)} collective-permute-done((f32[16,16,128]{2,1,0:T(8,128)S(1)}, f32[16,16,128]{2,1,0:T(8,128)S(1)}, u32[]{:S(2)}, u32[]{:S(2)}) %collective-permute-start.32) | collective-permute-done | bytes 131104 | tf_op jit(solution)/shard_map/ppermute | solution.py:24
  156.0 0.7 shard_map.64
  156.8 1.0 copy.14
  (79 shorter events, 8.0 us)
Async XLA Ops:
  4.0 10.4 %collective-permute-start = (f32[2,128,128]{2,1,0:T(8,128)S(1)}, f32[2,128,128]{2,1,0:T(8,128)S(1)}, u32[]{:S(2)}, u32[]{:S(2)}) collective-permute-start(f32[2,128,128]{2,1,0:T(8,128)S(1)} %pad_maximum_fusion.5), channel_id=1, source_target_pairs={{0,16},{16,0},{1,17},{17,1},{2,18},{18,2},{3,19},{19,3},{4,20},{20... | collective-permute-start | bytes 393224 | tf_op jit(solution)/shard_map/ppermute | solution.py:216
  10.0 16.1 %all-to-all-start = ((f32[8,72,128]{2,1,0:T(8,128)}), f32[8,72,128]{2,1,0:T(8,128)S(1)}, u32[]{:S(2)}, u32[]{:S(2)}) async-start(f32[8,72,128]{2,1,0:T(8,128)} %pad_maximum_fusion.3), calls=%async_computation | async-start | bytes 589824 | tf_op jit(solution)/shard_map/all_to_all | solution.py:219
  15.0 6.3 %collective-permute-start.7 = (f32[128,128]{1,0:T(8,128)S(1)}, f32[128,128]{1,0:T(8,128)S(1)}, u32[]{:S(2)}, u32[]{:S(2)}) collective-permute-start(f32[128,128]{1,0:T(8,128)S(1)} %get-tuple-element.52), channel_id=1, source_target_pairs={{0,2},{2,4},{4,6},{6,0},{1,3},{3,5},{5,7},{7,1},{8,10},{10,12},{12... | collective-permute-start | bytes 196616 | tf_op jit(solution)/shard_map/ppermute | solution.py:24
  16.9 8.6 %collective-permute-start.9 = (f32[128,128]{1,0:T(8,128)S(1)}, f32[128,128]{1,0:T(8,128)S(1)}, u32[]{:S(2)}, u32[]{:S(2)}) collective-permute-start(f32[128,128]{1,0:T(8,128)S(1)} %get-tuple-element.52), channel_id=1, source_target_pairs={{0,6},{2,0},{4,2},{6,4},{1,7},{3,1},{5,3},{7,5},{8,14},{10,8},{12,... | collective-permute-start | bytes 196616 | tf_op jit(solution)/shard_map/ppermute | solution.py:24
  19.1 5.8 %collective-permute-start.8 = (f32[128,128]{1,0:T(8,128)S(1)}, f32[128,128]{1,0:T(8,128)S(1)}, u32[]{:S(2)}, u32[]{:S(2)}) collective-permute-start(f32[128,128]{1,0:T(8,128)S(1)} %get-tuple-element.52), channel_id=1, source_target_pairs={{0,4},{2,6},{4,0},{6,2},{1,5},{3,7},{5,1},{7,3},{8,12},{10,14},{12... | collective-permute-start | bytes 196616 | tf_op jit(solution)/shard_map/ppermute | solution.py:24
  26.9 7.0 %collective-permute-start.13 = (f32[8,16,128]{2,1,0:T(8,128)S(1)}, f32[8,16,128]{2,1,0:T(8,128)S(1)}, u32[]{:S(2)}, u32[]{:S(2)}) collective-permute-start(f32[8,16,128]{2,1,0:T(8,128)S(1)} %get-tuple-element.38), channel_id=1, source_target_pairs={{0,8},{8,0},{1,9},{9,1},{2,10},{10,2},{3,11},{11,3},{4,12},{12,4},... | collective-permute-start | bytes 196616 | tf_op jit(solution)/shard_map/ppermute | solution.py:24
  29.0 10.1 %collective-permute-start.3 = (f32[128,128]{1,0:T(8,128)S(1)}, f32[128,128]{1,0:T(8,128)S(1)}, u32[]{:S(2)}, u32[]{:S(2)}) collective-permute-start(f32[128,128]{1,0:T(8,128)S(1)} %get-tuple-element.48), channel_id=1, source_target_pairs={{0,96},{32,0},{64,32},{96,64},{1,97},{33,1},{65,33},{97,65},{2,98}... | collective-permute-start | bytes 196616 | tf_op jit(solution)/shard_map/ppermute | solution.py:24
  32.3 7.0 %collective-permute-start.2 = (f32[128,128]{1,0:T(8,128)S(1)}, f32[128,128]{1,0:T(8,128)S(1)}, u32[]{:S(2)}, u32[]{:S(2)}) collective-permute-start(f32[128,128]{1,0:T(8,128)S(1)} %get-tuple-element.48), channel_id=1, source_target_pairs={{0,64},{32,96},{64,0},{96,32},{1,65},{33,97},{65,1},{97,33},{2,66}... | collective-permute-start | bytes 196616 | tf_op jit(solution)/shard_map/ppermute | solution.py:24
  33.1 6.1 %collective-permute-start.1 = (f32[128,128]{1,0:T(8,128)S(1)}, f32[128,128]{1,0:T(8,128)S(1)}, u32[]{:S(2)}, u32[]{:S(2)}) collective-permute-start(f32[128,128]{1,0:T(8,128)S(1)} %get-tuple-element.48), channel_id=1, source_target_pairs={{0,32},{32,64},{64,96},{96,0},{1,33},{33,65},{65,97},{97,1},{2,34}... | collective-permute-start | bytes 196616 | tf_op jit(solution)/shard_map/ppermute | solution.py:24
  34.0 3.1 %collective-permute-start.14 = (f32[8,16,128]{2,1,0:T(8,128)S(1)}, f32[8,16,128]{2,1,0:T(8,128)S(1)}, u32[]{:S(2)}, u32[]{:S(2)}) collective-permute-start(f32[8,16,128]{2,1,0:T(8,128)S(1)} %add.78), channel_id=1, source_target_pairs={{0,1},{1,0},{2,3},{3,2},{4,5},{5,4},{6,7},{7,6},{8,9},{9,8},{10,11... | collective-permute-start | bytes 196616 | tf_op jit(solution)/shard_map/ppermute | solution.py:24
  34.7 24.2 %collective-permute-start.12 = (f32[6,128,128]{2,1,0:T(8,128)}, f32[6,128,128]{2,1,0:T(8,128)S(1)}, u32[]{:S(2)}, u32[]{:S(2)}) collective-permute-start(f32[6,128,128]{2,1,0:T(8,128)} %constant_dynamic-update-slice_fusion), channel_id=1, source_target_pairs={{0,96},{32,0},{64,32},{96,64},{1,97},{33,1},{65,33},{97,65},{2,98}... | collective-permute-start | bytes 1179656 | tf_op jit(solution)/shard_map/ppermute | solution.py:24
  37.1 9.6 %collective-permute-start.17 = (f32[8,16,128]{2,1,0:T(8,128)S(1)}, f32[8,16,128]{2,1,0:T(8,128)S(1)}, u32[]{:S(2)}, u32[]{:S(2)}) collective-permute-start(f32[8,16,128]{2,1,0:T(8,128)S(1)} %add.79), channel_id=1, source_target_pairs={{0,6},{2,0},{4,2},{6,4},{1,7},{3,1},{5,3},{7,5},{8,14},{10,8},{12,... | collective-permute-start | bytes 196616 | tf_op jit(solution)/shard_map/ppermute | solution.py:24
  39.2 11.8 %collective-permute-start.16 = (f32[8,16,128]{2,1,0:T(8,128)S(1)}, f32[8,16,128]{2,1,0:T(8,128)S(1)}, u32[]{:S(2)}, u32[]{:S(2)}) collective-permute-start(f32[8,16,128]{2,1,0:T(8,128)S(1)} %add.79), channel_id=1, source_target_pairs={{0,4},{2,6},{4,0},{6,2},{1,5},{3,7},{5,1},{7,3},{8,12},{10,14},{12... | collective-permute-start | bytes 196616 | tf_op jit(solution)/shard_map/ppermute | solution.py:24
  39.3 19.4 %collective-permute-start.5 = (f32[4,128,128]{2,1,0:T(8,128)S(1)}, f32[4,128,128]{2,1,0:T(8,128)S(1)}, u32[]{:S(2)}, u32[]{:S(2)}) collective-permute-start(f32[4,128,128]{2,1,0:T(8,128)S(1)} %get-tuple-element.46), channel_id=1, source_target_pairs={{0,4},{2,6},{4,0},{6,2},{1,5},{3,7},{5,1},{7,3},{8,12},{10,14},{12... | collective-permute-start | bytes 786440 | tf_op jit(solution)/shard_map/ppermute | solution.py:24
  42.8 16.0 %collective-permute-start.4 = (f32[4,128,128]{2,1,0:T(8,128)S(1)}, f32[4,128,128]{2,1,0:T(8,128)S(1)}, u32[]{:S(2)}, u32[]{:S(2)}) collective-permute-start(f32[4,128,128]{2,1,0:T(8,128)S(1)} %get-tuple-element.46), channel_id=1, source_target_pairs={{0,2},{2,4},{4,6},{6,0},{1,3},{3,5},{5,7},{7,1},{8,10},{10,12},{12... | collective-permute-start | bytes 786440 | tf_op jit(solution)/shard_map/ppermute | solution.py:24
  46.7 12.1 %collective-permute-start.6 = (f32[4,128,128]{2,1,0:T(8,128)S(1)}, f32[4,128,128]{2,1,0:T(8,128)S(1)}, u32[]{:S(2)}, u32[]{:S(2)}) collective-permute-start(f32[4,128,128]{2,1,0:T(8,128)S(1)} %get-tuple-element.46), channel_id=1, source_target_pairs={{0,6},{2,0},{4,2},{6,4},{1,7},{3,1},{5,3},{7,5},{8,14},{10,8},{12,... | collective-permute-start | bytes 786440 | tf_op jit(solution)/shard_map/ppermute | solution.py:24
  50.9 6.3 %collective-permute-start.15 = (f32[8,16,128]{2,1,0:T(8,128)S(1)}, f32[8,16,128]{2,1,0:T(8,128)S(1)}, u32[]{:S(2)}, u32[]{:S(2)}) collective-permute-start(f32[8,16,128]{2,1,0:T(8,128)S(1)} %add.79), channel_id=1, source_target_pairs={{0,2},{2,4},{4,6},{6,0},{1,3},{3,5},{5,7},{7,1},{8,10},{10,12},{12... | collective-permute-start | bytes 196616 | tf_op jit(solution)/shard_map/ppermute | solution.py:24
  57.2 13.7 %collective-permute-start.11 = (f32[6,128,128]{2,1,0:T(8,128)}, f32[6,128,128]{2,1,0:T(8,128)S(1)}, u32[]{:S(2)}, u32[]{:S(2)}) collective-permute-start(f32[6,128,128]{2,1,0:T(8,128)} %constant_dynamic-update-slice_fusion), channel_id=1, source_target_pairs={{0,64},{32,96},{64,0},{96,32},{1,65},{33,97},{65,1},{97,33},{2,66}... | collective-permute-start | bytes 1179656 | tf_op jit(solution)/shard_map/ppermute | solution.py:24
  58.7 19.7 %collective-permute-start.10 = (f32[6,128,128]{2,1,0:T(8,128)}, f32[6,128,128]{2,1,0:T(8,128)S(1)}, u32[]{:S(2)}, u32[]{:S(2)}) collective-permute-start(f32[6,128,128]{2,1,0:T(8,128)} %constant_dynamic-update-slice_fusion), channel_id=1, source_target_pairs={{0,32},{32,64},{64,96},{96,0},{1,33},{33,65},{65,97},{97,1},{2,34}... | collective-permute-start | bytes 1179656 | tf_op jit(solution)/shard_map/ppermute | solution.py:24
  58.9 0.8 copy-start.2
  71.0 7.4 %copy-start.3 = (f32[6,128,128]{2,1,0:T(8,128)}, f32[6,128,128]{2,1,0:T(8,128)S(1)}, u32[]{:S(2)}) copy-start(f32[6,128,128]{2,1,0:T(8,128)S(1)} %collective-permute-done.11) | copy-start | bytes 1179652
  78.4 0.8 copy-start.4
  79.3 7.0 %collective-permute-start.18 = (f32[4,4,128,128]{3,2,1,0:T(8,128)S(1)}, f32[4,4,128,128]{3,2,1,0:T(8,128)S(1)}, u32[]{:S(2)}, u32[]{:S(2)}) collective-permute-start(f32[4,4,128,128]{3,2,1,0:T(8,128)S(1)} %pad_maximum_fusion.e0_ref), channel_id=1, source_target_pairs={{0,1},{1,0},{2,3},{3,2},{4,5},{5,4},{6,7},{7,6},{8,9},{9,8},{10,11... | collective-permute-start | bytes 3145736 | tf_op jit(solution)/shard_map/ppermute | solution.py:24
  79.4 6.9 %collective-permute-start.19 = (f32[4,4,128,128]{3,2,1,0:T(8,128)S(1)}, f32[4,4,128,128]{3,2,1,0:T(8,128)}, u32[]{:S(2)}, u32[]{:S(2)}) collective-permute-start(f32[4,4,128,128]{3,2,1,0:T(8,128)S(1)} %pad_maximum_fusion.1.o0_ref), channel_id=1, source_target_pairs={{0,1},{1,0},{2,3},{3,2},{4,5},{5,4},{6,7},{7,6},{8,9},{9,8},{10,11... | collective-permute-start | bytes 3145736 | tf_op jit(solution)/shard_map/ppermute | solution.py:24
  86.3 5.1 %copy-start.1 = (f32[1,2,128,128]{3,2,1,0:T(8,128)S(1)}, f32[1,2,128,128]{3,2,1,0:T(8,128)}, u32[]{:S(2)}) copy-start(f32[1,2,128,128]{3,2,1,0:T(8,128)} %maximum_bitcast_fusion.1) | copy-start | bytes 393220
  88.7 4.5 %collective-permute-start.20 = (f32[8,16,128]{2,1,0:T(8,128)S(1)}, f32[8,16,128]{2,1,0:T(8,128)S(1)}, u32[]{:S(2)}, u32[]{:S(2)}) collective-permute-start(f32[8,16,128]{2,1,0:T(8,128)S(1)} %shard_map.59.first_ref), channel_id=1, source_target_pairs={{0,8},{1,9},{2,10},{3,11},{4,12},{5,13},{6,14},{7,15},{16,24},{17,... | collective-permute-start | bytes 196616 | tf_op jit(solution)/shard_map/ppermute | solution.py:251
  94.0 1.3 collective-permute-start.21
  95.2 3.7 %collective-permute-start.24 = (f32[2,16,128]{2,1,0:T(8,128)S(1)}, f32[2,16,128]{2,1,0:T(8,128)S(1)}, u32[]{:S(2)}, u32[]{:S(2)}) collective-permute-start(f32[2,16,128]{2,1,0:T(8,128)S(1)} %pad_maximum_fusion.7), channel_id=1, source_target_pairs={{0,6},{2,0},{4,2},{6,4},{1,7},{3,1},{5,3},{7,5},{8,14},{10,8},{12,... | collective-permute-start | bytes 49160 | tf_op jit(solution)/shard_map/ppermute | solution.py:24
  95.2 5.2 %collective-permute-start.23 = (f32[2,16,128]{2,1,0:T(8,128)S(1)}, f32[2,16,128]{2,1,0:T(8,128)S(1)}, u32[]{:S(2)}, u32[]{:S(2)}) collective-permute-start(f32[2,16,128]{2,1,0:T(8,128)S(1)} %pad_maximum_fusion.7), channel_id=1, source_target_pairs={{0,4},{2,6},{4,0},{6,2},{1,5},{3,7},{5,1},{7,3},{8,12},{10,14},{12... | collective-permute-start | bytes 49160 | tf_op jit(solution)/shard_map/ppermute | solution.py:24
  96.7 5.0 %collective-permute-start.22 = (f32[2,16,128]{2,1,0:T(8,128)S(1)}, f32[2,16,128]{2,1,0:T(8,128)S(1)}, u32[]{:S(2)}, u32[]{:S(2)}) collective-permute-start(f32[2,16,128]{2,1,0:T(8,128)S(1)} %pad_maximum_fusion.7), channel_id=1, source_target_pairs={{0,2},{2,4},{4,6},{6,0},{1,3},{3,5},{5,7},{7,1},{8,10},{10,12},{12... | collective-permute-start | bytes 49160 | tf_op jit(solution)/shard_map/ppermute | solution.py:24
  104.7 14.0 %all-to-all-start.1 = ((f32[16,16,128]{2,1,0:T(8,128)}), f32[16,16,128]{2,1,0:T(8,128)S(1)}, u32[]{:S(2)}, u32[]{:S(2)}) async-start(f32[16,16,128]{2,1,0:T(8,128)} %bitcast.42), calls=%async_computation.1 | async-start | bytes 262144 | tf_op jit(solution)/shard_map/all_to_all | solution.py:264
  118.7 2.2 %copy-start = (f32[2,128,32,128]{3,1,2,0:T(8,128)S(1)}, f32[2,128,32,128]{3,1,2,0:T(8,128)}, u32[]{:S(2)}) copy-start(f32[2,128,32,128]{3,1,2,0:T(8,128)} %copy.16) | copy-start | bytes 12582916
  122.8 13.0 %collective-permute-start.29 = (f32[2,16,16,128]{3,2,1,0:T(8,128)S(1)}, f32[2,16,16,128]{3,2,1,0:T(8,128)}, u32[]{:S(2)}, u32[]{:S(2)}) collective-permute-start(f32[2,16,16,128]{3,2,1,0:T(8,128)S(1)} %get-tuple-element.29), channel_id=1, source_target_pairs={{0,32},{32,64},{64,96},{96,0},{1,33},{33,65},{65,97},{97,1},{2,34}... | collective-permute-start | bytes 786440 | tf_op jit(solution)/shard_map/ppermute | solution.py:24
  123.6 13.0 %collective-permute-start.30 = (f32[2,16,16,128]{3,2,1,0:T(8,128)S(1)}, f32[2,16,16,128]{3,2,1,0:T(8,128)}, u32[]{:S(2)}, u32[]{:S(2)}) collective-permute-start(f32[2,16,16,128]{3,2,1,0:T(8,128)S(1)} %get-tuple-element.30), channel_id=1, source_target_pairs={{0,64},{32,96},{64,0},{96,32},{1,65},{33,97},{65,1},{97,33},{2,66}... | collective-permute-start | bytes 786440 | tf_op jit(solution)/shard_map/ppermute | solution.py:24
  126.3 10.3 %collective-permute-start.31 = (f32[2,16,16,128]{3,2,1,0:T(8,128)S(1)}, f32[2,16,16,128]{3,2,1,0:T(8,128)}, u32[]{:S(2)}, u32[]{:S(2)}) collective-permute-start(f32[2,16,16,128]{3,2,1,0:T(8,128)S(1)} %get-tuple-element.31), channel_id=1, source_target_pairs={{0,96},{32,0},{64,32},{96,64},{1,97},{33,1},{65,33},{97,65},{2,98}... | collective-permute-start | bytes 786440 | tf_op jit(solution)/shard_map/ppermute | solution.py:24
  128.6 14.2 %collective-permute-start.25 = (f32[4,15,16,128]{3,2,1,0:T(8,128)S(1)}, f32[4,15,16,128]{3,2,1,0:T(8,128)}, u32[]{:S(2)}, u32[]{:S(2)}) collective-permute-start(f32[4,15,16,128]{3,2,1,0:T(8,128)S(1)} %get-tuple-element.27), channel_id=1, source_target_pairs={{0,16},{16,0},{1,17},{17,1},{2,18},{18,2},{3,19},{19,3},{4,20},{20... | collective-permute-start | bytes 1474568 | tf_op jit(solution)/shard_map/ppermute | solution.py:24
  132.1 23.5 %all-to-all-start.2 = ((f32[16,136,128]{2,1,0:T(8,128)}), f32[16,136,128]{2,1,0:T(8,128)S(1)}, u32[]{:S(2)}, u32[]{:S(2)}) async-start(f32[16,136,128]{2,1,0:T(8,128)} %shard_map.60), calls=%async_computation.2 | async-start | bytes 2228224 | tf_op jit(solution)/shard_map/all_to_all | solution.py:273
  137.8 17.7 %collective-permute-start.32 = (f32[16,16,128]{2,1,0:T(8,128)S(1)}, f32[16,16,128]{2,1,0:T(8,128)S(1)}, u32[]{:S(2)}, u32[]{:S(2)}) collective-permute-start(f32[16,16,128]{2,1,0:T(8,128)S(1)} %slice_bitcast_fusion.3), channel_id=1, source_target_pairs={{0,16},{16,0},{1,17},{17,1},{2,18},{18,2},{3,19},{19,3},{4,20},{20... | collective-permute-start | bytes 393224 | tf_op jit(solution)/shard_map/ppermute | solution.py:24
  143.9 11.7 %collective-permute-start.27 = (f32[15,16,128]{2,1,0:T(8,128)S(1)}, f32[15,16,128]{2,1,0:T(8,128)S(1)}, u32[]{:S(2)}, u32[]{:S(2)}) collective-permute-start(f32[15,16,128]{2,1,0:T(8,128)S(1)} %get-tuple-element.40), channel_id=1, source_target_pairs={{0,64},{32,96},{64,0},{96,32},{1,65},{33,97},{65,1},{97,33},{2,66}... | collective-permute-start | bytes 368648 | tf_op jit(solution)/shard_map/ppermute | solution.py:24
  144.7 10.8 %collective-permute-start.28 = (f32[15,16,128]{2,1,0:T(8,128)S(1)}, f32[15,16,128]{2,1,0:T(8,128)S(1)}, u32[]{:S(2)}, u32[]{:S(2)}) collective-permute-start(f32[15,16,128]{2,1,0:T(8,128)S(1)} %get-tuple-element.41), channel_id=1, source_target_pairs={{0,96},{32,0},{64,32},{96,64},{1,97},{33,1},{65,33},{97,65},{2,98}... | collective-permute-start | bytes 368648 | tf_op jit(solution)/shard_map/ppermute | solution.py:24
  147.2 8.4 %collective-permute-start.26 = (f32[15,16,128]{2,1,0:T(8,128)S(1)}, f32[15,16,128]{2,1,0:T(8,128)S(1)}, u32[]{:S(2)}, u32[]{:S(2)}) collective-permute-start(f32[15,16,128]{2,1,0:T(8,128)S(1)} %get-tuple-element.42), channel_id=1, source_target_pairs={{0,32},{32,64},{64,96},{96,0},{1,33},{33,65},{65,97},{97,1},{2,34}... | collective-permute-start | bytes 368648 | tf_op jit(solution)/shard_map/ppermute | solution.py:24

commit v7 on v6

--- a/solution.py
+++ b/solution.py
@@ -221,9 +221,7 @@
     by_z = around(odd[0], "z")
     even = jnp.stack(around(even[0], "x"))
     even = jnp.stack(around(even, "z"))
-    by_x = around(jnp.concatenate([jnp.stack(by_z), column]), "x")
-    odd = jnp.stack([p[:4] for p in by_x])
-    coupling = jnp.stack([p[4:] for p in by_x])
+    odd = jnp.stack(around(jnp.stack(by_z), "x"))
 
     data = received[:, : sources * share].reshape(rows, sources, share, BLOCK)
     label = received[:, sources * share : sources * share + sources, None, :]
@@ -245,6 +243,7 @@
 
     even, odd, start = lax.optimization_barrier((even, odd, start))
     factors = (even, rotated(even, "core", 1), odd, rotated(odd, "core", 1))
+    coupling = jnp.stack(around(column, "x"))
 
     shape = (HALF, share, BLOCK)
     first = local_kernel(first_kernel, shape, place, start, *factors)

time: 159 us -> 142 us (0.89)
  waiting for transfers between devices: 51.8 us -> 31.7 us
  starting transfers between devices: 63.2 us -> 72.2 us
  local copies, waits for them, and re-layouts: 22 us -> 15.1 us
    ppermute x31 -> x34, waiting for transfers between devices: 48.7 us -> 27 us  [rotated(): lax.ppermute(array, axis, [(i, (i + step) % size) for i in range(size)])]
    ppermute x31 -> x34, starting transfers between devices: 43.1 us -> 51.6 us  [rotated(): lax.ppermute(array, axis, [(i, (i + step) % size) for i in range(size)])]
    unnamed x14 -> x5, local copies, waits for them, and re-layouts: 6.52 us -> 3.15 us
    another operation x6 -> x0, local copies, waits for them, and re-layouts: 2.8 us -> none  [the longest x3 2.74 us: per_device(): coupling = jnp.stack([p[4:] for p in by_x])]
    all_to_all x1, waiting for transfers between devices: 0.01 us -> 2.74 us  [per_device(): received = lax.all_to_all(packed, ROW, 0, 0, tiled=True)]
  transfers between devices with their start and end apart: 36 -> 39, of which waited for: 15 -> 15; matrix products, arithmetic and copies ran while one was open for 14% -> 13% of each run, Pallas kernels for 1% -> 3%
where the time goes in v7:
time: 142 us; the launch traced here: 141 us
  starting transfers between devices  72.2 us (51%)
  waiting for transfers between devices  31.7 us (22%)
  local copies, waits for them, and re-layouts  15.1 us (11%)
  Pallas kernels  10.6 us (7%)
  other arithmetic  9.07 us (6%)
    ppermute x34, starting transfers between devices, rotated(): lax.ppermute(array, axis, [(i, (i + step) % size) for i in range(size)])  51.6 us
    ppermute x34, waiting for transfers between devices, rotated(): lax.ppermute(array, axis, [(i, (i + step) % size) for i in range(size)])  27 us
    pallas_call x5, Pallas kernels, local_kernel(): pl.pallas_call(kernel, out_shape=jax.ShapeDtypeStruct(shape, jnp.float32)...  8.69 us
    another operation x1, local copies, waits for them, and re-layouts, per_device(): upper = with_layout_constraint(upper, Layout(major_to_minor=(0, 1, 2, 3)))  6.61 us
    all_to_all x1, starting transfers between devices, per_device(): lax.all_to_all(copies.reshape(rows * 2, share, BLOCK), ROW + ('yl',), 0,...  5.92 us
    all_to_all x1, starting transfers between devices, per_device(): received = lax.all_to_all(packed, ROW, 0, 0, tiled=True)  4.3 us
    all_to_all x1, starting transfers between devices, per_device(): arrived = lax.all_to_all(outgoing, COL, 0, 0, tiled=True)  3.7 us
    ppermute x1, starting transfers between devices, per_device(): other = lax.ppermute(pair, 'yh', [(0, 1), (1, 0)])  3.39 us
  transfers between devices with their start and end apart: 39, of which 15 were waited for; matrix products, arithmetic and copies ran while one was open for 13% of the time, Pallas kernels for 3%

profile of v7, /device:TPU:0, one launch (start us, length us, event | category | flops | bytes accessed | tf_op | source)
XLA Modules:
  0.0 140.9 jit_solution(7401558703904184910)
XLA Ops:
  0.6 1.3 slice.80
  2.0 1.1 fusion.5
  3.1 0.9 fusion.4
  4.0 3.4 %collective-permute-start = (f32[2,128,128]{2,1,0:T(8,128)S(1)}, f32[2,128,128]{2,1,0:T(8,128)S(1)}, u32[]{:S(2)}, u32[]{:S(2)}) collective-permute-start(f32[2,128,128]{2,1,0:T(8,128)S(1)} %pad_maximum_fusion.6), channel_id=1, source_target_pairs={{0,16},{16,0},{1,17},{17,1},{2,18},{18,2},{3,19},{19,3},{4,20},{20... | collective-permute-start | bytes 393224 | tf_op jit(solution)/shard_map/ppermute | solution.py:216
  7.4 0.8 add_convert_fusion
  8.2 1.0 copy.12
  9.2 0.8 pad_maximum_fusion.3
  10.0 4.3 %all-to-all-start = ((f32[8,72,128]{2,1,0:T(8,128)}), f32[8,72,128]{2,1,0:T(8,128)S(1)}, u32[]{:S(2)}, u32[]{:S(2)}) async-start(f32[8,72,128]{2,1,0:T(8,128)} %pad_maximum_fusion.3), calls=%async_computation | async-start | bytes 589824 | tf_op jit(solution)/shard_map/all_to_all | solution.py:219
  14.4 0.6 fusion.12
  15.0 4.0 %collective-permute-start.9 = (f32[128,128]{1,0:T(8,128)S(1)}, f32[128,128]{1,0:T(8,128)S(1)}, u32[]{:S(2)}, u32[]{:S(2)}) collective-permute-start(f32[128,128]{1,0:T(8,128)S(1)} %get-tuple-element.55), channel_id=1, source_target_pairs={{0,6},{2,0},{4,2},{6,4},{1,7},{3,1},{5,3},{7,5},{8,14},{10,8},{12,... | collective-permute-start | bytes 196616 | tf_op jit(solution)/shard_map/ppermute | solution.py:24
  19.1 1.3 collective-permute-start.7
  20.3 2.7 %all-to-all-done.received_ref = f32[8,72,128]{2,1,0:T(8,128)S(1)} async-done(((f32[8,72,128]{2,1,0:T(8,128)}), f32[8,72,128]{2,1,0:T(8,128)S(1)}, u32[]{:S(2)}, u32[]{:S(2)}) %all-to-all-start) | async-done | bytes 294944 | tf_op jit(solution)/shard_map/all_to_all | solution.py:219
  23.2 0.6 select_reduce_fusion
  23.8 1.4 %collective-permute-start.13 = (f32[8,16,128]{2,1,0:T(8,128)S(1)}, f32[8,16,128]{2,1,0:T(8,128)S(1)}, u32[]{:S(2)}, u32[]{:S(2)}) collective-permute-start(f32[8,16,128]{2,1,0:T(8,128)S(1)} %get-tuple-element.38), channel_id=1, source_target_pairs={{0,8},{8,0},{1,9},{9,1},{2,10},{10,2},{3,11},{11,3},{4,12},{12,4},... | collective-permute-start | bytes 196616 | tf_op jit(solution)/shard_map/ppermute | solution.py:24
  25.3 3.6 %collective-permute-start.11 = (f32[4,128,128]{2,1,0:T(8,128)S(1)}, f32[4,128,128]{2,1,0:T(8,128)S(1)}, u32[]{:S(2)}, u32[]{:S(2)}) collective-permute-start(f32[4,128,128]{2,1,0:T(8,128)S(1)} %get-tuple-element.44), channel_id=1, source_target_pairs={{0,64},{32,96},{64,0},{96,32},{1,65},{33,97},{65,1},{97,33},{2,66}... | collective-permute-start | bytes 786440 | tf_op jit(solution)/shard_map/ppermute | solution.py:24
  29.0 0.6 fusion.11
  29.6 1.2 collective-permute-start.3
  30.8 1.5 %collective-permute-start.2 = (f32[128,128]{1,0:T(8,128)S(1)}, f32[128,128]{1,0:T(8,128)S(1)}, u32[]{:S(2)}, u32[]{:S(2)}) collective-permute-start(f32[128,128]{1,0:T(8,128)S(1)} %get-tuple-element.52), channel_id=1, source_target_pairs={{0,64},{32,96},{64,0},{96,32},{1,65},{33,97},{65,1},{97,33},{2,66}... | collective-permute-start | bytes 196616 | tf_op jit(solution)/shard_map/ppermute | solution.py:24
  32.3 3.5 %collective-permute-start.17 = (f32[8,16,128]{2,1,0:T(8,128)S(1)}, f32[8,16,128]{2,1,0:T(8,128)S(1)}, u32[]{:S(2)}, u32[]{:S(2)}) collective-permute-start(f32[8,16,128]{2,1,0:T(8,128)S(1)} %add.79), channel_id=1, source_target_pairs={{0,6},{2,0},{4,2},{6,4},{1,7},{3,1},{5,3},{7,5},{8,14},{10,8},{12,... | collective-permute-start | bytes 196616 | tf_op jit(solution)/shard_map/ppermute | solution.py:24
  35.9 2.3 %collective-permute-start.10 = (f32[4,128,128]{2,1,0:T(8,128)S(1)}, f32[4,128,128]{2,1,0:T(8,128)S(1)}, u32[]{:S(2)}, u32[]{:S(2)}) collective-permute-start(f32[4,128,128]{2,1,0:T(8,128)S(1)} %get-tuple-element.44), channel_id=1, source_target_pairs={{0,32},{32,64},{64,96},{96,0},{1,33},{33,65},{65,97},{97,1},{2,34}... | collective-permute-start | bytes 786440 | tf_op jit(solution)/shard_map/ppermute | solution.py:24
  38.2 1.1 collective-permute-start.12
  39.3 2.2 %collective-permute-start.16 = (f32[8,16,128]{2,1,0:T(8,128)S(1)}, f32[8,16,128]{2,1,0:T(8,128)S(1)}, u32[]{:S(2)}, u32[]{:S(2)}) collective-permute-start(f32[8,16,128]{2,1,0:T(8,128)S(1)} %add.79), channel_id=1, source_target_pairs={{0,4},{2,6},{4,0},{6,2},{1,5},{3,7},{5,1},{7,3},{8,12},{10,14},{12... | collective-permute-start | bytes 196616 | tf_op jit(solution)/shard_map/ppermute | solution.py:24
  41.5 1.0 collective-permute-start.15
  42.6 2.5 %collective-permute-done.16 = f32[8,16,128]{2,1,0:T(8,128)S(1)} collective-permute-done((f32[8,16,128]{2,1,0:T(8,128)S(1)}, f32[8,16,128]{2,1,0:T(8,128)S(1)}, u32[]{:S(2)}, u32[]{:S(2)}) %collective-permute-start.16) | collective-permute-done | bytes 65568 | tf_op jit(solution)/shard_map/ppermute | solution.py:24
  45.1 2.3 %collective-permute-start.5 = (f32[4,128,128]{2,1,0:T(8,128)S(1)}, f32[4,128,128]{2,1,0:T(8,128)S(1)}, u32[]{:S(2)}, u32[]{:S(2)}) collective-permute-start(f32[4,128,128]{2,1,0:T(8,128)S(1)} %get-tuple-element.48), channel_id=1, source_target_pairs={{0,4},{2,6},{4,0},{6,2},{1,5},{3,7},{5,1},{7,3},{8,12},{10,14},{12... | collective-permute-start | bytes 786440 | tf_op jit(solution)/shard_map/ppermute | solution.py:24
  47.4 0.9 collective-permute-start.4
  48.3 2.3 %collective-permute-start.6 = (f32[4,128,128]{2,1,0:T(8,128)S(1)}, f32[4,128,128]{2,1,0:T(8,128)S(1)}, u32[]{:S(2)}, u32[]{:S(2)}) collective-permute-start(f32[4,128,128]{2,1,0:T(8,128)S(1)} %get-tuple-element.48), channel_id=1, source_target_pairs={{0,6},{2,0},{4,2},{6,4},{1,7},{3,1},{5,3},{7,5},{8,14},{10,8},{12,... | collective-permute-start | bytes 786440 | tf_op jit(solution)/shard_map/ppermute | solution.py:24
  50.8 4.7 %collective-permute-done.5 = f32[4,128,128]{2,1,0:T(8,128)S(1)} collective-permute-done((f32[4,128,128]{2,1,0:T(8,128)S(1)}, f32[4,128,128]{2,1,0:T(8,128)S(1)}, u32[]{:S(2)}, u32[]{:S(2)}) %collective-permute-start.5) | collective-permute-done | bytes 262176 | tf_op jit(solution)/shard_map/ppermute | solution.py:24
  55.5 2.8 %collective-permute-done.4 = f32[4,128,128]{2,1,0:T(8,128)S(1)} collective-permute-done((f32[4,128,128]{2,1,0:T(8,128)S(1)}, f32[4,128,128]{2,1,0:T(8,128)S(1)}, u32[]{:S(2)}, u32[]{:S(2)}) %collective-permute-start.4) | collective-permute-done | bytes 262176 | tf_op jit(solution)/shard_map/ppermute | solution.py:24
  59.1 1.6 %fusion.8 = (f32[1,2,128,128]{3,2,1,0:T(8,128)}, f32[2,128,128]{2,1,0:T(8,128)}) fusion(f32[1,128,128]{2,1,0:T(8,128)} %get-tuple-element.54, f32[1,128,128]{2,1,0:T(8,128)} %get-tuple-element.51), kind=kLoop, calls=%fused_computation.43 | loop fusion | flops 32768 | bytes 393216 | tf_op jit(solution)/shard_map/stack | solution.py:246
  60.7 1.7 %collective-permute-start.22 = (f32[2,128,128]{2,1,0:T(8,128)}, f32[2,128,128]{2,1,0:T(8,128)}, u32[]{:S(2)}, u32[]{:S(2)}) collective-permute-start(f32[2,128,128]{2,1,0:T(8,128)} %get-tuple-element.50), channel_id=1, source_target_pairs={{0,64},{32,96},{64,0},{96,32},{1,65},{33,97},{65,1},{97,33},{2,66}... | collective-permute-start | bytes 393224 | tf_op jit(solution)/shard_map/ppermute | solution.py:24
  62.4 0.9 collective-permute-start.21
  63.2 2.4 %collective-permute-start.23 = (f32[2,128,128]{2,1,0:T(8,128)}, f32[2,128,128]{2,1,0:T(8,128)}, u32[]{:S(2)}, u32[]{:S(2)}) collective-permute-start(f32[2,128,128]{2,1,0:T(8,128)} %get-tuple-element.50), channel_id=1, source_target_pairs={{0,96},{32,0},{64,32},{96,64},{1,97},{33,1},{65,33},{97,65},{2,98}... | collective-permute-start | bytes 393224 | tf_op jit(solution)/shard_map/ppermute | solution.py:24
  65.9 1.8 %shard_map.60 = f32[16,136,128]{2,1,0:T(8,128)} custom-call(s32[32]{0:T(128)S(1)} %convert_element_type.39.goal_ref, f32[8,72,128]{2,1,0:T(8,128)S(1)} %all-to-all-done.received_ref), custom_call_target="tpu_custom_call" | custom-call | flops 600000000 | bytes 5000000 | tf_op jit(solution)/shard_map/pallas_call | solution.py:164
  67.7 2.4 %shard_map.59.first_ref = f32[8,16,128]{2,1,0:T(8,128)S(1)} custom-call(s32[5]{0:T(128)S(1)} %stack.123.place_ref, f32[8,16,128]{2,1,0:T(8,128)S(1)} %add_add_fusion.1.start_ref, f32[4,4,128,128]{3,2,1,0:T(8,128)S(1)} %pad_maximum_fusion.e0_ref, f32[4,4,128,128]{3,2,1,0:T(8,128)S(1)} %collective-permute-done.18.e1_ref, ...), custom_call_target="tpu_custom_call" | custom-call | flops 600000000 | bytes 5000000 | tf_op jit(solution)/shard_map/pallas_call | solution.py:164
  70.1 3.3 %collective-permute-start.20 = (f32[8,16,128]{2,1,0:T(8,128)S(1)}, f32[8,16,128]{2,1,0:T(8,128)S(1)}, u32[]{:S(2)}, u32[]{:S(2)}) collective-permute-start(f32[8,16,128]{2,1,0:T(8,128)S(1)} %shard_map.59.first_ref), channel_id=1, source_target_pairs={{0,8},{1,9},{2,10},{3,11},{4,12},{5,13},{6,14},{7,15},{16,24},{17,... | collective-permute-start | bytes 196616 | tf_op jit(solution)/shard_map/ppermute | solution.py:250
  73.4 1.1 pad_maximum_fusion.2.x_ref
  74.5 0.8 collective-permute-done.20.passed_ref
  75.2 0.8 shard_map.61
  76.1 1.2 collective-permute-done.24
  77.2 2.3 %collective-permute-start.27 = (f32[2,16,128]{2,1,0:T(8,128)S(1)}, f32[2,16,128]{2,1,0:T(8,128)S(1)}, u32[]{:S(2)}, u32[]{:S(2)}) collective-permute-start(f32[2,16,128]{2,1,0:T(8,128)S(1)} %pad_maximum_fusion.9), channel_id=1, source_target_pairs={{0,6},{2,0},{4,2},{6,4},{1,7},{3,1},{5,3},{7,5},{8,14},{10,8},{12,... | collective-permute-start | bytes 49160 | tf_op jit(solution)/shard_map/ppermute | solution.py:24
  81.0 3.8 %collective-permute-done.26 = f32[2,16,128]{2,1,0:T(8,128)S(1)} collective-permute-done((f32[2,16,128]{2,1,0:T(8,128)S(1)}, f32[2,16,128]{2,1,0:T(8,128)S(1)}, u32[]{:S(2)}, u32[]{:S(2)}) %collective-permute-start.26) | collective-permute-done | bytes 16416 | tf_op jit(solution)/shard_map/ppermute | solution.py:24
  85.0 3.0 %shard_map.62 = f32[8,2,16,128]{3,2,1,0:T(8,128)} custom-call(s32[5]{0:T(128)S(1)} %stack.123.place_ref, f32[4,2,16,128]{3,2,1,0:T(8,128)S(1)} %pad_maximum_fusion.8.start_ref, f32[8,16,128]{2,1,0:T(8,128)S(1)} %shard_map.59.first_ref, f32[4,4,128,128]{3,2,1,0:T(8,128)S(1)} %pad_maximum_fusion.e0_ref, f32[4,4,128,128]{3,2,1,0:T(8,128)S(1)} %collective-permute-done.18.e1_ref, ...), custom_call_target="tpu_custom_call" | custom-call | flops 600000000 | bytes 5000000 | tf_op jit(solution)/shard_map/pallas_call | solution.py:164
  88.1 5.9 %all-to-all-start.1 = ((f32[16,16,128]{2,1,0:T(8,128)}), f32[16,16,128]{2,1,0:T(8,128)S(1)}, u32[]{:S(2)}, u32[]{:S(2)}) async-start(f32[16,16,128]{2,1,0:T(8,128)} %bitcast.42), calls=%async_computation.1 | async-start | bytes 262144 | tf_op jit(solution)/shard_map/all_to_all | solution.py:263
  94.0 6.6 %copy.16 = f32[2,128,32,128]{3,1,2,0:T(8,128)} copy(f32[2,128,32,128]{3,2,1,0:T(8,128)} %bitcast.82) | data formatting | bytes 8388608 | tf_op jit(solution)/shard_map/layout_constraint | solution.py:257
  100.6 1.2 all-to-all-done.1
  101.9 2.2 %copy-done = f32[2,128,32,128]{3,1,2,0:T(8,128)S(1)} copy-done((f32[2,128,32,128]{3,1,2,0:T(8,128)S(1)}, f32[2,128,32,128]{3,1,2,0:T(8,128)}, u32[]{:S(2)}) %copy-start) | copy-done | bytes 4194328
  104.0 1.9 %shard_map.63 = (f32[4,15,16,128]{3,2,1,0:T(8,128)S(1)}, f32[4,15,16,128]{3,2,1,0:T(8,128)S(1)}, f32[2,16,16,128]{3,2,1,0:T(8,128)S(1)}, f32[2,16,16,128]{3,2,1,...) custom-call(s32[5]{0:T(128)S(1)} %stack.123.place_ref, f32[8,2,16,128]{3,2,1,0:T(8,128)S(1)} %bitcast.79, ...), custom_call_target="tpu_custom_call" | custom-call | flops 900000000 | bytes 8000000 | tf_op jit(solution)/shard_map/pallas_call | solution.py:179
  106.0 0.8 collective-permute-start.32
  106.8 2.7 %collective-permute-start.33 = (f32[2,16,16,128]{3,2,1,0:T(8,128)S(1)}, f32[2,16,16,128]{3,2,1,0:T(8,128)}, u32[]{:S(2)}, u32[]{:S(2)}) collective-permute-start(f32[2,16,16,128]{3,2,1,0:T(8,128)S(1)} %get-tuple-element.30), channel_id=1, source_target_pairs={{0,64},{32,96},{64,0},{96,32},{1,65},{33,97},{65,1},{97,33},{2,66}... | collective-permute-start | bytes 786440 | tf_op jit(solution)/shard_map/ppermute | solution.py:24
  109.4 1.5 %collective-permute-start.34 = (f32[2,16,16,128]{3,2,1,0:T(8,128)S(1)}, f32[2,16,16,128]{3,2,1,0:T(8,128)}, u32[]{:S(2)}, u32[]{:S(2)}) collective-permute-start(f32[2,16,16,128]{3,2,1,0:T(8,128)S(1)} %get-tuple-element.31), channel_id=1, source_target_pairs={{0,96},{32,0},{64,32},{96,64},{1,97},{33,1},{65,33},{97,65},{2,98}... | collective-permute-start | bytes 786440 | tf_op jit(solution)/shard_map/ppermute | solution.py:24
  110.9 0.8 slice.91
  111.7 3.0 %collective-permute-start.28 = (f32[4,15,16,128]{3,2,1,0:T(8,128)S(1)}, f32[4,15,16,128]{3,2,1,0:T(8,128)}, u32[]{:S(2)}, u32[]{:S(2)}) collective-permute-start(f32[4,15,16,128]{3,2,1,0:T(8,128)S(1)} %get-tuple-element.27), channel_id=1, source_target_pairs={{0,16},{16,0},{1,17},{17,1},{2,18},{18,2},{3,19},{19,3},{4,20},{20... | collective-permute-start | bytes 1474568 | tf_op jit(solution)/shard_map/ppermute | solution.py:24
  114.7 0.6 constant_dynamic-slice_fusion
  115.3 3.7 %all-to-all-start.2 = ((f32[16,136,128]{2,1,0:T(8,128)}), f32[16,136,128]{2,1,0:T(8,128)S(1)}, u32[]{:S(2)}, u32[]{:S(2)}) async-start(f32[16,136,128]{2,1,0:T(8,128)} %shard_map.60), calls=%async_computation.2 | async-start | bytes 2228224 | tf_op jit(solution)/shard_map/all_to_all | solution.py:272
  119.0 0.6 collective-permute-done.33
  119.6 1.2 add_add_fusion
  120.8 3.0 %collective-permute-start.35 = (f32[16,16,128]{2,1,0:T(8,128)S(1)}, f32[16,16,128]{2,1,0:T(8,128)S(1)}, u32[]{:S(2)}, u32[]{:S(2)}) collective-permute-start(f32[16,16,128]{2,1,0:T(8,128)S(1)} %slice_bitcast_fusion), channel_id=1, source_target_pairs={{0,16},{16,0},{1,17},{17,1},{2,18},{18,2},{3,19},{19,3},{4,20},{20... | collective-permute-start | bytes 393224 | tf_op jit(solution)/shard_map/ppermute | solution.py:24
  123.9 2.9 %collective-permute-done.28 = f32[4,15,16,128]{3,2,1,0:T(8,128)} collective-permute-done((f32[4,15,16,128]{3,2,1,0:T(8,128)S(1)}, f32[4,15,16,128]{3,2,1,0:T(8,128)}, u32[]{:S(2)}, u32[]{:S(2)}) %collective-permute-start.28) | collective-permute-done | bytes 491552 | tf_op jit(solution)/shard_map/ppermute | solution.py:24
  126.8 1.1 add.84
  128.0 3.2 %collective-permute-start.31 = (f32[15,16,128]{2,1,0:T(8,128)S(1)}, f32[15,16,128]{2,1,0:T(8,128)S(1)}, u32[]{:S(2)}, u32[]{:S(2)}) collective-permute-start(f32[15,16,128]{2,1,0:T(8,128)S(1)} %get-tuple-element.41), channel_id=1, source_target_pairs={{0,96},{32,0},{64,32},{96,64},{1,97},{33,1},{65,33},{97,65},{2,98}... | collective-permute-start | bytes 368648 | tf_op jit(solution)/shard_map/ppermute | solution.py:24
  131.3 7.4 %collective-permute-done.35 = f32[16,16,128]{2,1,0:T(8,128)S(1)} collective-permute-done((f32[16,16,128]{2,1,0:T(8,128)S(1)}, f32[16,16,128]{2,1,0:T(8,128)S(1)}, u32[]{:S(2)}, u32[]{:S(2)}) %collective-permute-start.35) | collective-permute-done | bytes 131104 | tf_op jit(solution)/shard_map/ppermute | solution.py:24
  139.2 0.7 shard_map.64
  139.9 1.0 copy.14
  (69 shorter events, 4.3 us)
Async XLA Ops:
  4.0 10.4 %collective-permute-start = (f32[2,128,128]{2,1,0:T(8,128)S(1)}, f32[2,128,128]{2,1,0:T(8,128)S(1)}, u32[]{:S(2)}, u32[]{:S(2)}) collective-permute-start(f32[2,128,128]{2,1,0:T(8,128)S(1)} %pad_maximum_fusion.6), channel_id=1, source_target_pairs={{0,16},{16,0},{1,17},{17,1},{2,18},{18,2},{3,19},{19,3},{4,20},{20... | collective-permute-start | bytes 393224 | tf_op jit(solution)/shard_map/ppermute | solution.py:216
  10.0 13.0 %all-to-all-start = ((f32[8,72,128]{2,1,0:T(8,128)}), f32[8,72,128]{2,1,0:T(8,128)S(1)}, u32[]{:S(2)}, u32[]{:S(2)}) async-start(f32[8,72,128]{2,1,0:T(8,128)} %pad_maximum_fusion.3), calls=%async_computation | async-start | bytes 589824 | tf_op jit(solution)/shard_map/all_to_all | solution.py:219
  15.0 10.2 %collective-permute-start.9 = (f32[128,128]{1,0:T(8,128)S(1)}, f32[128,128]{1,0:T(8,128)S(1)}, u32[]{:S(2)}, u32[]{:S(2)}) collective-permute-start(f32[128,128]{1,0:T(8,128)S(1)} %get-tuple-element.55), channel_id=1, source_target_pairs={{0,6},{2,0},{4,2},{6,4},{1,7},{3,1},{5,3},{7,5},{8,14},{10,8},{12,... | collective-permute-start | bytes 196616 | tf_op jit(solution)/shard_map/ppermute | solution.py:24
  19.1 6.2 %collective-permute-start.8 = (f32[128,128]{1,0:T(8,128)S(1)}, f32[128,128]{1,0:T(8,128)S(1)}, u32[]{:S(2)}, u32[]{:S(2)}) collective-permute-start(f32[128,128]{1,0:T(8,128)S(1)} %get-tuple-element.55), channel_id=1, source_target_pairs={{0,4},{2,6},{4,0},{6,2},{1,5},{3,7},{5,1},{7,3},{8,12},{10,14},{12... | collective-permute-start | bytes 196616 | tf_op jit(solution)/shard_map/ppermute | solution.py:24
  19.1 6.2 %collective-permute-start.7 = (f32[128,128]{1,0:T(8,128)S(1)}, f32[128,128]{1,0:T(8,128)S(1)}, u32[]{:S(2)}, u32[]{:S(2)}) collective-permute-start(f32[128,128]{1,0:T(8,128)S(1)} %get-tuple-element.55), channel_id=1, source_target_pairs={{0,2},{2,4},{4,6},{6,0},{1,3},{3,5},{5,7},{7,1},{8,10},{10,12},{12... | collective-permute-start | bytes 196616 | tf_op jit(solution)/shard_map/ppermute | solution.py:24
  23.8 5.0 %collective-permute-start.13 = (f32[8,16,128]{2,1,0:T(8,128)S(1)}, f32[8,16,128]{2,1,0:T(8,128)S(1)}, u32[]{:S(2)}, u32[]{:S(2)}) collective-permute-start(f32[8,16,128]{2,1,0:T(8,128)S(1)} %get-tuple-element.38), channel_id=1, source_target_pairs={{0,8},{8,0},{1,9},{9,1},{2,10},{10,2},{3,11},{11,3},{4,12},{12,4},... | collective-permute-start | bytes 196616 | tf_op jit(solution)/shard_map/ppermute | solution.py:24
  25.3 23.0 %collective-permute-start.11 = (f32[4,128,128]{2,1,0:T(8,128)S(1)}, f32[4,128,128]{2,1,0:T(8,128)S(1)}, u32[]{:S(2)}, u32[]{:S(2)}) collective-permute-start(f32[4,128,128]{2,1,0:T(8,128)S(1)} %get-tuple-element.44), channel_id=1, source_target_pairs={{0,64},{32,96},{64,0},{96,32},{1,65},{33,97},{65,1},{97,33},{2,66}... | collective-permute-start | bytes 786440 | tf_op jit(solution)/shard_map/ppermute | solution.py:24
  28.9 3.4 %collective-permute-start.14 = (f32[8,16,128]{2,1,0:T(8,128)S(1)}, f32[8,16,128]{2,1,0:T(8,128)S(1)}, u32[]{:S(2)}, u32[]{:S(2)}) collective-permute-start(f32[8,16,128]{2,1,0:T(8,128)S(1)} %add.78), channel_id=1, source_target_pairs={{0,1},{1,0},{2,3},{3,2},{4,5},{5,4},{6,7},{7,6},{8,9},{9,8},{10,11... | collective-permute-start | bytes 196616 | tf_op jit(solution)/shard_map/ppermute | solution.py:24
  29.6 6.3 %collective-permute-start.3 = (f32[128,128]{1,0:T(8,128)S(1)}, f32[128,128]{1,0:T(8,128)S(1)}, u32[]{:S(2)}, u32[]{:S(2)}) collective-permute-start(f32[128,128]{1,0:T(8,128)S(1)} %get-tuple-element.52), channel_id=1, source_target_pairs={{0,96},{32,0},{64,32},{96,64},{1,97},{33,1},{65,33},{97,65},{2,98}... | collective-permute-start | bytes 196616 | tf_op jit(solution)/shard_map/ppermute | solution.py:24
  30.8 7.4 %collective-permute-start.2 = (f32[128,128]{1,0:T(8,128)S(1)}, f32[128,128]{1,0:T(8,128)S(1)}, u32[]{:S(2)}, u32[]{:S(2)}) collective-permute-start(f32[128,128]{1,0:T(8,128)S(1)} %get-tuple-element.52), channel_id=1, source_target_pairs={{0,64},{32,96},{64,0},{96,32},{1,65},{33,97},{65,1},{97,33},{2,66}... | collective-permute-start | bytes 196616 | tf_op jit(solution)/shard_map/ppermute | solution.py:24
  32.3 7.0 %collective-permute-start.1 = (f32[128,128]{1,0:T(8,128)S(1)}, f32[128,128]{1,0:T(8,128)S(1)}, u32[]{:S(2)}, u32[]{:S(2)}) collective-permute-start(f32[128,128]{1,0:T(8,128)S(1)} %get-tuple-element.52), channel_id=1, source_target_pairs={{0,32},{32,64},{64,96},{96,0},{1,33},{33,65},{65,97},{97,1},{2,34}... | collective-permute-start | bytes 196616 | tf_op jit(solution)/shard_map/ppermute | solution.py:24
  32.3 9.2 %collective-permute-start.17 = (f32[8,16,128]{2,1,0:T(8,128)S(1)}, f32[8,16,128]{2,1,0:T(8,128)S(1)}, u32[]{:S(2)}, u32[]{:S(2)}) collective-permute-start(f32[8,16,128]{2,1,0:T(8,128)S(1)} %add.79), channel_id=1, source_target_pairs={{0,6},{2,0},{4,2},{6,4},{1,7},{3,1},{5,3},{7,5},{8,14},{10,8},{12,... | collective-permute-start | bytes 196616 | tf_op jit(solution)/shard_map/ppermute | solution.py:24
  35.9 14.8 %collective-permute-start.10 = (f32[4,128,128]{2,1,0:T(8,128)S(1)}, f32[4,128,128]{2,1,0:T(8,128)S(1)}, u32[]{:S(2)}, u32[]{:S(2)}) collective-permute-start(f32[4,128,128]{2,1,0:T(8,128)S(1)} %get-tuple-element.44), channel_id=1, source_target_pairs={{0,32},{32,64},{64,96},{96,0},{1,33},{33,65},{65,97},{97,1},{2,34}... | collective-permute-start | bytes 786440 | tf_op jit(solution)/shard_map/ppermute | solution.py:24
  38.2 12.5 %collective-permute-start.12 = (f32[4,128,128]{2,1,0:T(8,128)S(1)}, f32[4,128,128]{2,1,0:T(8,128)S(1)}, u32[]{:S(2)}, u32[]{:S(2)}) collective-permute-start(f32[4,128,128]{2,1,0:T(8,128)S(1)} %get-tuple-element.44), channel_id=1, source_target_pairs={{0,96},{32,0},{64,32},{96,64},{1,97},{33,1},{65,33},{97,65},{2,98}... | collective-permute-start | bytes 786440 | tf_op jit(solution)/shard_map/ppermute | solution.py:24
  39.3 5.8 %collective-permute-start.16 = (f32[8,16,128]{2,1,0:T(8,128)S(1)}, f32[8,16,128]{2,1,0:T(8,128)S(1)}, u32[]{:S(2)}, u32[]{:S(2)}) collective-permute-start(f32[8,16,128]{2,1,0:T(8,128)S(1)} %add.79), channel_id=1, source_target_pairs={{0,4},{2,6},{4,0},{6,2},{1,5},{3,7},{5,1},{7,3},{8,12},{10,14},{12... | collective-permute-start | bytes 196616 | tf_op jit(solution)/shard_map/ppermute | solution.py:24
  41.5 5.9 %collective-permute-start.15 = (f32[8,16,128]{2,1,0:T(8,128)S(1)}, f32[8,16,128]{2,1,0:T(8,128)S(1)}, u32[]{:S(2)}, u32[]{:S(2)}) collective-permute-start(f32[8,16,128]{2,1,0:T(8,128)S(1)} %add.79), channel_id=1, source_target_pairs={{0,2},{2,4},{4,6},{6,0},{1,3},{3,5},{5,7},{7,1},{8,10},{10,12},{12... | collective-permute-start | bytes 196616 | tf_op jit(solution)/shard_map/ppermute | solution.py:24
  45.1 10.4 %collective-permute-start.5 = (f32[4,128,128]{2,1,0:T(8,128)S(1)}, f32[4,128,128]{2,1,0:T(8,128)S(1)}, u32[]{:S(2)}, u32[]{:S(2)}) collective-permute-start(f32[4,128,128]{2,1,0:T(8,128)S(1)} %get-tuple-element.48), channel_id=1, source_target_pairs={{0,4},{2,6},{4,0},{6,2},{1,5},{3,7},{5,1},{7,3},{8,12},{10,14},{12... | collective-permute-start | bytes 786440 | tf_op jit(solution)/shard_map/ppermute | solution.py:24
  47.4 10.9 %collective-permute-start.4 = (f32[4,128,128]{2,1,0:T(8,128)S(1)}, f32[4,128,128]{2,1,0:T(8,128)S(1)}, u32[]{:S(2)}, u32[]{:S(2)}) collective-permute-start(f32[4,128,128]{2,1,0:T(8,128)S(1)} %get-tuple-element.48), channel_id=1, source_target_pairs={{0,2},{2,4},{4,6},{6,0},{1,3},{3,5},{5,7},{7,1},{8,10},{10,12},{12... | collective-permute-start | bytes 786440 | tf_op jit(solution)/shard_map/ppermute | solution.py:24
  48.3 10.0 %collective-permute-start.6 = (f32[4,128,128]{2,1,0:T(8,128)S(1)}, f32[4,128,128]{2,1,0:T(8,128)S(1)}, u32[]{:S(2)}, u32[]{:S(2)}) collective-permute-start(f32[4,128,128]{2,1,0:T(8,128)S(1)} %get-tuple-element.48), channel_id=1, source_target_pairs={{0,6},{2,0},{4,2},{6,4},{1,7},{3,1},{5,3},{7,5},{8,14},{10,8},{12,... | collective-permute-start | bytes 786440 | tf_op jit(solution)/shard_map/ppermute | solution.py:24
  58.4 9.2 %collective-permute-start.18 = (f32[4,4,128,128]{3,2,1,0:T(8,128)S(1)}, f32[4,4,128,128]{3,2,1,0:T(8,128)S(1)}, u32[]{:S(2)}, u32[]{:S(2)}) collective-permute-start(f32[4,4,128,128]{3,2,1,0:T(8,128)S(1)} %pad_maximum_fusion.e0_ref), channel_id=1, source_target_pairs={{0,1},{1,0},{2,3},{3,2},{4,5},{5,4},{6,7},{7,6},{8,9},{9,8},{10,11... | collective-permute-start | bytes 3145736 | tf_op jit(solution)/shard_map/ppermute | solution.py:24
  58.5 9.2 %collective-permute-start.19 = (f32[4,4,128,128]{3,2,1,0:T(8,128)S(1)}, f32[4,4,128,128]{3,2,1,0:T(8,128)}, u32[]{:S(2)}, u32[]{:S(2)}) collective-permute-start(f32[4,4,128,128]{3,2,1,0:T(8,128)S(1)} %pad_maximum_fusion.1.o0_ref), channel_id=1, source_target_pairs={{0,1},{1,0},{2,3},{3,2},{4,5},{5,4},{6,7},{7,6},{8,9},{9,8},{10,11... | collective-permute-start | bytes 3145736 | tf_op jit(solution)/shard_map/ppermute | solution.py:24
  60.7 12.7 %collective-permute-start.22 = (f32[2,128,128]{2,1,0:T(8,128)}, f32[2,128,128]{2,1,0:T(8,128)}, u32[]{:S(2)}, u32[]{:S(2)}) collective-permute-start(f32[2,128,128]{2,1,0:T(8,128)} %get-tuple-element.50), channel_id=1, source_target_pairs={{0,64},{32,96},{64,0},{96,32},{1,65},{33,97},{65,1},{97,33},{2,66}... | collective-permute-start | bytes 393224 | tf_op jit(solution)/shard_map/ppermute | solution.py:24
  62.4 11.0 %collective-permute-start.21 = (f32[2,128,128]{2,1,0:T(8,128)}, f32[2,128,128]{2,1,0:T(8,128)}, u32[]{:S(2)}, u32[]{:S(2)}) collective-permute-start(f32[2,128,128]{2,1,0:T(8,128)} %get-tuple-element.50), channel_id=1, source_target_pairs={{0,32},{32,64},{64,96},{96,0},{1,33},{33,65},{65,97},{97,1},{2,34}... | collective-permute-start | bytes 393224 | tf_op jit(solution)/shard_map/ppermute | solution.py:24
  63.2 10.1 %collective-permute-start.23 = (f32[2,128,128]{2,1,0:T(8,128)}, f32[2,128,128]{2,1,0:T(8,128)}, u32[]{:S(2)}, u32[]{:S(2)}) collective-permute-start(f32[2,128,128]{2,1,0:T(8,128)} %get-tuple-element.50), channel_id=1, source_target_pairs={{0,96},{32,0},{64,32},{96,64},{1,97},{33,1},{65,33},{97,65},{2,98}... | collective-permute-start | bytes 393224 | tf_op jit(solution)/shard_map/ppermute | solution.py:24
  67.7 5.7 %copy-start.1 = (f32[1,2,128,128]{3,2,1,0:T(8,128)S(1)}, f32[1,2,128,128]{3,2,1,0:T(8,128)}, u32[]{:S(2)}) copy-start(f32[1,2,128,128]{3,2,1,0:T(8,128)} %get-tuple-element.49) | copy-start | bytes 393220
  70.1 5.2 %collective-permute-start.20 = (f32[8,16,128]{2,1,0:T(8,128)S(1)}, f32[8,16,128]{2,1,0:T(8,128)S(1)}, u32[]{:S(2)}, u32[]{:S(2)}) collective-permute-start(f32[8,16,128]{2,1,0:T(8,128)S(1)} %shard_map.59.first_ref), channel_id=1, source_target_pairs={{0,8},{1,9},{2,10},{3,11},{4,12},{5,13},{6,14},{7,15},{16,24},{17,... | collective-permute-start | bytes 196616 | tf_op jit(solution)/shard_map/ppermute | solution.py:250
  76.0 1.3 collective-permute-start.24
  77.2 3.7 %collective-permute-start.27 = (f32[2,16,128]{2,1,0:T(8,128)S(1)}, f32[2,16,128]{2,1,0:T(8,128)S(1)}, u32[]{:S(2)}, u32[]{:S(2)}) collective-permute-start(f32[2,16,128]{2,1,0:T(8,128)S(1)} %pad_maximum_fusion.9), channel_id=1, source_target_pairs={{0,6},{2,0},{4,2},{6,4},{1,7},{3,1},{5,3},{7,5},{8,14},{10,8},{12,... | collective-permute-start | bytes 49160 | tf_op jit(solution)/shard_map/ppermute | solution.py:24
  79.5 5.2 %collective-permute-start.26 = (f32[2,16,128]{2,1,0:T(8,128)S(1)}, f32[2,16,128]{2,1,0:T(8,128)S(1)}, u32[]{:S(2)}, u32[]{:S(2)}) collective-permute-start(f32[2,16,128]{2,1,0:T(8,128)S(1)} %pad_maximum_fusion.9), channel_id=1, source_target_pairs={{0,4},{2,6},{4,0},{6,2},{1,5},{3,7},{5,1},{7,3},{8,12},{10,14},{12... | collective-permute-start | bytes 49160 | tf_op jit(solution)/shard_map/ppermute | solution.py:24
  80.1 5.0 %collective-permute-start.25 = (f32[2,16,128]{2,1,0:T(8,128)S(1)}, f32[2,16,128]{2,1,0:T(8,128)S(1)}, u32[]{:S(2)}, u32[]{:S(2)}) collective-permute-start(f32[2,16,128]{2,1,0:T(8,128)S(1)} %pad_maximum_fusion.9), channel_id=1, source_target_pairs={{0,2},{2,4},{4,6},{6,0},{1,3},{3,5},{5,7},{7,1},{8,10},{10,12},{12... | collective-permute-start | bytes 49160 | tf_op jit(solution)/shard_map/ppermute | solution.py:24
  88.1 13.8 %all-to-all-start.1 = ((f32[16,16,128]{2,1,0:T(8,128)}), f32[16,16,128]{2,1,0:T(8,128)S(1)}, u32[]{:S(2)}, u32[]{:S(2)}) async-start(f32[16,16,128]{2,1,0:T(8,128)} %bitcast.42), calls=%async_computation.1 | async-start | bytes 262144 | tf_op jit(solution)/shard_map/all_to_all | solution.py:263
  101.9 2.2 %copy-start = (f32[2,128,32,128]{3,1,2,0:T(8,128)S(1)}, f32[2,128,32,128]{3,1,2,0:T(8,128)}, u32[]{:S(2)}) copy-start(f32[2,128,32,128]{3,1,2,0:T(8,128)} %copy.16) | copy-start | bytes 12582916
  106.0 13.0 %collective-permute-start.32 = (f32[2,16,16,128]{3,2,1,0:T(8,128)S(1)}, f32[2,16,16,128]{3,2,1,0:T(8,128)}, u32[]{:S(2)}, u32[]{:S(2)}) collective-permute-start(f32[2,16,16,128]{3,2,1,0:T(8,128)S(1)} %get-tuple-element.29), channel_id=1, source_target_pairs={{0,32},{32,64},{64,96},{96,0},{1,33},{33,65},{65,97},{97,1},{2,34}... | collective-permute-start | bytes 786440 | tf_op jit(solution)/shard_map/ppermute | solution.py:24
  106.8 12.9 %collective-permute-start.33 = (f32[2,16,16,128]{3,2,1,0:T(8,128)S(1)}, f32[2,16,16,128]{3,2,1,0:T(8,128)}, u32[]{:S(2)}, u32[]{:S(2)}) collective-permute-start(f32[2,16,16,128]{3,2,1,0:T(8,128)S(1)} %get-tuple-element.30), channel_id=1, source_target_pairs={{0,64},{32,96},{64,0},{96,32},{1,65},{33,97},{65,1},{97,33},{2,66}... | collective-permute-start | bytes 786440 | tf_op jit(solution)/shard_map/ppermute | solution.py:24
  109.4 10.2 %collective-permute-start.34 = (f32[2,16,16,128]{3,2,1,0:T(8,128)S(1)}, f32[2,16,16,128]{3,2,1,0:T(8,128)}, u32[]{:S(2)}, u32[]{:S(2)}) collective-permute-start(f32[2,16,16,128]{3,2,1,0:T(8,128)S(1)} %get-tuple-element.31), channel_id=1, source_target_pairs={{0,96},{32,0},{64,32},{96,64},{1,97},{33,1},{65,33},{97,65},{2,98}... | collective-permute-start | bytes 786440 | tf_op jit(solution)/shard_map/ppermute | solution.py:24
  111.7 15.1 %collective-permute-start.28 = (f32[4,15,16,128]{3,2,1,0:T(8,128)S(1)}, f32[4,15,16,128]{3,2,1,0:T(8,128)}, u32[]{:S(2)}, u32[]{:S(2)}) collective-permute-start(f32[4,15,16,128]{3,2,1,0:T(8,128)S(1)} %get-tuple-element.27), channel_id=1, source_target_pairs={{0,16},{16,0},{1,17},{17,1},{2,18},{18,2},{3,19},{19,3},{4,20},{20... | collective-permute-start | bytes 1474568 | tf_op jit(solution)/shard_map/ppermute | solution.py:24
  115.3 23.4 %all-to-all-start.2 = ((f32[16,136,128]{2,1,0:T(8,128)}), f32[16,136,128]{2,1,0:T(8,128)S(1)}, u32[]{:S(2)}, u32[]{:S(2)}) async-start(f32[16,136,128]{2,1,0:T(8,128)} %shard_map.60), calls=%async_computation.2 | async-start | bytes 2228224 | tf_op jit(solution)/shard_map/all_to_all | solution.py:272
  120.8 17.8 %collective-permute-start.35 = (f32[16,16,128]{2,1,0:T(8,128)S(1)}, f32[16,16,128]{2,1,0:T(8,128)S(1)}, u32[]{:S(2)}, u32[]{:S(2)}) collective-permute-start(f32[16,16,128]{2,1,0:T(8,128)S(1)} %slice_bitcast_fusion), channel_id=1, source_target_pairs={{0,16},{16,0},{1,17},{17,1},{2,18},{18,2},{3,19},{19,3},{4,20},{20... | collective-permute-start | bytes 393224 | tf_op jit(solution)/shard_map/ppermute | solution.py:24
  127.9 10.7 %collective-permute-start.30 = (f32[15,16,128]{2,1,0:T(8,128)S(1)}, f32[15,16,128]{2,1,0:T(8,128)S(1)}, u32[]{:S(2)}, u32[]{:S(2)}) collective-permute-start(f32[15,16,128]{2,1,0:T(8,128)S(1)} %get-tuple-element.40), channel_id=1, source_target_pairs={{0,64},{32,96},{64,0},{96,32},{1,65},{33,97},{65,1},{97,33},{2,66}... | collective-permute-start | bytes 368648 | tf_op jit(solution)/shard_map/ppermute | solution.py:24
  128.0 10.6 %collective-permute-start.31 = (f32[15,16,128]{2,1,0:T(8,128)S(1)}, f32[15,16,128]{2,1,0:T(8,128)S(1)}, u32[]{:S(2)}, u32[]{:S(2)}) collective-permute-start(f32[15,16,128]{2,1,0:T(8,128)S(1)} %get-tuple-element.41), channel_id=1, source_target_pairs={{0,96},{32,0},{64,32},{96,64},{1,97},{33,1},{65,33},{97,65},{2,98}... | collective-permute-start | bytes 368648 | tf_op jit(solution)/shard_map/ppermute | solution.py:24
  131.3 7.4 %collective-permute-start.29 = (f32[15,16,128]{2,1,0:T(8,128)S(1)}, f32[15,16,128]{2,1,0:T(8,128)S(1)}, u32[]{:S(2)}, u32[]{:S(2)}) collective-permute-start(f32[15,16,128]{2,1,0:T(8,128)S(1)} %get-tuple-element.42), channel_id=1, source_target_pairs={{0,32},{32,64},{64,96},{96,0},{1,33},{33,65},{65,97},{97,1},{2,34}... | collective-permute-start | bytes 368648 | tf_op jit(solution)/shard_map/ppermute | solution.py:24
